TPU v7x, 16 devices: a whole 2x2x2 slice. The times are simulated.
16 devices in a mesh: tp: 2 (over z), dp: 8 (over y, x, core).
Axes of the slice: x: 2, y: 2, z: 2, core: 2. Of those that a mesh axis runs over, the one named last changes fastest.
Arguments:
- w_query: bfloat16 [1024, 1024], P(('dp', 'tp'))
- b_query: bfloat16 [1024], P(('dp', 'tp'))
- w_key: bfloat16 [1024, 1024], P(('dp', 'tp'))
- b_key: bfloat16 [1024], P(('dp', 'tp'))
- w_value: bfloat16 [1024, 1024], P(('dp', 'tp'))
- b_value: bfloat16 [1024], P(('dp', 'tp'))
- w_out: bfloat16 [1024, 1024], P(('dp', 'tp'))
- w_gate: bfloat16 [2816, 1024], P(('dp', 'tp'))
- w_up: bfloat16 [2816, 1024], P(('dp', 'tp'))
- w_down: bfloat16 [1024, 2816], P(('dp', 'tp'))
- gain_attn: bfloat16 [1024], P(('dp', 'tp'))
- gain_mlp: bfloat16 [1024], P(('dp', 'tp'))
- hidden: bfloat16 [2048, 1024], P('dp')
- k_cache: bfloat16 [2048, 64, 16, 64], P('dp', None, 'tp')
- v_cache: bfloat16 [2048, 64, 16, 64], P('dp', None, 'tp')
- lengths: int32 [2048], P('dp')
Outputs:
- output 1: bfloat16 [1024, 1024], P('tp')
- output 2: bfloat16 [1024], P('tp')
- output 3: bfloat16 [1024, 1024], P('tp')
- output 4: bfloat16 [1024], P('tp')
- output 5: bfloat16 [1024, 1024], P('tp')
- output 6: bfloat16 [1024], P('tp')
- output 7: bfloat16 [1024, 1024], P(None, 'tp')
- output 8: bfloat16 [2816, 1024], P('tp')
- output 9: bfloat16 [2816, 1024], P('tp')
- output 10: bfloat16 [1024, 2816], P(None, 'tp')
- output 11: bfloat16 [1024], replicated
- output 12: bfloat16 [1024], replicated
- output 13: bfloat16 [2048, 1024], P('dp')
- output 14: bfloat16 [2048, 64, 16, 64], P('dp', None, 'tp')
- output 15: bfloat16 [2048, 64, 16, 64], P('dp', None, 'tp')
All inputs are finite; a program needn't handle non-finite values.
Results may differ from a plain program's by a relative error of at most 0.0153168.
Values are sent between devices in bfloat16 or wider.
A program may use at most 1 GiB of HBM per device.

v0:
```python
import jax
import jax.numpy as jnp
from jax import lax
from jax.sharding import PartitionSpec as P

EPS = 1e-6
THETA = 1000000.0


def rms_scale(act_rows, gain_vec):
    rows_f32 = act_rows.astype(jnp.float32)
    inv_rms = lax.rsqrt(jnp.mean(rows_f32 * rows_f32, axis=-1, keepdims=True) + EPS)
    return (rows_f32 * inv_rms * gain_vec.astype(jnp.float32)).astype(jnp.bfloat16)


def project(act_rows, weight, bias_vec):
    result = jnp.einsum("bd,nd->bn", act_rows, weight, preferred_element_type=jnp.float32)
    return (result + bias_vec.astype(jnp.float32)).astype(jnp.bfloat16)


def rotary(vectors, positions):
    head_dim = vectors.shape[-1]
    half_dim = head_dim // 2
    inv_freq = 1.0 / (THETA ** (jnp.arange(0, head_dim, 2, dtype=jnp.float32) / head_dim))
    angles = positions.astype(jnp.float32)[:, None] * inv_freq[None, :]
    cosine = jnp.cos(angles)[:, None, :]
    sine_tab = jnp.sin(angles)[:, None, :]
    vectors_f32 = vectors.astype(jnp.float32)
    first_half = vectors_f32[..., :half_dim]
    second_half = vectors_f32[..., half_dim:]
    return jnp.concatenate([first_half * cosine - second_half * sine_tab, second_half * cosine + first_half * sine_tab], axis=-1).astype(jnp.bfloat16)


def decode_step(synced, hidden, k_cache, v_cache, lengths):
    w_query, b_query, w_key, b_key, w_value, b_value, w_out, w_gate, w_up, w_down, gain_attn, gain_mlp = synced
    roll_count, cache_len, kv_local, head_dim = k_cache.shape
    q_local = w_query.shape[0] // head_dim
    normed = rms_scale(hidden, gain_attn)
    query_rot = rotary(project(normed, w_query, b_query).reshape(roll_count, q_local, head_dim), lengths)
    key_rot = rotary(project(normed, w_key, b_key).reshape(roll_count, kv_local, head_dim), lengths)
    value_new = project(normed, w_value, b_value).reshape(roll_count, kv_local, head_dim)
    slot_ids = jnp.arange(cache_len)
    at_slot = (slot_ids[None, :] == lengths[:, None])[:, :, None, None]
    k_cache_new = jnp.where(at_slot, key_rot[:, None], k_cache)
    v_cache_new = jnp.where(at_slot, value_new[:, None], v_cache)
    grouped = query_rot.reshape(roll_count, kv_local, q_local // kv_local, head_dim)
    scores = jnp.einsum("bkgd,bskd->bkgs", grouped, k_cache_new, preferred_element_type=jnp.float32) * head_dim ** -0.5
    visible = (slot_ids[None, :] <= lengths[:, None])[:, None, None, :]
    attn_probs = jax.nn.softmax(jnp.where(visible, scores, -1e30), axis=-1).astype(jnp.bfloat16)
    attended = jnp.einsum("bkgs,bskd->bkgd", attn_probs, v_cache_new, preferred_element_type=jnp.float32).astype(jnp.bfloat16).reshape(roll_count, q_local * head_dim)
    attn_part = jnp.einsum("bn,dn->bd", attended, w_out, preferred_element_type=jnp.float32).astype(jnp.bfloat16)
    attn_sum = lax.psum(attn_part, "tp")
    mid_hidden = (hidden.astype(jnp.float32) + attn_sum.astype(jnp.float32)).astype(jnp.bfloat16)
    normed_mlp = rms_scale(mid_hidden, gain_mlp)
    gate_val = jnp.einsum("bd,fd->bf", normed_mlp, w_gate, preferred_element_type=jnp.float32).astype(jnp.bfloat16)
    up_val = jnp.einsum("bd,fd->bf", normed_mlp, w_up, preferred_element_type=jnp.float32).astype(jnp.bfloat16)
    gated = (jax.nn.silu(gate_val.astype(jnp.float32)) * up_val.astype(jnp.float32)).astype(jnp.bfloat16)
    down_part = jnp.einsum("bf,df->bd", gated, w_down, preferred_element_type=jnp.float32).astype(jnp.bfloat16)
    down_sum = lax.psum(down_part, "tp")
    hidden_out = (mid_hidden.astype(jnp.float32) + down_sum.astype(jnp.float32)).astype(jnp.bfloat16)
    return (hidden_out, k_cache_new, v_cache_new)


def solution(mesh):
    dp_size = mesh.shape["dp"]
    tp_size = mesh.shape["tp"]

    def head_rows(block):
        gathered = lax.all_gather(block, "dp", axis=0, tiled=False)
        grouped = gathered.reshape((tp_size, dp_size // tp_size) + block.shape)
        swapped = lax.all_to_all(grouped, "tp", 0, 0, tiled=True)
        return jnp.swapaxes(swapped, 0, 1).reshape((dp_size * block.shape[0],) + block.shape[1:])

    def column_share(block):
        swapped = lax.all_to_all(block, "tp", 1, 0, tiled=True)
        return lax.all_gather(swapped, "dp", axis=0, tiled=True)

    def kv_rows(block, head_dim):
        rank_rows = head_rows(block)
        kv_heads = rank_rows.shape[0] * tp_size // head_dim
        if kv_heads >= tp_size:
            return rank_rows
        whole_rows = lax.all_gather(rank_rows, "tp", axis=0, tiled=True)
        start_row = (lax.axis_index("tp") // (tp_size // kv_heads)) * head_dim
        return lax.dynamic_slice_in_dim(whole_rows, start_row, head_dim, axis=0)

    def whole_vector(block):
        return lax.all_gather(block, ("dp", "tp"), axis=0, tiled=True)

    def local_step(w_query, b_query, w_key, b_key, w_value, b_value, w_out, w_gate, w_up, w_down, gain_attn, gain_mlp, hidden, k_cache, v_cache, lengths):
        head_dim = k_cache.shape[-1]
        synced = (head_rows(w_query), head_rows(b_query),
                  kv_rows(w_key, head_dim), kv_rows(b_key, head_dim),
                  kv_rows(w_value, head_dim), kv_rows(b_value, head_dim),
                  column_share(w_out), head_rows(w_gate), head_rows(w_up), column_share(w_down),
                  whole_vector(gain_attn), whole_vector(gain_mlp))
        return synced + decode_step(synced, hidden, k_cache, v_cache, lengths)

    row_spec = P(("dp", "tp"), None)
    flat_spec = P(("dp", "tp"))
    cache_spec = P("dp", None, "tp", None)
    in_specs = (row_spec, flat_spec, row_spec, flat_spec, row_spec, flat_spec, row_spec, row_spec, row_spec, row_spec, flat_spec, flat_spec, P("dp", None), cache_spec, cache_spec, P("dp"))
    out_specs = (P("tp", None), P("tp"), P("tp", None), P("tp"), P("tp", None), P("tp"), P(None, "tp"), P("tp", None), P("tp", None), P(None, "tp"), P(None), P(None), P("dp", None), cache_spec, cache_spec)
    return jax.shard_map(local_step, mesh=mesh, in_specs=in_specs, out_specs=out_specs, check_vma=False)
```

profile of v0, /device:TPU:0, one launch (start us, length us, event | category | flops | bytes accessed | tf_op | source)
XLA Modules:
  0.0 295.1 jit_solution(18294023447226985107)
XLA Ops:
  10.4 8.9 %all_to_all.78 = bf16[64,2,512]{2,0,1:T(8,128)(2,1)} all-to-all(bf16[64,2,512]{2,0,1:T(8,128)(2,1)S(1)} %bitcast.77), channel_id=1, replica_groups=mesh['tp'=2,'dp'=8] {'tp'}, dimensions={1} | all-to-all | bytes 262144 | tf_op jit(solution)/shard_map/all_to_all | solution.py:75
  19.9 1.2 dynamic-slice
  24.3 12.9 %all-reduce.6 = (bf16[512]{0:T(512)(128)(2,1)S(1)}, bf16[512]{0:T(512)(128)(2,1)S(1)}, bf16[512]{0:T(512)(128)(2,1)S(1)}) all-reduce(bf16[512]{0:T(512)(128)(2,1)S(1)} %dynamic-update-slice, bf16[512]{0:T(512)(128)(2,1)S(1)} %dynamic-update-slice.1, bf16[512]{0:T(512)(128)(2,1)S(1)} %dynamic-update-slice.2), channel_id=3, replica_groups=mesh['tp'=2,'dp'=8] {'dp'}, use_global_device_ids=true, to_apply=%add | all-reduce | flops 1536 | bytes 6144
  38.0 3.2 %all-to-all-start.1 = ((bf16[2,2,128]{2,1,0:T(2,128)(2,1)}), bf16[2,2,128]{2,1,0:T(2,128)(2,1)S(1)}, u32[]{:S(2)}, u32[]{:S(2)}) async-start(bf16[2,2,128]{2,1,0:T(2,128)(2,1)} %reshape.325), calls=%async_computation.1 | async-start | bytes 2048 | tf_op jit(solution)/shard_map/all_to_all | solution.py:71
  41.9 2.8 all-to-all-done.1
  44.7 3.2 %all-to-all-start.3 = ((bf16[2,2,128]{2,1,0:T(2,128)(2,1)}), bf16[2,2,128]{2,1,0:T(2,128)(2,1)S(1)}, u32[]{:S(2)}, u32[]{:S(2)}) async-start(bf16[2,2,128]{2,1,0:T(2,128)(2,1)} %reshape.327), calls=%async_computation.3 | async-start | bytes 2048 | tf_op jit(solution)/shard_map/all_to_all | solution.py:71
  48.7 2.8 all-to-all-done.3
  51.5 3.2 %all-to-all-start.5 = ((bf16[2,2,128]{2,1,0:T(2,128)(2,1)}), bf16[2,2,128]{2,1,0:T(2,128)(2,1)S(1)}, u32[]{:S(2)}, u32[]{:S(2)}) async-start(bf16[2,2,128]{2,1,0:T(2,128)(2,1)} %reshape.329), calls=%async_computation.5 | async-start | bytes 2048 | tf_op jit(solution)/shard_map/all_to_all | solution.py:71
  55.3 3.0 %all-to-all-done.5 = bf16[2,2,128]{2,1,0:T(2,128)(2,1)S(1)} async-done(((bf16[2,2,128]{2,1,0:T(2,128)(2,1)}), bf16[2,2,128]{2,1,0:T(2,128)(2,1)S(1)}, u32[]{:S(2)}, u32[]{:S(2)}) %all-to-all-start.5) | async-done | bytes 1056 | tf_op jit(solution)/shard_map/all_to_all | solution.py:71
  58.3 3.6 %all-to-all-start = ((bf16[2,4,64,1024]{3,2,1,0:T(8,128)(2,1)}), bf16[2,4,64,1024]{3,2,1,0:T(8,128)(2,1)S(1)}, u32[]{:S(2)}, u32[]{:S(2)}) async-start(bf16[2,4,64,1024]{3,2,1,0:T(8,128)(2,1)} %bitcast.75), calls=%async_computation | async-start | bytes 2097152 | tf_op jit(solution)/shard_map/all_to_all | solution.py:71
  62.1 9.5 %all-to-all-done = bf16[2,4,64,1024]{3,2,1,0:T(8,128)(2,1)S(1)} async-done(((bf16[2,4,64,1024]{3,2,1,0:T(8,128)(2,1)}), bf16[2,4,64,1024]{3,2,1,0:T(8,128)(2,1)S(1)}, u32[]{:S(2)}, u32[]{:S(2)}) %all-to-all-start) | async-done | bytes 1048608 | tf_op jit(solution)/shard_map/all_to_all | solution.py:71
  71.7 3.6 %all-to-all-start.2 = ((bf16[2,4,64,1024]{3,2,1,0:T(8,128)(2,1)}), bf16[2,4,64,1024]{3,2,1,0:T(8,128)(2,1)S(1)}, u32[]{:S(2)}, u32[]{:S(2)}) async-start(bf16[2,4,64,1024]{3,2,1,0:T(8,128)(2,1)} %bitcast.70), calls=%async_computation.2 | async-start | bytes 2097152 | tf_op jit(solution)/shard_map/all_to_all | solution.py:71
  77.0 35.0 %all-reduce.5 = (bf16[1024]{0:T(1024)(128)(2,1)S(1)}, bf16[1024]{0:T(1024)(128)(2,1)S(1)}) all-reduce(bf16[1024]{0:T(1024)(128)(2,1)S(1)} %dynamic-update-slice.3, bf16[1024]{0:T(1024)(128)(2,1)S(1)} %dynamic-update-slice.4), channel_id=1, replica_groups=mesh['tp'=2,'dp'=8] {'dp','tp'}, use_global_device_ids=true, to_apply=%add.3 | all-reduce | flops 2048 | bytes 8192
  114.6 3.6 %all-to-all-start.4 = ((bf16[2,4,64,1024]{3,2,1,0:T(8,128)(2,1)}), bf16[2,4,64,1024]{3,2,1,0:T(8,128)(2,1)S(1)}, u32[]{:S(2)}, u32[]{:S(2)}) async-start(bf16[2,4,64,1024]{3,2,1,0:T(8,128)(2,1)} %bitcast.67), calls=%async_computation.4 | async-start | bytes 2097152 | tf_op jit(solution)/shard_map/all_to_all | solution.py:71
  120.2 18.9 %multiply_reduce_fusion.1 = (f32[256,8,64]{0,1,2:T(8,128)S(1)}, bf16[256,64,8,64]{0,3,2,1:T(8,128)(2,1)}) fusion(f32[256,8,64]{0,2,1:T(8,128)S(1)} %get-tuple-element.36, bf16[256,64,8,64]{0,3,2,1:T(8,128)(2,1)} %param.29, bf16[256,8,64]{0,2,1:T(8,128)(2,1)S(1)} %get-tuple-element.37, pred[256,64]{0,1:T(8,128)(4,1)S(1)} %get-tuple-element.35), kind=kLoop, calls=%fused_computation.3 | loop fusion | flops 33423360 | bytes 34881536
  141.4 17.1 %multiply_reduce_fusion = (bf16[256,8,64]{0,2,1:T(8,128)(2,1)S(1)}, bf16[256,64,8,64]{0,3,2,1:T(8,128)(2,1)}) fusion(f32[256,8,64]{0,1,2:T(8,128)S(1)} %copy.116, bf16[256,64,8,64]{0,3,2,1:T(8,128)(2,1)} %param.30, bf16[256,8,64]{0,2,1:T(8,128)(2,1)S(1)} %bitcast.66, pred[256,64]{0,1:T(8,128)(4,1)S(1)} %get-tuple-element.35), kind=kLoop, calls=%fused_computation.2 | loop fusion | flops 33423360 | bytes 34619392 | tf_op jit(solution)/shard_map/bkgs,bskd->bkgd/dot_general | solution.py:50
  158.6 2.5 convolution_convert_fusion.2
  161.2 13.1 %all_to_all.79 = bf16[64,2,1408]{2,0,1:T(8,128)(2,1)} all-to-all(bf16[64,2,1408]{2,0,1:T(8,128)(2,1)S(1)} %bitcast.64), channel_id=1, replica_groups=mesh['tp'=2,'dp'=8] {'tp'}, dimensions={1} | all-to-all | bytes 720896 | tf_op jit(solution)/shard_map/all_to_all | solution.py:75
  174.3 3.9 %all-to-all-start.7 = ((bf16[2,4,176,1024]{3,2,1,0:T(8,128)(2,1)}), bf16[2,4,176,1024]{3,2,1,0:T(8,128)(2,1)S(1)}, u32[]{:S(2)}, u32[]{:S(2)}) async-start(bf16[2,4,176,1024]{3,2,1,0:T(8,128)(2,1)} %bitcast.57), calls=%async_computation.7 | async-start | bytes 5767168 | tf_op jit(solution)/shard_map/all_to_all | solution.py:71
  178.3 34.2 %all-to-all-done.7 = bf16[2,4,176,1024]{3,2,1,0:T(8,128)(2,1)S(1)} async-done(((bf16[2,4,176,1024]{3,2,1,0:T(8,128)(2,1)}), bf16[2,4,176,1024]{3,2,1,0:T(8,128)(2,1)S(1)}, u32[]{:S(2)}, u32[]{:S(2)}) %all-to-all-start.7) | async-done | bytes 2883616 | tf_op jit(solution)/shard_map/all_to_all | solution.py:71
  212.5 1.6 copy-done.1
  214.1 5.1 %all-to-all-start.8 = ((bf16[2,4,176,1024]{3,2,1,0:T(8,128)(2,1)}), bf16[2,4,176,1024]{3,2,1,0:T(8,128)(2,1)}, u32[]{:S(2)}, u32[]{:S(2)}) async-start(bf16[2,4,176,1024]{3,2,1,0:T(8,128)(2,1)} %bitcast.58), calls=%async_computation.8 | async-start | bytes 5767168 | tf_op jit(solution)/shard_map/all_to_all | solution.py:71
  219.5 1.3 fusion.20
  220.8 2.3 copy.96
  223.1 24.0 %all-to-all-done.8 = bf16[2,4,176,1024]{3,2,1,0:T(8,128)(2,1)} async-done(((bf16[2,4,176,1024]{3,2,1,0:T(8,128)(2,1)}), bf16[2,4,176,1024]{3,2,1,0:T(8,128)(2,1)}, u32[]{:S(2)}, u32[]{:S(2)}) %all-to-all-start.8) | async-done | bytes 2883616 | tf_op jit(solution)/shard_map/all_to_all | solution.py:71
  247.0 3.7 %copy.97 = bf16[2,4,176,1024]{3,2,0,1:T(8,128)(2,1)} copy(bf16[2,4,176,1024]{3,2,1,0:T(8,128)(2,1)} %all-to-all-done.8) | data formatting | bytes 5767168 | tf_op jit(solution)/shard_map/all_to_all | solution.py:71
  250.7 2.2 fusion.5
  252.9 5.9 %convolution_convert_fusion.3 = bf16[256,1024]{1,0:T(8,128)(2,1)} fusion(bf16[1024,1408]{1,0:T(8,128)(2,1)} %all-gather.18.cloned.1.call-done, bf16[1408,1024]{1,0:T(8,128)(2,1)} %bitcast.59, f32[256,1408]{1,0:T(8,128)} %fusion.5, bf16[256,1024]{1,0:T(8,128)(2,1)S(1)} %get-tuple-element.21, f32[1024]{0:T(1024)S(1)} %convert_element_type.135, ...), kind=kOutput, calls=%fused_computation.19 | convolution fusion | flops 1480589312 | bytes 8262656 | tf_op jit(solution)/shard_map/bf,df->bd/dot_general | solution.py:58
  258.8 25.0 %all-reduce.12.cloned.1.call-done = bf16[256,1024]{1,0:T(8,128)(2,1)} async-done(((bf16[256,1024]{1,0:T(8,128)(2,1)}), bf16[256,1024]{1,0:T(8,128)(2,1)}) %all-reduce.12.cloned.1.call-update) | async-done | bytes 524304 | tf_op jit(solution)/shard_map/psum | solution.py:59
  283.8 2.2 fusion.23
  286.0 1.0 copy.141
  287.0 1.6 copy.142
  (116 shorter events, 17.6 us)
Async XLA Ops:
  7.2 54.7 %copy-start.4 = (bf16[256,1024]{1,0:T(8,128)(2,1)S(1)}, bf16[256,1024]{1,0:T(8,128)(2,1)}, u32[]{:S(2)}) copy-start(bf16[256,1024]{1,0:T(8,128)(2,1)} %param.28) | copy-start | bytes 1572868
  7.2 54.9 %copy-start.12 = (s32[256]{0:T(256)S(1)}, s32[256]{0:T(256)}, u32[]{:S(2)}) copy-start(s32[256]{0:T(256)} %param.31) | copy-start | bytes 3076
  7.2 51.1 %all-gather.20.cloned.1.call-start = ((), (), s32[]{:S(2)}) async-start(), calls=%async_computation.14 | async-start | bytes 1179648 | tf_op jit(solution)/shard_map/all_gather | solution.py:69
  7.9 54.2 %all-gather.22.cloned.1.call-start = ((), (), s32[]{:S(2)}) async-start(), calls=%async_computation.15 | async-start | bytes 1179648 | tf_op jit(solution)/shard_map/all_gather | solution.py:69
  8.7 105.9 %all-gather.24.cloned.1.call-start = ((), (), s32[]{:S(2)}) async-start(), calls=%async_computation.16 | async-start | bytes 1179648 | tf_op jit(solution)/shard_map/all_gather | solution.py:69
  9.4 149.2 %all-gather.16.cloned.1.call-start = ((), (), s32[]{:S(2)}) async-start(), calls=%async_computation.10 | async-start | bytes 1179648 | tf_op jit(solution)/shard_map/all_gather | solution.py:76
  19.2 56.0 %copy-start.17 = (u32[16]{0:T(128)S(1)}, u32[16]{0:T(128)}, u32[]{:S(2)}) copy-start(u32[16]{0:T(128)} %constant.43) | copy-start | bytes 196
  19.2 57.3 %copy-start.15 = (bf16[64]{0:T(256)(128)(2,1)S(1)}, bf16[64]{0:T(256)(128)(2,1)}, u32[]{:S(2)}) copy-start(bf16[64]{0:T(256)(128)(2,1)} %param.26) | copy-start | bytes 388
  19.2 57.6 %copy-start.16 = (bf16[64]{0:T(256)(128)(2,1)S(1)}, bf16[64]{0:T(256)(128)(2,1)}, u32[]{:S(2)}) copy-start(bf16[64]{0:T(256)(128)(2,1)} %param.27) | copy-start | bytes 388
  19.3 155.1 %all-gather.26.cloned.1.call-start = ((), (), s32[]{:S(2)}) async-start(), calls=%async_computation.17 | async-start | bytes 3244032 | tf_op jit(solution)/shard_map/all_gather | solution.py:69
  38.0 6.8 %all-to-all-start.1 = ((bf16[2,2,128]{2,1,0:T(2,128)(2,1)}), bf16[2,2,128]{2,1,0:T(2,128)(2,1)S(1)}, u32[]{:S(2)}, u32[]{:S(2)}) async-start(bf16[2,2,128]{2,1,0:T(2,128)(2,1)} %reshape.325), calls=%async_computation.1 | async-start | bytes 2048 | tf_op jit(solution)/shard_map/all_to_all | solution.py:71
  44.7 6.8 %all-to-all-start.3 = ((bf16[2,2,128]{2,1,0:T(2,128)(2,1)}), bf16[2,2,128]{2,1,0:T(2,128)(2,1)S(1)}, u32[]{:S(2)}, u32[]{:S(2)}) async-start(bf16[2,2,128]{2,1,0:T(2,128)(2,1)} %reshape.327), calls=%async_computation.3 | async-start | bytes 2048 | tf_op jit(solution)/shard_map/all_to_all | solution.py:71
  51.5 6.8 %all-to-all-start.5 = ((bf16[2,2,128]{2,1,0:T(2,128)(2,1)}), bf16[2,2,128]{2,1,0:T(2,128)(2,1)S(1)}, u32[]{:S(2)}, u32[]{:S(2)}) async-start(bf16[2,2,128]{2,1,0:T(2,128)(2,1)} %reshape.329), calls=%async_computation.5 | async-start | bytes 2048 | tf_op jit(solution)/shard_map/all_to_all | solution.py:71
  54.7 123.6 %all-gather.28.cloned.1.call-start = ((), (), s32[]{:S(2)}) async-start(), calls=%async_computation.18 | async-start | bytes 3244032 | tf_op jit(solution)/shard_map/all_gather | solution.py:69
  58.3 13.4 %all-to-all-start = ((bf16[2,4,64,1024]{3,2,1,0:T(8,128)(2,1)}), bf16[2,4,64,1024]{3,2,1,0:T(8,128)(2,1)S(1)}, u32[]{:S(2)}, u32[]{:S(2)}) async-start(bf16[2,4,64,1024]{3,2,1,0:T(8,128)(2,1)} %bitcast.75), calls=%async_computation | async-start | bytes 2097152 | tf_op jit(solution)/shard_map/all_to_all | solution.py:71
  71.7 42.9 %all-to-all-start.2 = ((bf16[2,4,64,1024]{3,2,1,0:T(8,128)(2,1)}), bf16[2,4,64,1024]{3,2,1,0:T(8,128)(2,1)S(1)}, u32[]{:S(2)}, u32[]{:S(2)}) async-start(bf16[2,4,64,1024]{3,2,1,0:T(8,128)(2,1)} %bitcast.70), calls=%async_computation.2 | async-start | bytes 2097152 | tf_op jit(solution)/shard_map/all_to_all | solution.py:71
  112.0 2.5 copy-start.13
  112.0 107.4 %copy-start.14 = (bf16[1024]{0:T(1024)(128)(2,1)}, bf16[1024]{0:T(1024)(128)(2,1)S(1)}, u32[]{:S(2)}) copy-start(bf16[1024]{0:T(1024)(128)(2,1)S(1)} %get-tuple-element.64) | copy-start | bytes 6148
  112.4 2.2 copy-start.9
  112.6 2.0 copy-start.10
  112.8 1.8 copy-start.11
  114.6 25.1 %all-to-all-start.4 = ((bf16[2,4,64,1024]{3,2,1,0:T(8,128)(2,1)}), bf16[2,4,64,1024]{3,2,1,0:T(8,128)(2,1)S(1)}, u32[]{:S(2)}, u32[]{:S(2)}) async-start(bf16[2,4,64,1024]{3,2,1,0:T(8,128)(2,1)} %bitcast.67), calls=%async_computation.4 | async-start | bytes 2097152 | tf_op jit(solution)/shard_map/all_to_all | solution.py:71
  118.2 101.2 %all-reduce.10.cloned.1.call-start = ((), (), s32[]{:S(2)}) async-start(), calls=%async_computation.12 | async-start | bytes 1048576 | tf_op jit(solution)/shard_map/psum | solution.py:52
  141.4 19.8 %copy-start.8 = (bf16[64,2816]{1,0:T(8,128)(2,1)S(1)}, bf16[64,2816]{1,0:T(8,128)(2,1)}, u32[]{:S(2)}) copy-start(bf16[64,2816]{1,0:T(8,128)(2,1)} %param.25) | copy-start | bytes 1081348
  161.1 91.8 %all-gather.18.cloned.1.call-start = ((), (), s32[]{:S(2)}) async-start(), calls=%async_computation.11 | async-start | bytes 3244032 | tf_op jit(solution)/shard_map/all_gather | solution.py:76
  174.3 38.2 %all-to-all-start.7 = ((bf16[2,4,176,1024]{3,2,1,0:T(8,128)(2,1)}), bf16[2,4,176,1024]{3,2,1,0:T(8,128)(2,1)S(1)}, u32[]{:S(2)}, u32[]{:S(2)}) async-start(bf16[2,4,176,1024]{3,2,1,0:T(8,128)(2,1)} %bitcast.57), calls=%async_computation.7 | async-start | bytes 5767168 | tf_op jit(solution)/shard_map/all_to_all | solution.py:71
  212.5 1.6 copy-start.1
  214.1 33.0 %all-to-all-start.8 = ((bf16[2,4,176,1024]{3,2,1,0:T(8,128)(2,1)}), bf16[2,4,176,1024]{3,2,1,0:T(8,128)(2,1)}, u32[]{:S(2)}, u32[]{:S(2)}) async-start(bf16[2,4,176,1024]{3,2,1,0:T(8,128)(2,1)} %bitcast.58), calls=%async_computation.8 | async-start | bytes 5767168 | tf_op jit(solution)/shard_map/all_to_all | solution.py:71
  219.2 64.7 %all-reduce.12.cloned.1.call-start = ((), (), s32[]{:S(2)}) async-start(), calls=%async_computation.13 | async-start | bytes 1048576 | tf_op jit(solution)/shard_map/psum | solution.py:59
  223.0 27.7 %copy-start = (bf16[2,4,176,1024]{3,2,0,1:T(8,128)(2,1)}, bf16[2,4,176,1024]{3,2,0,1:T(8,128)(2,1)S(1)}, u32[]{:S(2)}) copy-start(bf16[2,4,176,1024]{3,2,0,1:T(8,128)(2,1)S(1)} %copy.96) | copy-start | bytes 8650756
  252.9 33.1 %copy-start.2 = (bf16[1024,512]{1,0:T(8,128)(2,1)S(1)}, bf16[1024,512]{1,0:T(8,128)(2,1)}, u32[]{:S(2)}) copy-start(bf16[1024,512]{1,0:T(8,128)(2,1)} %all-gather.16.cloned.1.call-done) | copy-start | bytes 3145732
  283.8 3.2 %copy-start.3 = (bf16[1024,1408]{1,0:T(8,128)(2,1)S(1)}, bf16[1024,1408]{1,0:T(8,128)(2,1)}, u32[]{:S(2)}) copy-start(bf16[1024,1408]{1,0:T(8,128)(2,1)} %all-gather.18.cloned.1.call-done) | copy-start | bytes 8650756
  (3 other events, 2.9 us)
Sparse Core Ops, SparseCore 0:
  9.9 22.2 all-gather.19
  34.0 19.3 all-gather.21
  55.3 19.3 all-gather.23
  76.4 19.7 all-gather.15
  97.8 27.5 all-gather.25
  127.2 27.0 all-gather.27
  161.2 34.0 all-reduce.9
  197.2 27.0 all-gather.17
  259.0 24.8 all-reduce.11
where the time goes:
time: 296 us; the launch traced here: 295 us
  waiting for transfers between devices  105 us (35%)
  blocking collectives  69.8 us (24%)
  other arithmetic  40.5 us (14%)
  starting transfers between devices  29.9 us (10%)
  local copies, waits for them, and re-layouts  22.6 us (8%)
  between operations  15.6 us (5%)
  matrix products  12.1 us (4%)
    all_to_all x8, waiting for transfers between devices, head_rows(): swapped = lax.all_to_all(grouped, 'tp', 0, 0, tiled=True)  76.4 us
    unnamed x2, blocking collectives  47.9 us
    all_to_all x8, starting transfers between devices, head_rows(): swapped = lax.all_to_all(grouped, 'tp', 0, 0, tiled=True)  29.3 us
    psum x1, waiting for transfers between devices, decode_step(): down_sum = lax.psum(down_part, 'tp')  25 us
    all_to_all x2, blocking collectives, column_share(): swapped = lax.all_to_all(block, 'tp', 1, 0, tiled=True)  21.9 us
    unnamed x2, other arithmetic  18.9 us
    dot_general x1, other arithmetic, decode_step(): jnp.einsum('bkgs,bskd->bkgd', attn_probs, v_cache_new, preferred_element_...  17.1 us
    unnamed x57, local copies, waits for them, and re-layouts  14.4 us
  transfers between devices with their start and end apart: 17, of which 7 were waited for; matrix products, arithmetic and copies ran while one was open for 20% of the time, Pallas kernels for 0%

commit v1 on v0

v1 whole, which is shorter than its diff:
```python
import jax
import jax.numpy as jnp
from jax import lax
from jax.experimental import pallas as pl
from jax.experimental.pallas import tpu as pltpu
from jax.sharding import PartitionSpec as P

EPS = 1e-6
THETA = 1000000.0
MESH = pl.DeviceIdType.MESH
F32 = jnp.float32
BF16 = jnp.bfloat16
ROW_BYTES = (((1,), (1,)), ((), ()))
NAT = (((1,), (0,)), ((), ()))
GROUP = 8


def dot(lhs, rhs, dims):
    return lax.dot_general(lhs, rhs, dims, preferred_element_type=F32)


class Place:
    def __init__(self):
        tp = lax.axis_index("tp")
        dp = lax.axis_index("dp")
        self.z = tp
        self.dp = dp
        self.y = dp // 4
        self.x = (dp // 2) % 2
        self.c = dp % 2
        self.home = lax.rem(self.y + self.z, 2) == 0
        self.away = lax.rem(self.y + self.z, 2) == 1
        self.to_x = (tp, dp + 2 - 4 * self.x)
        self.to_y = (tp, dp + 4 - 8 * self.y)
        self.to_c = (tp, dp + 1 - 2 * self.c)
        self.to_z = (1 - tp, dp)


def remote(src, dst, send, recv, device):
    return pltpu.make_async_remote_copy(
        src_ref=src, dst_ref=dst, send_sem=send, recv_sem=recv, device_id=device, device_id_type=MESH)


class Rows:
    def __init__(self, place, buf, pieces, sems):
        self.p, self.buf, self.pieces = place, buf, pieces
        self.sx, self.sy, self.sz, self.sc, self.r, self.rc = sems

    def block(self, k, core=0):
        p = self.p
        x = 1 - p.x if k & 1 else p.x
        z = 1 - p.z if k & 2 else p.z
        c = 1 - p.c if core else p.c
        return (x * 2 + c) * 2 + z

    def at(self, k, core=0):
        return self.buf.at[self.block(k, core)]

    def _own(self, send, recv, device):
        start = 0
        for ref in self.pieces:
            n = ref.shape[0]
            remote(ref, self.buf.at[self.block(0), pl.ds(start, n)], send, recv, device).start()
            start += n

    def _fwd(self, k, send, recv, device):
        remote(self.at(k), self.at(k), send, recv, device).start()

    def wait(self, k):
        remote(self.at(k), self.at(k), self.sx.at[k], self.r.at[k], self.p.to_x).wait_recv()

    def wait_core(self, k):
        remote(self.at(k, 1), self.at(k, 1), self.sc.at[k], self.rc.at[k], self.p.to_c).wait_recv()

    def own_away(self):
        @pl.when(self.p.away)
        def _():
            self._own(self.sz.at[0], self.r.at[2], self.p.to_z)

    def own_home(self):
        @pl.when(self.p.home)
        def _():
            self._own(self.sx.at[0], self.r.at[1], self.p.to_x)
            self._own(self.sy.at[0], self.r.at[0], self.p.to_y)
            self._own(self.sc.at[0], self.rc.at[0], self.p.to_c)

    def local(self):
        @pl.when(self.p.home)
        def _():
            start = 0
            for ref in self.pieces:
                n = ref.shape[0]
                self.buf[self.block(0), pl.ds(start, n)] = ref[...]
                start += n

    def k0(self):
        @pl.when(self.p.away)
        def _():
            self.wait(0)
            self._fwd(0, self.sx.at[0], self.r.at[1], self.p.to_x)
            self._fwd(0, self.sc.at[0], self.rc.at[0], self.p.to_c)

    def k2(self):
        self.wait(2)
        self._fwd(2, self.sx.at[2], self.r.at[3], self.p.to_x)

        @pl.when(self.p.home)
        def _():
            self._fwd(2, self.sy.at[2], self.r.at[2], self.p.to_y)

        self._fwd(2, self.sc.at[2], self.rc.at[2], self.p.to_c)

    def last(self, k):
        self.wait(k)
        self._fwd(k, self.sc.at[k], self.rc.at[k], self.p.to_c)

    def drain(self):
        p = self.p
        for k in (0, 2):
            remote(self.at(k), self.at(k), self.sx.at[k], self.r.at[k], p.to_x).wait_send()
        for k in range(4):
            remote(self.at(k), self.at(k), self.sc.at[k], self.rc.at[k], p.to_c).wait_send()

        @pl.when(p.home)
        def _():
            for k in (0, 2):
                remote(self.at(k), self.at(k), self.sy.at[k], self.r.at[k], p.to_y).wait_send()

        @pl.when(p.away)
        def _():
            remote(self.at(0), self.at(0), self.sz.at[0], self.r.at[0], p.to_z).wait_send()


class Cols:
    def __init__(self, place, buf, own, sems):
        self.p, self.buf, self.own = place, buf, own
        self.n = buf.shape[-1]
        self.sx, self.sy, self.sz, self.sc, self.r, self.rc = sems

    def block(self, k, core=0):
        p = self.p
        x = 1 - p.x if k & 1 else p.x
        y = 1 - p.y if k & 2 else p.y
        z = 1 - p.z if k & 4 else p.z
        c = 1 - p.c if core else p.c
        return (y * 4 + x * 2 + c) * 2 + z

    def at(self, k, core=0):
        return self.buf.at[self.block(k, core)]

    def half(self, z):
        return self.own.at[:, pl.ds(pl.multiple_of(z * self.n, 128), self.n)]

    def wait(self, k):
        remote(self.at(k), self.at(k), self.sx.at[k], self.r.at[k], self.p.to_x).wait_recv()

    def wait_core(self, k):
        remote(self.at(k, 1), self.at(k, 1), self.sc.at[k], self.rc.at[k], self.p.to_c).wait_recv()

    def send_z(self):
        remote(self.half(1 - self.p.z), self.at(0), self.sz.at[0], self.r.at[4], self.p.to_z).start()

    def _send(self, k, to, src=None):
        p = self.p
        src = self.at(k) if src is None else src
        if "x" in to:
            remote(src, self.at(k), self.sx.at[k], self.r.at[k ^ 1], p.to_x).start()
        if "y" in to:
            remote(src, self.at(k), self.sy.at[k], self.r.at[k ^ 2], p.to_y).start()
        if "c" in to:
            remote(src, self.at(k), self.sc.at[k], self.rc.at[k], p.to_c).start()

    def own_sends(self):
        self._send(0, "xyc", self.half(self.p.z))

    def local(self):
        self.buf[self.block(0)] = self.own[:, pl.ds(pl.multiple_of(self.p.z * self.n, 128), self.n)]

    ROUTE = {4: "xyc", 1: "yc", 2: "c", 5: "c", 6: "xc", 3: "c", 7: "c"}

    def step(self, k):
        self.wait(k)
        self._send(k, self.ROUTE[k])

    def drain(self):
        p = self.p
        for k, to in [(0, "xyc"), *self.ROUTE.items()]:
            for axis, sem, dev in (("x", self.sx, p.to_x), ("y", self.sy, p.to_y), ("c", self.sc, p.to_c)):
                if axis in to:
                    remote(self.at(k), self.at(k), sem.at[k], self.r.at[k], dev).wait_send()
        remote(self.at(0), self.at(0), self.sz.at[0], self.r.at[0], p.to_z).wait_send()


def row_sems():
    dma = pltpu.SemaphoreType.DMA
    return [dma((4,)), dma((4,)), dma((1,)), dma((4,)), dma((4,)), dma((4,))]


def col_sems():
    dma = pltpu.SemaphoreType.DMA
    return [dma((8,)), dma((8,)), dma((1,)), dma((8,)), dma((8,)), dma((8,))]


def layer_kernel(wq, wk, wv, wo, wg, wu, wd, small, x_ref, cos_ref, sin_ref, len_ref, k_hbm, v_hbm,
                 wqkv, wgu, wout, wdn, k_buf, v_buf, smalls, hid,
                 h_ref, sc_ref, o_ref, part, part_in, x1_ref, h2_ref, a_ref, down, down_in,
                 k_sem, v_sem, s_send, s_recv, p_send, p_recv, d_send, d_recv, *sems):
    place = Place()
    me = place.dp * 2 + place.z
    qkv = Rows(place, wqkv, (wq, wk, wv), sems[0:6])
    gu = Rows(place, wgu, (wg, wu), sems[6:12])
    out = Cols(place, wout, wo, sems[12:18])
    dn = Cols(place, wdn, wd, sems[18:24])
    order = [(0, 0), (0, 1), (2, 0), (2, 1), (1, 0), (1, 1), (3, 0), (3, 1)]

    def cache_copy(i):
        head = qkv.block(*order[i])
        return (pltpu.make_async_copy(k_hbm.at[:, head], k_buf.at[:, head], k_sem.at[i]),
                pltpu.make_async_copy(v_hbm.at[:, head], v_buf.at[:, head], v_sem.at[i]))

    barrier = pltpu.get_barrier_semaphore()
    for i in range(1, 16):
        other = lax.rem(me + i, 16)
        pl.semaphore_signal(barrier, inc=1, device_id=(other % 2, other // 2), device_id_type=MESH)
    for i in range(8):
        for copy in cache_copy(i):
            copy.start()
    pl.semaphore_wait(barrier, 15)

    def small_copy(i):
        other = lax.rem(me + i, 16)
        return remote(small, smalls.at[me], s_send.at[i], s_recv.at[i], (other % 2, other // 2))

    for i in range(1, 16):
        small_copy(i).start()
    qkv.own_away()
    qkv.own_home()
    out.send_z()
    gu.own_away()
    dn.send_z()

    qkv.local()
    gu.local()
    out.local()
    dn.local()
    smalls[me] = small[...]
    for i in range(1, 16):
        small_copy(i).wait_recv()

    def gain_row(i):
        pair = smalls[...].astype(F32).reshape(8, 2, 8, 128)
        rows = pair[:, 0, i] + pair[:, 1, i]
        return jnp.concatenate([rows[d:d + 1] for d in range(8)], axis=1)

    def normed(rows, i):
        inv = lax.rsqrt(jnp.mean(rows * rows, axis=-1, keepdims=True) + EPS)
        return (rows * inv * gain_row(i)).astype(BF16)

    h_ref[...] = normed(x_ref[...].astype(F32), 3)

    eye = lax.broadcasted_iota(jnp.int32, (64, 128), 1) % 64 == lax.broadcasted_iota(jnp.int32, (64, 128), 0)

    def bias_column(head, i):
        row = smalls[place.z * 8 + head].astype(F32)[i:i + 1]
        return jnp.sum(jnp.where(eye, row, 0.0), axis=1, keepdims=True)

    def attend(i):
        k, core = order[i]
        head = qkv.block(k, core)
        if core:
            qkv.wait_core(k)
        res = dot(wqkv[head], h_ref[...], ROW_BYTES)
        cos, sin = cos_ref[...], sin_ref[...]

        def rotated(start, b):
            v = (res[start:start + 64] + bias_column(head, b)).astype(BF16).astype(F32)
            lo, hi = v[:32], v[32:]
            return jnp.concatenate([lo * cos - hi * sin, hi * cos + lo * sin], axis=0).astype(BF16)

        q = rotated(0, 0).astype(F32)
        k_new = rotated(64, 1)
        v_new = (res[128:192] + bias_column(head, 2)).astype(BF16)
        lens = len_ref[...]
        for copy in cache_copy(i):
            copy.wait()

        def score_group(g, carry):
            rows = []
            for j in range(GROUP):
                s = g * GROUP + j
                kv = jnp.where(lens == s.astype(F32), k_new.astype(F32), k_buf[s, head].astype(F32))
                k_buf[s, head] = kv.astype(BF16)
                rows.append(jnp.sum(q * kv, axis=0, keepdims=True))
            sc_ref[pl.ds(pl.multiple_of(g * GROUP, GROUP), GROUP)] = jnp.concatenate(rows, axis=0)
            return carry

        lax.fori_loop(0, 64 // GROUP, score_group, 0)
        slot = lax.broadcasted_iota(jnp.int32, (64, 256), 0).astype(F32)
        scores = jnp.where(slot <= lens, sc_ref[...] * 0.125, -1e30)
        e = jnp.exp(scores - jnp.max(scores, axis=0, keepdims=True))
        sc_ref[...] = (e / jnp.sum(e, axis=0, keepdims=True)).astype(BF16).astype(F32)

        def value_group(g, acc):
            probs = sc_ref[pl.ds(pl.multiple_of(g * GROUP, GROUP), GROUP)]
            for j in range(GROUP):
                s = g * GROUP + j
                vv = jnp.where(lens == s.astype(F32), v_new.astype(F32), v_buf[s, head].astype(F32))
                v_buf[s, head] = vv.astype(BF16)
                acc = acc + probs[j:j + 1] * vv
            return acc

        acc = lax.fori_loop(0, 64 // GROUP, value_group, jnp.zeros((64, 256), F32))
        o_ref[pl.ds(pl.multiple_of(head * 64, 64), 64)] = acc.astype(BF16)

    qkv.k0()
    attend(0)
    attend(1)
    qkv.k2()
    out.own_sends()
    gu.own_home()
    dn.own_sends()
    attend(2)
    out.step(4)
    attend(3)
    out.step(1)
    out.step(2)
    qkv.last(1)
    attend(4)
    out.step(6)
    attend(5)
    qkv.last(3)
    attend(6)
    attend(7)
    for k in (5, 3, 7):
        out.step(k)
    gu.k0()
    gu.k2()
    dn.step(4)
    for k in range(8):
        out.wait_core(k)

    o = o_ref[...].T
    part[...] = dot(o, wout[...].reshape(1024, 512), ROW_BYTES).astype(BF16)
    swap = remote(part, part_in, p_send, p_recv, place.to_z)
    swap.start()
    dn.step(1)
    dn.step(2)
    swap.wait_recv()
    total = (part[...].astype(F32) + part_in[...].astype(F32)).astype(BF16)
    x1 = (x_ref[...].astype(F32) + total.astype(F32)).astype(BF16)
    x1_ref[...] = x1
    h2_ref[...] = normed(x1.astype(F32), 4)

    def gated(i):
        k, core = order[i]
        if core:
            gu.wait_core(k)
        block = gu.block(k, core)
        res = dot(wgu[block], h2_ref[...], ROW_BYTES).astype(BF16).astype(F32)
        g, u = res[:176], res[176:]
        a_ref[block] = (g / (1.0 + jnp.exp(-g)) * u).astype(BF16)

    for i in range(4):
        gated(i)
    dn.step(6)
    gu.last(1)
    gated(4)
    gated(5)
    dn.step(5)
    dn.step(3)
    gu.last(3)
    gated(6)
    gated(7)

    def down_copy(i, pair):
        rows = pl.ds(pl.multiple_of(pair * 128, 128), 128)
        return remote(down.at[rows], down_in.at[rows], d_send.at[i], d_recv.at[i], place.to_z)

    def down_pair(i):
        k, core = i // 2, i % 2
        if core:
            dn.wait_core(k)
            dn.wait_core(k + 4)
        pair = dn.block(k, core) // 2
        w = wdn[pl.ds(pair * 2, 2)].reshape(128, 1408)
        rows = pl.ds(pl.multiple_of(pair * 128, 128), 128)
        down[rows] = dot(w, a_ref[...].reshape(1408, 256), NAT).astype(BF16)
        down_copy(i, pair).start()

    for i in range(6):
        down_pair(i)
    dn.step(7)
    down_pair(6)
    down_pair(7)
    for i in range(8):
        pair = dn.block(i // 2, i % 2) // 2
        down_copy(i, pair).wait_recv()
        rows = pl.ds(pl.multiple_of(pair * 128, 128), 128)
        both = (down[rows].astype(F32) + down_in[rows].astype(F32)).T.astype(BF16).astype(F32)
        hid[:, rows] = (x1_ref[:, rows].astype(F32) + both).astype(BF16)

    for group in (qkv, gu, out, dn):
        group.drain()
    for i in range(1, 16):
        small_copy(i).wait_send()
    swap.wait_send()
    for i in range(8):
        down_copy(i, dn.block(i // 2, i % 2) // 2).wait_send()


def store_kernel(wqkv, wgu, wout, wdn, smalls, hid,
                 wq, wk, wv, wo, wg, wu, wd, hid_out, bq, bk, bv, ga, gm, sem):
    pairs = [(wdn, wd), (wgu.at[:, pl.ds(0, 176)], wg), (wgu.at[:, pl.ds(176, 176)], wu),
             (wqkv.at[:, pl.ds(0, 64)], wq), (wqkv.at[:, pl.ds(64, 64)], wk), (wqkv.at[:, pl.ds(128, 64)], wv),
             (wout, wo), (hid, hid_out)]
    copies = [pltpu.make_async_copy(src, dst, sem.at[i]) for i, (src, dst) in enumerate(pairs)]
    for copy in copies:
        copy.start()
    z = lax.axis_index("tp")
    plane = smalls[pl.ds(z * 8, 8)].astype(F32).reshape(4, 2, 8, 128)
    whole = smalls[...].astype(F32).reshape(8, 2, 8, 128)
    for i, ref in enumerate((bq, bk, bv)):
        ref[...] = (plane[:, 0, i] + plane[:, 1, i]).astype(BF16)
    for i, ref in enumerate((ga, gm)):
        ref[...] = (whole[:, 0, 3 + i] + whole[:, 1, 3 + i]).astype(BF16)
    for copy in copies:
        copy.wait()


def local_step(w_query, b_query, w_key, b_key, w_value, b_value, w_out, w_gate, w_up, w_down, gain_attn, gain_mlp,
               hidden, k_cache, v_cache, lengths):
    z = lax.axis_index("tp")
    vectors = jnp.stack([b_query, b_key, b_value, gain_attn, gain_mlp])
    zeros = jnp.zeros_like(vectors)
    small = jnp.concatenate([jnp.where(z == 0, vectors, zeros), jnp.where(z == 0, zeros, vectors)], axis=1)
    small = jnp.pad(small, ((0, 3), (0, 0)))
    inv_freq = 1.0 / (THETA ** (jnp.arange(0, 64, 2, dtype=F32) / 64))
    angles = inv_freq[:, None] * lengths.astype(F32)[None, :]
    cos, sin = jnp.cos(angles), jnp.sin(angles)
    lens = lengths.astype(F32)[None, :]
    k_view = jnp.transpose(k_cache, (1, 2, 3, 0))
    v_view = jnp.transpose(v_cache, (1, 2, 3, 0))

    vmem = pl.BlockSpec(memory_space=pltpu.VMEM)
    hbm = pl.BlockSpec(memory_space=pltpu.HBM)
    anywhere = pl.BlockSpec(memory_space=pl.ANY)
    dma = pltpu.SemaphoreType.DMA
    shapes = [(8, 192, 1024), (8, 352, 1024), (16, 64, 512), (16, 64, 1408), k_view.shape, v_view.shape,
              (16, 8, 128), (256, 1024)]
    held = pl.pallas_call(
        layer_kernel,
        out_shape=[pltpu.VMEM(s, BF16) for s in shapes],
        in_specs=[vmem] * 12 + [hbm] * 2,
        out_specs=[vmem] * 8,
        scratch_shapes=[
            pltpu.VMEM((256, 1024), BF16),
            pltpu.VMEM((64, 256), F32),
            pltpu.VMEM((512, 256), BF16),
            pltpu.VMEM((256, 1024), BF16),
            pltpu.VMEM((256, 1024), BF16),
            pltpu.VMEM((256, 1024), BF16),
            pltpu.VMEM((256, 1024), BF16),
            pltpu.VMEM((8, 176, 256), BF16),
            pltpu.VMEM((1024, 256), BF16),
            pltpu.VMEM((1024, 256), BF16),
            dma((8,)), dma((8,)), dma((16,)), dma((16,)), dma, dma, dma((8,)), dma((8,)),
            *row_sems(), *row_sems(), *col_sems(), *col_sems(),
        ],
        compiler_params=pltpu.CompilerParams(collective_id=0, has_side_effects=True, vmem_limit_bytes=9 * 2**20),
        name="layer",
    )(w_query, w_key, w_value, w_out, w_gate, w_up, w_down, small, hidden, cos, sin, lens, k_view, v_view)

    def shape(*dims):
        return jax.ShapeDtypeStruct(dims, BF16)

    outs = pl.pallas_call(
        store_kernel,
        out_shape=[shape(8, 64, 1024)] * 3 + [shape(16, 64, 512), shape(8, 176, 1024), shape(8, 176, 1024),
                   shape(16, 64, 1408), shape(256, 1024),
                   shape(4, 128), shape(4, 128), shape(4, 128), shape(8, 128), shape(8, 128)],
        in_specs=[anywhere] * 4 + [vmem, anywhere],
        out_specs=[hbm] * 8 + [vmem] * 5,
        scratch_shapes=[dma((10,))],
        compiler_params=pltpu.CompilerParams(vmem_limit_bytes=2 * 2**20),
        name="store",
    )(*held[:4], *held[6:])
    k_out, v_out = held[4:6]
    wq, wk, wv, wo, wg, wu, wd, hid, bq, bk, bv, ga, gm = outs
    flat = lambda a, n: a.reshape(-1, n)
    return (flat(wq, 1024), bq.reshape(512), flat(wk, 1024), bk.reshape(512), flat(wv, 1024), bv.reshape(512),
            flat(wo, 512), flat(wg, 1024), flat(wu, 1024), flat(wd, 1408), ga.reshape(1024), gm.reshape(1024),
            hid, jnp.transpose(k_out, (3, 0, 1, 2)), jnp.transpose(v_out, (3, 0, 1, 2)))


def solution(mesh):
    row_spec = P(("dp", "tp"), None)
    flat_spec = P(("dp", "tp"))
    cache_spec = P("dp", None, "tp", None)
    in_specs = (row_spec, flat_spec, row_spec, flat_spec, row_spec, flat_spec, row_spec, row_spec, row_spec, row_spec,
                flat_spec, flat_spec, P("dp", None), cache_spec, cache_spec, P("dp"))
    out_specs = (P("tp", None), P("tp"), P("tp", None), P("tp"), P("tp", None), P("tp"), P(None, "tp"), P("tp", None),
                 P("tp", None), P(None, "tp"), P(None), P(None), P("dp", None), cache_spec, cache_spec)
    return jax.shard_map(local_step, mesh=mesh, in_specs=in_specs, out_specs=out_specs, check_vma=False)
```

time: 296 us -> 130 us (0.44)
  Pallas kernels: 0 us -> 114 us
  waiting for transfers between devices: 105 us -> 0 us
  blocking collectives: 69.8 us -> 0 us
  other arithmetic: 40.5 us -> 0.98 us
  starting transfers between devices: 29.9 us -> 0 us
  between operations: 15.6 us -> 0.68 us
  matrix products: 12.1 us -> 0 us
  local copies, waits for them, and re-layouts: 22.6 us -> 13.1 us
    pallas_call x0 -> x2, Pallas kernels: none -> 114 us  [the longest x1 109 us: local_step(): pl.pallas_call(layer_kernel, out_shape=[pltpu.VMEM(s, BF16) for s in shap...]
    all_to_all x8 -> x0, waiting for transfers between devices: 76.4 us -> none  [head_rows(): swapped = lax.all_to_all(grouped, 'tp', 0, 0, tiled=True)]
    unnamed x2 -> x0, blocking collectives: 47.9 us -> none
    all_to_all x8 -> x0, starting transfers between devices: 29.3 us -> none  [head_rows(): swapped = lax.all_to_all(grouped, 'tp', 0, 0, tiled=True)]
    psum x2 -> x0, waiting for transfers between devices: 25 us -> none  [the longest x1 25 us: decode_step(): down_sum = lax.psum(down_part, 'tp')]
    all_to_all x2 -> x0, blocking collectives: 21.9 us -> none  [column_share(): swapped = lax.all_to_all(block, 'tp', 1, 0, tiled=True)]
    unnamed x2 -> x0, other arithmetic: 18.9 us -> none
    dot_general x1 -> x0, other arithmetic: 17.1 us -> none  [decode_step(): jnp.einsum('bkgs,bskd->bkgd', attn_probs, v_cache_new, preferred_element_...]
  transfers between devices with their start and end apart: 17 -> 0, of which waited for: 7 -> 0; matrix products, arithmetic and copies ran while one was open for 20% -> 0% of each run, Pallas kernels for 0% -> 0%
where the time goes in v1:
time: 130 us; the launch traced here: 129 us
  Pallas kernels  114 us (88%)
  local copies, waits for them, and re-layouts  13.1 us (10%)
    pallas_call x1, Pallas kernels, local_step(): pl.pallas_call(layer_kernel, out_shape=[pltpu.VMEM(s, BF16) for s in shap...  109 us
    unnamed x2, local copies, waits for them, and re-layouts  12.3 us
    pallas_call x1, Pallas kernels, local_step(): pl.pallas_call(store_kernel, out_shape=[shape(8, 64, 1024)] * 3 + [shape(...  5.51 us

profile of v1, /device:TPU:0, one launch (start us, length us, event | category | flops | bytes accessed | tf_op | source)
XLA Modules:
  0.0 128.8 jit_solution(14747582347569130891)
XLA Ops:
  0.7 0.7 convert_element_type.6
  1.3 0.7 stack.23
  2.1 0.1 fusion.2.small
  2.2 0.2 multiply_sine_fusion
  2.4 108.6 %layer.1 = (bf16[8,192,1024]{2,1,0:T(8,128)(2,1)S(1)}, bf16[8,352,1024]{2,1,0:T(8,128)(2,1)S(1)}, bf16[16,64,512]{2,1,0:T(8,128)(2,1)S(1)}, bf16[16,64,1408]{2,1...) custom-call(bf16[64,1024]{1,0:T(8,128)(2,1)} %wq.1, ...), custom_call_target="tpu_custom_call" | custom-call | tf_op jit(solution)/shard_map/layer/pallas_call | solution.py:450
  111.0 5.5 %store.1 = (bf16[8,64,1024]{2,1,0:T(8,128)(2,1)}, bf16[8,64,1024]{2,1,0:T(8,128)(2,1)}, bf16[8,64,1024]{2,1,0:T(8,128)(2,1)}, bf16[16,64,512]{2,1,0:T(8,128)(2,1...) custom-call(bf16[8,192,1024]{2,1,0:T(8,128)(2,1)S(1)} %get-tuple-ele, ...), custom_call_target="tpu_custom_call" | custom-call | tf_op jit(solution)/shard_map/store/pallas_call | solution.py:476
  116.5 6.2 %copy.33 = bf16[256,64,8,64]{0,3,2,1:T(8,128)(2,1)} copy(bf16[256,64,8,64]{0,3,2,1:T(8,128)(2,1)S(1)} %bitcast.23) | data formatting | bytes 33554432
  122.7 6.2 %copy.34 = bf16[256,64,8,64]{0,3,2,1:T(8,128)(2,1)} copy(bf16[256,64,8,64]{0,3,2,1:T(8,128)(2,1)S(1)} %bitcast.22) | data formatting | bytes 33554432
  (2 shorter events, 0.0 us)

commit v2 on v1

v2 whole, which is shorter than its diff:
```python
import jax
import jax.numpy as jnp
from jax import lax
from jax.experimental import pallas as pl
from jax.experimental.pallas import tpu as pltpu
from jax.sharding import PartitionSpec as P

EPS = 1e-6
THETA = 1000000.0
MESH = pl.DeviceIdType.MESH
F32 = jnp.float32
BF16 = jnp.bfloat16
ROW_BYTES = (((1,), (1,)), ((), ()))
NAT = (((1,), (0,)), ((), ()))
GROUP = 8


def dot(lhs, rhs, dims):
    return lax.dot_general(lhs, rhs, dims, preferred_element_type=F32)


HOME_STEPS = (
    (
        ("s", "q0", 0, "c", 0), ("s", "q1", 0, "c", 0), ("s", "q2", 0, "c", 0), ("s", "g0", 0, "c", 0),
        ("s", "g1", 0, "c", 0), ("s", "u0", 0, "c", 0), ("s", "u1", 0, "c", 0), ("s", "o", 0, "c", 0),
        ("s", "d", 0, "c", 0), ("s", "o", "z", "z", 4), ("s", "d", "z", "z", 4), ("s", "q0", 0, "y", 0),
        ("s", "q0", 0, "x", 1),
    ),
    (
        ("s", "q2", 0, "y", 0), ("s", "q2", 0, "x", 1),
    ),
    (
        ("s", "o", 0, "y", 2), ("s", "o", 0, "x", 1), ("w", "q0", "c", 0), ("w", "q1", "c", 0), ("w", "q2", "c", 0),
    ),
    (
        ("w", "q0", "t"), ("w", "q0", 1), ("s", "q0", 1, "c", 1), ("w", "q0", 2), ("s", "q0", 2, "c", 2),
        ("s", "q0", "t", "z", 2), ("s", "q1", 0, "y", 0), ("s", "q1", 0, "x", 1), ("w", "o", 2), ("s", "o", 2, "c", 2),
        ("w", "q2", 1), ("s", "q2", 1, "c", 1), ("w", "q2", 2), ("s", "q2", 2, "c", 2), ("s", "q2", 2, "y", 2),
        ("s", "q2", 2, "x", 3), ("w", "o", 1), ("s", "o", 1, "c", 1), ("w", "o", 4), ("s", "o", 4, "c", 4),
        ("w", "q1", "t"), ("s", "q1", "t", "z", 2), ("w", "o", 6), ("s", "o", 6, "c", 6), ("s", "o", 4, "y", 6),
        ("s", "o", 4, "x", 5), ("w", "q1", 1), ("s", "q1", 1, "c", 1), ("w", "q1", 2), ("s", "q1", 2, "c", 2),
    ),
    (
        ("s", "q1", 1, "y", 1), ("s", "o", 2, "x", 3), ("w", "q0", "c", 1), ("w", "q1", "c", 1), ("w", "q2", "c", 1),
    ),
    (
        ("w", "u1", "t"), ("w", "q2", 3), ("s", "q2", 3, "c", 3), ("s", "u1", "t", "z", 2), ("s", "u1", 0, "y", 0),
        ("s", "o", 6, "x", 7), ("s", "q1", 2, "x", 3),
    ),
    (
        ("w", "u1", 2), ("s", "u1", 2, "c", 2), ("w", "o", 5), ("s", "o", 5, "c", 5), ("w", "q0", "c", 2),
        ("w", "q1", "c", 2), ("w", "q2", "c", 2),
    ),
    (
        ("w", "o", 3), ("s", "o", 3, "c", 3), ("w", "g0", "t"), ("w", "o", 7), ("s", "o", 7, "c", 7),
        ("s", "g0", "t", "z", 2), ("s", "o", 5, "y", 7), ("s", "u1", 0, "x", 1), ("w", "u0", 2), ("s", "u0", 2, "c", 2),
        ("s", "u0", 0, "y", 0), ("w", "q1", 3), ("s", "q1", 3, "c", 3), ("w", "g1", "t"), ("s", "g1", "t", "z", 2),
        ("s", "u0", 0, "x", 1), ("w", "g0", 2), ("s", "g0", 2, "c", 2), ("s", "u0", 2, "y", 2), ("w", "q0", 3),
        ("s", "q0", 3, "c", 3),
    ),
    (
        ("w", "u1", 1), ("s", "u1", 1, "c", 1), ("s", "g0", 0, "x", 1), ("w", "q0", "c", 3), ("w", "q1", "c", 3),
        ("w", "q2", "c", 3),
    ),
    (
        ("w", "g1", 2), ("s", "g1", 2, "c", 2), ("s", "g0", 0, "y", 0), ("w", "o", "c", 0), ("w", "o", "c", 1),
        ("w", "o", "c", 2), ("w", "o", "c", 3), ("w", "o", "c", 4), ("w", "o", "c", 5), ("w", "o", "c", 6),
        ("w", "o", "c", 7),
    ),
    (
        ("w", "d", 2), ("s", "d", 2, "c", 2), ("w", "u0", 1), ("s", "u0", 1, "c", 1), ("s", "g1", 0, "x", 1),
        ("w", "d", 4), ("s", "d", 4, "c", 4), ("s", "u0", 1, "y", 1), ("w", "d", 6), ("s", "d", 6, "c", 6),
        ("w", "g0", 1), ("s", "g0", 1, "c", 1), ("s", "g1", 2, "x", 3), ("s", "g1", 0, "y", 0), ("w", "u1", 3),
        ("s", "u1", 3, "c", 3), ("w", "g1", 1), ("s", "g1", 1, "c", 1), ("s", "d", 0, "x", 1), ("s", "g1", 1, "y", 1),
        ("w", "g1", 3), ("s", "g1", 3, "c", 3), ("s", "d", 4, "x", 5), ("w", "g0", 3), ("s", "g0", 3, "c", 3),
    ),
    (
        ("s", "d", 0, "y", 2),
    ),
    (
        ("w", "d", 1), ("s", "d", 1, "c", 1), ("w", "g0", "c", 0), ("w", "g1", "c", 0), ("w", "u0", "c", 0),
        ("w", "u1", "c", 0),
    ),
    (
        ("s", "d", 2, "x", 3),
    ),
    (
        ("w", "u0", 3), ("s", "u0", 3, "c", 3), ("w", "g0", "c", 1), ("w", "g1", "c", 1), ("w", "u0", "c", 1),
        ("w", "u1", "c", 1),
    ),
    (),
    (
        ("s", "d", 4, "y", 6), ("w", "g0", "c", 2), ("w", "g1", "c", 2), ("w", "u0", "c", 2), ("w", "u1", "c", 2),
    ),
    (),
    (
        ("w", "d", 5), ("s", "d", 5, "c", 5), ("w", "g0", "c", 3), ("w", "g1", "c", 3), ("w", "u0", "c", 3),
        ("w", "u1", "c", 3),
    ),
    (),
    (
        ("w", "d", "c", 0), ("w", "d", "c", 4),
    ),
    (),
    (
        ("s", "d", 5, "y", 7), ("w", "d", "c", 1), ("w", "d", "c", 5),
    ),
    (),
    (
        ("w", "d", "c", 2), ("w", "d", "c", 6),
    ),
    (
        ("w", "d", 3), ("s", "d", 3, "c", 3), ("w", "d", 7), ("s", "d", 7, "c", 7),
    ),
    (
        ("w", "d", "c", 3), ("w", "d", "c", 7),
    ),
    (),
    (),
    (),
    (),
    (),
    (),
    (),
    (),
    (),
)
HOME_BLOCKS = {
    "attend": ((0, 0), (0, 1), (1, 0), (1, 1), (2, 0), (2, 1), (3, 0), (3, 1)),
    "gated": ((0, 0), (0, 1), (1, 0), (1, 1), (2, 0), (2, 1), (3, 0), (3, 1)),
    "down": ((0, 0), (0, 1), (1, 0), (1, 1), (2, 0), (2, 1), (3, 0), (3, 1)),
}
AWAY_STEPS = (
    (
        ("s", "o", 0, "c", 0), ("s", "d", 0, "c", 0), ("s", "q0", "own", "z", 2), ("s", "q0", "own", "y", "t"),
        ("s", "o", 0, "x", 1), ("s", "d", 0, "x", 1),
    ),
    (
        ("s", "q2", "own", "z", 2), ("s", "o", 0, "y", 2), ("s", "q1", "own", "y", "t"), ("w", "o", 1),
        ("s", "o", 1, "c", 1), ("w", "o", 4), ("s", "o", 4, "c", 4), ("s", "o", 4, "x", 5), ("s", "o", "z", "z", 4),
        ("w", "q0", 0), ("s", "q0", 0, "c", 0), ("s", "q0", 0, "x", 1), ("s", "q1", "own", "z", 2),
        ("s", "o", 4, "y", 6), ("s", "u1", "own", "y", "t"), ("w", "d", 1), ("s", "d", 1, "c", 1), ("w", "d", 4),
        ("s", "d", 4, "c", 4), ("w", "q2", 0), ("s", "q2", 0, "c", 0), ("s", "q2", 0, "x", 1),
        ("s", "u1", "own", "z", 2), ("w", "o", 5), ("s", "o", 5, "c", 5), ("w", "o", 2), ("s", "o", 2, "c", 2),
        ("s", "g0", "own", "y", "t"), ("s", "o", 2, "x", 3), ("w", "q0", 2), ("s", "q0", 2, "c", 2), ("w", "q0", 1),
        ("s", "q0", 1, "c", 1), ("w", "q1", 0), ("s", "q1", 0, "c", 0),
    ),
    (
        ("s", "u0", "own", "z", 2), ("s", "q0", 2, "x", 3), ("w", "q0", "c", 0), ("w", "q1", "c", 0),
        ("w", "q2", "c", 0),
    ),
    (
        ("w", "q1", 2), ("s", "q1", 2, "c", 2), ("w", "q2", 1), ("s", "q2", 1, "c", 1), ("w", "q2", 2),
        ("s", "q2", 2, "c", 2), ("s", "g1", "own", "y", "t"), ("s", "q2", 2, "x", 3),
    ),
    (
        ("w", "o", 3), ("s", "o", 3, "c", 3), ("w", "o", 6), ("s", "o", 6, "c", 6), ("s", "g0", "own", "z", 2),
        ("s", "q1", 2, "x", 3), ("w", "q0", "c", 2), ("w", "q1", "c", 2), ("w", "q2", "c", 2),
    ),
    (
        ("w", "q0", 3), ("s", "q0", 3, "c", 3), ("w", "q1", 1), ("s", "q1", 1, "c", 1), ("s", "q0", 3, "y", 3),
    ),
    (
        ("w", "q2", 3), ("s", "q2", 3, "c", 3), ("w", "u1", 2), ("s", "u1", 2, "c", 2), ("s", "g1", "own", "z", 2),
        ("s", "d", 0, "y", 2), ("s", "u1", 2, "x", 3), ("w", "q0", "c", 1), ("w", "q1", "c", 1), ("w", "q2", "c", 1),
    ),
    (
        ("w", "u1", 0), ("s", "u1", 0, "c", 0), ("s", "d", "z", "z", 4), ("w", "o", 7), ("s", "o", 7, "c", 7),
        ("w", "q1", 3), ("s", "q1", 3, "c", 3),
    ),
    (
        ("w", "g0", 2), ("s", "g0", 2, "c", 2), ("s", "d", 4, "y", 6), ("s", "u1", 0, "x", 1), ("w", "q0", "c", 3),
        ("w", "q1", "c", 3), ("w", "q2", "c", 3),
    ),
    (
        ("w", "u0", 0), ("s", "u0", 0, "c", 0), ("w", "o", "c", 0), ("w", "o", "c", 1), ("w", "o", "c", 2),
        ("w", "o", "c", 3), ("w", "o", "c", 4), ("w", "o", "c", 5), ("w", "o", "c", 6), ("w", "o", "c", 7),
    ),
    (
        ("w", "u1", 3), ("s", "u1", 3, "c", 3), ("s", "u1", 3, "y", 3), ("s", "g0", 2, "x", 3), ("w", "g1", 2),
        ("s", "g1", 2, "c", 2), ("w", "u0", 2), ("s", "u0", 2, "c", 2), ("w", "u1", 1), ("s", "u1", 1, "c", 1),
        ("s", "u0", 2, "x", 3), ("w", "g0", 0), ("s", "g0", 0, "c", 0), ("w", "g0", 3), ("s", "g0", 3, "c", 3),
        ("s", "g0", 3, "y", 3), ("s", "g0", 0, "x", 1), ("w", "u0", 1), ("s", "u0", 1, "c", 1), ("w", "u0", 3),
        ("s", "u0", 3, "c", 3), ("s", "u0", 3, "y", 3), ("s", "g1", 2, "x", 3),
    ),
    (
        ("w", "g1", 0), ("s", "g1", 0, "c", 0), ("w", "g0", 1), ("s", "g0", 1, "c", 1), ("s", "d", 4, "x", 5),
    ),
    (),
    (
        ("w", "g0", "c", 2), ("w", "g1", "c", 2), ("w", "u0", "c", 2), ("w", "u1", "c", 2),
    ),
    (
        ("w", "g0", "c", 0), ("w", "g1", "c", 0), ("w", "u0", "c", 0), ("w", "u1", "c", 0),
    ),
    (
        ("w", "g1", 1), ("s", "g1", 1, "c", 1),
    ),
    (
        ("w", "g1", 3), ("s", "g1", 3, "c", 3),
    ),
    (
        ("w", "g0", "c", 1), ("w", "g1", "c", 1), ("w", "u0", "c", 1), ("w", "u1", "c", 1),
    ),
    (
        ("w", "g0", "c", 3), ("w", "g1", "c", 3), ("w", "u0", "c", 3), ("w", "u1", "c", 3),
    ),
    (),
    (
        ("w", "d", 2), ("s", "d", 2, "c", 2), ("s", "d", 2, "x", 3), ("w", "d", "c", 0), ("w", "d", "c", 4),
    ),
    (
        ("w", "d", 5), ("s", "d", 5, "c", 5), ("s", "d", 5, "y", 7),
    ),
    (
        ("w", "d", "c", 1), ("w", "d", "c", 5),
    ),
    (
        ("w", "d", 6), ("s", "d", 6, "c", 6),
    ),
    (
        ("w", "d", "c", 2), ("w", "d", "c", 6),
    ),
    (
        ("w", "d", 3), ("s", "d", 3, "c", 3), ("w", "d", 7), ("s", "d", 7, "c", 7),
    ),
    (
        ("w", "d", "c", 3), ("w", "d", "c", 7),
    ),
    (),
    (),
    (),
    (),
    (),
    (),
    (),
    (),
    (),
)
AWAY_BLOCKS = {
    "attend": ((0, 0), (0, 1), (2, 0), (2, 1), (1, 0), (1, 1), (3, 0), (3, 1)),
    "gated": ((0, 0), (2, 0), (2, 1), (0, 1), (1, 0), (3, 0), (1, 1), (3, 1)),
    "down": ((0, 0), (0, 1), (1, 0), (1, 1), (2, 0), (2, 1), (3, 0), (3, 1)),
}


class Place:
    def __init__(self):
        tp = lax.axis_index("tp")
        dp = lax.axis_index("dp")
        self.z = tp
        self.dp = dp
        self.y = dp // 4
        self.x = (dp // 2) % 2
        self.c = dp % 2
        self.far = lax.rem(self.y + self.z, 2)
        self.device = {
            "x": (tp, dp + 2 - 4 * self.x),
            "y": (tp, dp + 4 - 8 * self.y),
            "c": (tp, dp + 1 - 2 * self.c),
            "z": (1 - tp, dp),
        }

    def at(self, axis, flip):
        here = getattr(self, axis)
        return 1 - here if flip else here

    def row_block(self, k, core=0):
        return (self.at("x", k & 1) * 2 + self.at("c", core)) * 2 + self.at("z", k & 2)

    def col_block(self, k, core=0):
        return (self.at("y", k & 2) * 4 + self.at("x", k & 1) * 2 + self.at("c", core)) * 2 + self.at("z", k & 4)


def remote(src, dst, send, recv, device):
    return pltpu.make_async_remote_copy(
        src_ref=src, dst_ref=dst, send_sem=send, recv_sem=recv, device_id=device, device_id_type=MESH)


class Rows:
    def __init__(self, place, buf, start, own, through, index, sems):
        self.p, self.buf, self.start, self.own, self.through = place, buf, start, own, through
        self.i, (self.send, self.r, self.rc) = index, sems
        self.n = own.shape[0]

    def block(self, k, core=0):
        return self.buf.at[self.p.row_block(k, core), pl.ds(self.start, self.n)]

    def copy(self, k, link, home):
        p = self.p
        slot = {"own": 0, "t": 4}.get(k, k)
        send = self.send.at[self.i, "xyzc".index(link), slot]
        if k == "own" or (home and k == 0):
            src = self.own
        elif k == "t":
            src = self.through
        else:
            src = self.block(k)
        if k == "own" and link == "y":
            dst, recv = self.through, self.r.at[self.i, 4]
        else:
            dst = self.block(0 if k in ("own", "t") else k)
            got = 2 if link == "z" else k ^ 1 if link == "x" else k
            recv = self.rc.at[self.i, k] if link == "c" else self.r.at[self.i, got]
        return remote(src, dst, send, recv, p.device[link])

    def wait(self, k, core):
        if k == "t":
            ref, recv = self.through, self.r.at[self.i, 4]
        else:
            ref, recv = self.block(k, core), (self.rc if core else self.r).at[self.i, k]
        remote(ref, ref, self.send.at[self.i, 0, 0], recv, self.p.device["x"]).wait_recv()

    def local(self):
        @pl.when(self.p.far == 0)
        def _():
            self.buf[self.p.row_block(0), pl.ds(self.start, self.n)] = self.own[...]


class Cols:
    def __init__(self, place, buf, own, index, sems):
        self.p, self.buf, self.own = place, buf, own
        self.n = buf.shape[-1]
        self.i, (self.send, self.r, self.rc) = index, sems

    def block(self, k, core=0):
        return self.buf.at[self.p.col_block(k, core)]

    def half(self, z):
        return self.own.at[:, pl.ds(pl.multiple_of(z * self.n, 128), self.n)]

    def copy(self, k, link, home):
        p = self.p
        if link == "z":
            return remote(self.half(1 - p.z), self.block(0), self.send.at[self.i, 2, 0], self.r.at[self.i, 4], p.device["z"])
        src = self.half(p.z) if k == 0 else self.block(k)
        got = k ^ 1 if link == "x" else k ^ 2
        recv = self.rc.at[self.i, k] if link == "c" else self.r.at[self.i, got]
        return remote(src, self.block(k), self.send.at[self.i, "xyzc".index(link), k], recv, p.device[link])

    def wait(self, k, core):
        ref, recv = self.block(k, core), (self.rc if core else self.r).at[self.i, k]
        remote(ref, ref, self.send.at[self.i, 0, 0], recv, self.p.device["x"]).wait_recv()

    def local(self):
        self.buf[self.p.col_block(0)] = self.own[:, pl.ds(pl.multiple_of(self.p.z * self.n, 128), self.n)]


def layer_kernel(wq, wk, wv, wo, wg, wu, wd, small, x_ref, cos_ref, sin_ref, len_ref, k_hbm, v_hbm,
                 wqkv, wgu, wout, wdn, k_lo, k_hi, v_lo, v_hi, smalls, hid,
                 h_ref, sc_ref, o_ref, part, part_in, x1_ref, h2_ref, a_ref, down, down_in, t_q, t_gu,
                 k_sem, v_sem, s_send, s_recv, p_send, p_recv, d_send, d_recv, row_s, row_r, row_c, col_s, col_r, col_c):
    place = Place()
    me = place.dp * 2 + place.z
    row_sem, col_sem = (row_s, row_r, row_c), (col_s, col_r, col_c)
    half = pl.ds(0, 88), pl.ds(88, 88)
    chunks = {}
    for i, ref in enumerate((wq, wk, wv)):
        chunks[f"q{i}"] = Rows(place, wqkv, 64 * i, ref, t_q.at[i], i, row_sem)
    for i in range(4):
        ref = (wg, wu)[i // 2].at[half[i % 2]]
        chunks["gu"[i // 2] + str(i % 2)] = Rows(place, wgu, 88 * i, ref, t_gu.at[i], 3 + i, row_sem)
    chunks["o"] = Cols(place, wout, wo, 0, col_sem)
    chunks["d"] = Cols(place, wdn, wd, 1, col_sem)
    roles = ((0, HOME_STEPS, HOME_BLOCKS), (1, AWAY_STEPS, AWAY_BLOCKS))
    step = iter(range(len(HOME_STEPS)))

    def go():
        now = next(step)
        for far, steps, _ in roles:
            if steps[now]:
                @pl.when(place.far == far)
                def _(far=far, steps=steps):
                    for action in steps[now]:
                        chunk = chunks[action[1]]
                        if action[0] == "s":
                            chunk.copy(action[2], action[3], far == 0).start()
                        elif action[2] == "c":
                            chunk.wait(action[3], 1)
                        else:
                            chunk.wait(action[2], 0)

    def by_role(kind, i, place_of, swap=False):
        home, away = (place_of(*blocks[kind][i]) for _, _, blocks in roles)
        if swap:
            home, away = away, home
        return home + place.far * (away - home)

    def cache_copy(i):
        head = by_role("attend", i, place.row_block)
        copies = []
        for hbm, lo, hi, sem in ((k_hbm, k_lo, k_hi, k_sem), (v_hbm, v_lo, v_hi, v_sem)):
            copies.append(pltpu.make_async_copy(hbm.at[pl.ds(0, 32), head], lo.at[:, head], sem.at[2 * i]))
            copies.append(pltpu.make_async_copy(hbm.at[pl.ds(32, 32), head], hi.at[:, head], sem.at[2 * i + 1]))
        return copies

    barrier = pltpu.get_barrier_semaphore()
    for i in range(1, 16):
        other = lax.rem(me + i, 16)
        pl.semaphore_signal(barrier, inc=1, device_id=(other % 2, other // 2), device_id_type=MESH)
    for i in range(8):
        for copy in cache_copy(i):
            copy.start()
    pl.semaphore_wait(barrier, 15)

    def small_copy(i):
        other = lax.rem(me + i, 16)
        return remote(small, smalls.at[me], s_send.at[i], s_recv.at[i], (other % 2, other // 2))

    for i in range(1, 16):
        small_copy(i).start()
    go()

    for chunk in chunks.values():
        chunk.local()
    smalls[me] = small[...]
    for i in range(1, 16):
        small_copy(i).wait_recv()

    def gain_row(i):
        pair = smalls[...].astype(F32).reshape(8, 2, 8, 128)
        rows = pair[:, 0, i] + pair[:, 1, i]
        return jnp.concatenate([rows[d:d + 1] for d in range(8)], axis=1)

    def normed(rows, i):
        inv = lax.rsqrt(jnp.mean(rows * rows, axis=-1, keepdims=True) + EPS)
        return (rows * inv * gain_row(i)).astype(BF16)

    h_ref[...] = normed(x_ref[...].astype(F32), 3)

    eye = lax.broadcasted_iota(jnp.int32, (64, 128), 1) % 64 == lax.broadcasted_iota(jnp.int32, (64, 128), 0)

    def bias_column(head, i):
        row = smalls[place.z * 8 + head].astype(F32)[i:i + 1]
        return jnp.sum(jnp.where(eye, row, 0.0), axis=1, keepdims=True)

    def attend(i):
        head = by_role("attend", i, place.row_block)
        res = dot(wqkv[head], h_ref[...], ROW_BYTES)
        cos, sin = cos_ref[...], sin_ref[...]

        def rotated(start, b):
            v = (res[start:start + 64] + bias_column(head, b)).astype(BF16).astype(F32)
            lo, hi = v[:32], v[32:]
            return jnp.concatenate([lo * cos - hi * sin, hi * cos + lo * sin], axis=0).astype(BF16)

        q = rotated(0, 0).astype(F32)
        k_new = rotated(64, 1)
        v_new = (res[128:192] + bias_column(head, 2)).astype(BF16)
        lens = len_ref[...]
        for copy in cache_copy(i):
            copy.wait()

        for base, buf in ((0, k_lo), (32, k_hi)):
            def score_group(g, carry, base=base, buf=buf):
                rows = []
                for j in range(GROUP):
                    s = g * GROUP + j
                    kv = jnp.where(lens == (base + s).astype(F32), k_new.astype(F32), buf[s, head].astype(F32))
                    buf[s, head] = kv.astype(BF16)
                    rows.append(jnp.sum(q * kv, axis=0, keepdims=True))
                sc_ref[pl.ds(pl.multiple_of(base + g * GROUP, GROUP), GROUP)] = jnp.concatenate(rows, axis=0)
                return carry

            lax.fori_loop(0, 32 // GROUP, score_group, 0)
        slot = lax.broadcasted_iota(jnp.int32, (64, 256), 0).astype(F32)
        scores = jnp.where(slot <= lens, sc_ref[...] * 0.125, -1e30)
        e = jnp.exp(scores - jnp.max(scores, axis=0, keepdims=True))
        sc_ref[...] = (e / jnp.sum(e, axis=0, keepdims=True)).astype(BF16).astype(F32)

        acc = jnp.zeros((64, 256), F32)
        for base, buf in ((0, v_lo), (32, v_hi)):
            def value_group(g, acc, base=base, buf=buf):
                probs = sc_ref[pl.ds(pl.multiple_of(base + g * GROUP, GROUP), GROUP)]
                for j in range(GROUP):
                    s = g * GROUP + j
                    vv = jnp.where(lens == (base + s).astype(F32), v_new.astype(F32), buf[s, head].astype(F32))
                    buf[s, head] = vv.astype(BF16)
                    acc = acc + probs[j:j + 1] * vv
                return acc

            acc = lax.fori_loop(0, 32 // GROUP, value_group, acc)
        o_ref[pl.ds(pl.multiple_of(head * 64, 64), 64)] = acc.astype(BF16)

    go()
    for i in range(8):
        attend(i)
        go()

    o = o_ref[...].T
    part[...] = dot(o, wout[...].reshape(1024, 512), ROW_BYTES).astype(BF16)
    swap = remote(part, part_in, p_send, p_recv, place.device["z"])
    swap.start()
    go()
    swap.wait_recv()
    total = (part[...].astype(F32) + part_in[...].astype(F32)).astype(BF16)
    x1 = (x_ref[...].astype(F32) + total.astype(F32)).astype(BF16)
    x1_ref[...] = x1
    h2_ref[...] = normed(x1.astype(F32), 4)
    go()

    for i in range(8):
        block = by_role("gated", i, place.row_block)
        res = dot(wgu[block], h2_ref[...], ROW_BYTES).astype(BF16).astype(F32)
        g, u = res[:176], res[176:]
        a_ref[block] = (g / (1.0 + jnp.exp(-g)) * u).astype(BF16)
        go()

    def pair_of(k, core):
        return place.col_block(k, core) // 2

    def down_copy(i, swap=False):
        pair = by_role("down", i, pair_of, swap)
        rows = pl.ds(pl.multiple_of(pair * 128, 128), 128)
        return rows, pair, remote(down.at[rows], down_in.at[rows], d_send.at[pair], d_recv.at[pair], place.device["z"])

    for i in range(8):
        rows, pair, copy = down_copy(i)
        w = wdn[pl.ds(pair * 2, 2)].reshape(128, 1408)
        down[rows] = dot(w, a_ref[...].reshape(1408, 256), NAT).astype(BF16)
        copy.start()
        go()
    for i in range(8):
        rows, _, copy = down_copy(i, True)
        copy.wait_recv()
        both = (down[rows].astype(F32) + down_in[rows].astype(F32)).T.astype(BF16).astype(F32)
        hid[:, rows] = (x1_ref[:, rows].astype(F32) + both).astype(BF16)
        go()

    for far, steps, _ in roles:
        @pl.when(place.far == far)
        def _(far=far, steps=steps):
            for action in sum(steps, ()):
                if action[0] == "s":
                    chunks[action[1]].copy(action[2], action[3], far == 0).wait_send()

    for i in range(1, 16):
        small_copy(i).wait_send()
    swap.wait_send()
    for i in range(8):
        down_copy(i)[2].wait_send()


def store_kernel(wqkv, wgu, wout, wdn, k_lo, k_hi, v_lo, v_hi, smalls, hid,
                 wq, wk, wv, wo, wg, wu, wd, k_out, v_out, hid_out, bq, bk, bv, ga, gm, sem):
    lo, hi = pl.ds(0, 32), pl.ds(32, 32)
    pairs = [(k_lo, k_out.at[lo]), (k_hi, k_out.at[hi]), (v_lo, v_out.at[lo]), (v_hi, v_out.at[hi]),
             (wdn, wd), (wgu.at[:, pl.ds(0, 176)], wg), (wgu.at[:, pl.ds(176, 176)], wu),
             (wqkv.at[:, pl.ds(0, 64)], wq), (wqkv.at[:, pl.ds(64, 64)], wk), (wqkv.at[:, pl.ds(128, 64)], wv),
             (wout, wo), (hid, hid_out)]
    copies = [pltpu.make_async_copy(src, dst, sem.at[i]) for i, (src, dst) in enumerate(pairs)]
    for copy in copies:
        copy.start()
    z = lax.axis_index("tp")
    plane = smalls[pl.ds(z * 8, 8)].astype(F32).reshape(4, 2, 8, 128)
    whole = smalls[...].astype(F32).reshape(8, 2, 8, 128)
    for i, ref in enumerate((bq, bk, bv)):
        ref[...] = (plane[:, 0, i] + plane[:, 1, i]).astype(BF16)
    for i, ref in enumerate((ga, gm)):
        ref[...] = (whole[:, 0, 3 + i] + whole[:, 1, 3 + i]).astype(BF16)
    for copy in copies:
        copy.wait()


def local_step(w_query, b_query, w_key, b_key, w_value, b_value, w_out, w_gate, w_up, w_down, gain_attn, gain_mlp,
               hidden, k_cache, v_cache, lengths):
    z = lax.axis_index("tp")
    vectors = jnp.stack([b_query, b_key, b_value, gain_attn, gain_mlp])
    zeros = jnp.zeros_like(vectors)
    small = jnp.concatenate([jnp.where(z == 0, vectors, zeros), jnp.where(z == 0, zeros, vectors)], axis=1)
    small = jnp.pad(small, ((0, 3), (0, 0)))
    inv_freq = 1.0 / (THETA ** (jnp.arange(0, 64, 2, dtype=F32) / 64))
    angles = inv_freq[:, None] * lengths.astype(F32)[None, :]
    cos, sin = jnp.cos(angles), jnp.sin(angles)
    lens = lengths.astype(F32)[None, :]
    k_view = jnp.transpose(k_cache, (1, 2, 3, 0))
    v_view = jnp.transpose(v_cache, (1, 2, 3, 0))

    vmem = pl.BlockSpec(memory_space=pltpu.VMEM)
    hbm = pl.BlockSpec(memory_space=pltpu.HBM)
    anywhere = pl.BlockSpec(memory_space=pl.ANY)
    dma = pltpu.SemaphoreType.DMA
    shapes = [(8, 192, 1024), (8, 352, 1024), (16, 64, 512), (16, 64, 1408), *[(32, 8, 64, 256)] * 4,
              (16, 8, 128), (256, 1024)]
    held = pl.pallas_call(
        layer_kernel,
        out_shape=[pltpu.VMEM(s, BF16) for s in shapes],
        in_specs=[vmem] * 12 + [hbm] * 2,
        out_specs=[vmem] * 10,
        scratch_shapes=[
            pltpu.VMEM((256, 1024), BF16),
            pltpu.VMEM((64, 256), F32),
            pltpu.VMEM((512, 256), BF16),
            pltpu.VMEM((256, 1024), BF16),
            pltpu.VMEM((256, 1024), BF16),
            pltpu.VMEM((256, 1024), BF16),
            pltpu.VMEM((256, 1024), BF16),
            pltpu.VMEM((8, 176, 256), BF16),
            pltpu.VMEM((1024, 256), BF16),
            pltpu.VMEM((1024, 256), BF16),
            pltpu.VMEM((3, 64, 1024), BF16),
            pltpu.VMEM((4, 88, 1024), BF16),
            dma((16,)), dma((16,)), dma((16,)), dma((16,)), dma, dma, dma((8,)), dma((8,)),
            dma((7, 4, 5)), dma((7, 5)), dma((7, 4)), dma((2, 4, 8)), dma((2, 8)), dma((2, 8)),
        ],
        compiler_params=pltpu.CompilerParams(collective_id=0, has_side_effects=True, vmem_limit_bytes=10 * 2**20),
        name="layer",
    )(w_query, w_key, w_value, w_out, w_gate, w_up, w_down, small, hidden, cos, sin, lens, k_view, v_view)

    def shape(*dims):
        return jax.ShapeDtypeStruct(dims, BF16)

    outs = pl.pallas_call(
        store_kernel,
        out_shape=[shape(8, 64, 1024)] * 3 + [shape(16, 64, 512), shape(8, 176, 1024), shape(8, 176, 1024),
                   shape(16, 64, 1408), shape(*k_view.shape), shape(*v_view.shape), shape(256, 1024),
                   shape(4, 128), shape(4, 128), shape(4, 128), shape(8, 128), shape(8, 128)],
        in_specs=[anywhere] * 8 + [vmem, anywhere],
        out_specs=[hbm] * 10 + [vmem] * 5,
        scratch_shapes=[dma((12,))],
        compiler_params=pltpu.CompilerParams(vmem_limit_bytes=2 * 2**20),
        name="store",
    )(*held)
    wq, wk, wv, wo, wg, wu, wd, k_out, v_out, hid, bq, bk, bv, ga, gm = outs
    flat = lambda a, n: a.reshape(-1, n)
    return (flat(wq, 1024), bq.reshape(512), flat(wk, 1024), bk.reshape(512), flat(wv, 1024), bv.reshape(512),
            flat(wo, 512), flat(wg, 1024), flat(wu, 1024), flat(wd, 1408), ga.reshape(1024), gm.reshape(1024),
            hid, jnp.transpose(k_out, (3, 0, 1, 2)), jnp.transpose(v_out, (3, 0, 1, 2)))


def solution(mesh):
    row_spec = P(("dp", "tp"), None)
    flat_spec = P(("dp", "tp"))
    cache_spec = P("dp", None, "tp", None)
    in_specs = (row_spec, flat_spec, row_spec, flat_spec, row_spec, flat_spec, row_spec, row_spec, row_spec, row_spec,
                flat_spec, flat_spec, P("dp", None), cache_spec, cache_spec, P("dp"))
    out_specs = (P("tp", None), P("tp"), P("tp", None), P("tp"), P("tp", None), P("tp"), P(None, "tp"), P("tp", None),
                 P("tp", None), P(None, "tp"), P(None), P(None), P("dp", None), cache_spec, cache_spec)
    return jax.shard_map(local_step, mesh=mesh, in_specs=in_specs, out_specs=out_specs, check_vma=False)
```

time: 130 us -> 95.7 us (0.74)
  Pallas kernels: 114 us -> 91.8 us
  local copies, waits for them, and re-layouts: 13.1 us -> 0.75 us
    pallas_call x1, Pallas kernels: 109 us -> 76.1 us  [local_step(): pl.pallas_call(layer_kernel, out_shape=[pltpu.VMEM(s, BF16) for s in shap...]
    unnamed x2, local copies, waits for them, and re-layouts: 12.3 us -> 0.01 us
    pallas_call x1, Pallas kernels: 5.51 us -> 15.7 us  [local_step(): pl.pallas_call(store_kernel, out_shape=[shape(8, 64, 1024)] * 3 + [shape(...]
where the time goes in v2:
time: 95.7 us; the launch traced here: 95.6 us
  Pallas kernels  91.8 us (96%)
  other arithmetic  2.18 us (2%)
    pallas_call x1, Pallas kernels, local_step(): pl.pallas_call(layer_kernel, out_shape=[pltpu.VMEM(s, BF16) for s in shap...  76.1 us
    pallas_call x1, Pallas kernels, local_step(): pl.pallas_call(store_kernel, out_shape=[shape(8, 64, 1024)] * 3 + [shape(...  15.7 us

profile of v2, /device:TPU:0, one launch (start us, length us, event | category | flops | bytes accessed | tf_op | source)
XLA Modules:
  0.0 95.6 jit_solution(10333497131957144837)
XLA Ops:
  0.7 0.7 convert_element_type.6
  1.4 0.0 copy-start
  1.4 0.7 stack.23
  2.1 0.7 fusion.2.small
  2.8 0.8 multiply_sine_fusion
  3.6 0.0 copy-done
  3.6 76.1 %layer.1 = (bf16[8,192,1024]{2,1,0:T(8,128)(2,1)S(1)}, bf16[8,352,1024]{2,1,0:T(8,128)(2,1)S(1)}, bf16[16,64,512]{2,1,0:T(8,128)(2,1)S(1)}, bf16[16,64,1408]{2,1...) custom-call(bf16[64,1024]{1,0:T(8,128)(2,1)} %wq.1, ...), custom_call_target="tpu_custom_call" | custom-call | tf_op jit(solution)/shard_map/layer/pallas_call | solution.py:585
  79.7 15.7 %store.1 = (bf16[8,64,1024]{2,1,0:T(8,128)(2,1)}, bf16[8,64,1024]{2,1,0:T(8,128)(2,1)}, bf16[8,64,1024]{2,1,0:T(8,128)(2,1)}, bf16[16,64,512]{2,1,0:T(8,128)(2,1...) custom-call(bf16[8,192,1024]{2,1,0:T(8,128)(2,1)S(1)} %get-tuple-ele, ...), custom_call_target="tpu_custom_call" | custom-call | tf_op jit(solution)/shard_map/store/pallas_call | solution.py:613
  (2 shorter events, 0.0 us)
Async XLA Ops:
  1.4 2.2 %copy-start = (f32[256]{0:T(256)}, f32[256]{0:T(256)S(1)}, u32[]{:S(2)}) copy-start(f32[256]{0:T(256)S(1)} %convert_element_type.6) | copy-start | bytes 3076

commit v3 on v2

--- a/solution.py
+++ b/solution.py
@@ -23,223 +23,207 @@
     (
         ("s", "q0", 0, "c", 0), ("s", "q1", 0, "c", 0), ("s", "q2", 0, "c", 0), ("s", "g0", 0, "c", 0),
         ("s", "g1", 0, "c", 0), ("s", "u0", 0, "c", 0), ("s", "u1", 0, "c", 0), ("s", "o", 0, "c", 0),
-        ("s", "d", 0, "c", 0), ("s", "o", "z", "z", 4), ("s", "d", "z", "z", 4), ("s", "q0", 0, "y", 0),
-        ("s", "q0", 0, "x", 1),
-    ),
-    (
-        ("s", "q2", 0, "y", 0), ("s", "q2", 0, "x", 1),
-    ),
-    (
-        ("s", "o", 0, "y", 2), ("s", "o", 0, "x", 1), ("w", "q0", "c", 0), ("w", "q1", "c", 0), ("w", "q2", "c", 0),
-    ),
-    (
-        ("w", "q0", "t"), ("w", "q0", 1), ("s", "q0", 1, "c", 1), ("w", "q0", 2), ("s", "q0", 2, "c", 2),
-        ("s", "q0", "t", "z", 2), ("s", "q1", 0, "y", 0), ("s", "q1", 0, "x", 1), ("w", "o", 2), ("s", "o", 2, "c", 2),
-        ("w", "q2", 1), ("s", "q2", 1, "c", 1), ("w", "q2", 2), ("s", "q2", 2, "c", 2), ("s", "q2", 2, "y", 2),
-        ("s", "q2", 2, "x", 3), ("w", "o", 1), ("s", "o", 1, "c", 1), ("w", "o", 4), ("s", "o", 4, "c", 4),
-        ("w", "q1", "t"), ("s", "q1", "t", "z", 2), ("w", "o", 6), ("s", "o", 6, "c", 6), ("s", "o", 4, "y", 6),
-        ("s", "o", 4, "x", 5), ("w", "q1", 1), ("s", "q1", 1, "c", 1), ("w", "q1", 2), ("s", "q1", 2, "c", 2),
-    ),
-    (
-        ("s", "q1", 1, "y", 1), ("s", "o", 2, "x", 3), ("w", "q0", "c", 1), ("w", "q1", "c", 1), ("w", "q2", "c", 1),
-    ),
-    (
-        ("w", "u1", "t"), ("w", "q2", 3), ("s", "q2", 3, "c", 3), ("s", "u1", "t", "z", 2), ("s", "u1", 0, "y", 0),
-        ("s", "o", 6, "x", 7), ("s", "q1", 2, "x", 3),
-    ),
-    (
-        ("w", "u1", 2), ("s", "u1", 2, "c", 2), ("w", "o", 5), ("s", "o", 5, "c", 5), ("w", "q0", "c", 2),
-        ("w", "q1", "c", 2), ("w", "q2", "c", 2),
-    ),
-    (
-        ("w", "o", 3), ("s", "o", 3, "c", 3), ("w", "g0", "t"), ("w", "o", 7), ("s", "o", 7, "c", 7),
-        ("s", "g0", "t", "z", 2), ("s", "o", 5, "y", 7), ("s", "u1", 0, "x", 1), ("w", "u0", 2), ("s", "u0", 2, "c", 2),
-        ("s", "u0", 0, "y", 0), ("w", "q1", 3), ("s", "q1", 3, "c", 3), ("w", "g1", "t"), ("s", "g1", "t", "z", 2),
-        ("s", "u0", 0, "x", 1), ("w", "g0", 2), ("s", "g0", 2, "c", 2), ("s", "u0", 2, "y", 2), ("w", "q0", 3),
-        ("s", "q0", 3, "c", 3),
-    ),
-    (
-        ("w", "u1", 1), ("s", "u1", 1, "c", 1), ("s", "g0", 0, "x", 1), ("w", "q0", "c", 3), ("w", "q1", "c", 3),
+        ("s", "d", 0, "c", 0), ("s", "o", "z", "z", 4), ("s", "d", "z", "z", 4), ("s", "q1", 0, "y", 0),
+        ("s", "q1", 0, "x", 1),
+    ),
+    (
+        ("s", "o", 0, "y", 2), ("s", "q2", 0, "y", 0), ("s", "o", 0, "x", 1), ("s", "q2", 0, "x", 1),
+    ),
+    (
+        ("w", "o", 4), ("s", "o", 4, "c", 4), ("w", "q0", "c", 0), ("w", "q1", "c", 0), ("w", "q2", "c", 0),
+    ),
+    (
+        ("w", "q1", "t"), ("w", "q1", 1), ("s", "q1", 1, "c", 1), ("s", "q1", "t", "z", 2), ("s", "o", 4, "y", 6),
+        ("s", "o", 4, "x", 5), ("w", "q1", 2), ("s", "q1", 2, "c", 2), ("w", "o", 1), ("s", "o", 1, "c", 1),
+        ("s", "q0", 0, "y", 0), ("s", "q0", 0, "x", 1), ("w", "q2", "t"), ("s", "q2", "t", "z", 2), ("w", "q2", 1),
+        ("s", "q2", 1, "c", 1), ("w", "q2", 2), ("s", "q2", 2, "c", 2), ("s", "g0", 0, "y", 0), ("s", "q1", 2, "x", 3),
+        ("w", "o", 5), ("s", "o", 5, "c", 5), ("w", "q0", "t"), ("s", "q0", "t", "z", 2), ("w", "o", 2),
+        ("s", "o", 2, "c", 2), ("w", "q0", 2), ("s", "q0", 2, "c", 2),
+    ),
+    (
+        ("w", "o", 6), ("s", "o", 6, "c", 6), ("w", "q0", 1), ("s", "q0", 1, "c", 1), ("s", "q0", 1, "y", 1),
+        ("s", "q2", 2, "x", 3),
+    ),
+    (
+        ("s", "q0", 2, "x", 3), ("w", "q0", "c", 1), ("w", "q1", "c", 1), ("w", "q2", "c", 1),
+    ),
+    (
+        ("w", "g0", 2), ("s", "g0", 2, "c", 2), ("w", "q1", 3), ("s", "q1", 3, "c", 3), ("w", "g0", "t"),
+        ("s", "g0", "t", "z", 2), ("s", "q1", 3, "y", 3), ("w", "q0", "c", 2), ("w", "q1", "c", 2), ("w", "q2", "c", 2),
+    ),
+    (
+        ("w", "q2", 3), ("s", "q2", 3, "c", 3), ("s", "o", 1, "y", 3), ("s", "g0", 0, "x", 1), ("w", "d", 4),
+        ("s", "d", 4, "c", 4), ("s", "o", 5, "y", 7), ("w", "u0", "t"), ("s", "u0", "t", "z", 2),
+        ("s", "u0", 0, "y", 0), ("s", "o", 6, "x", 7), ("w", "q0", 3), ("s", "q0", 3, "c", 3),
+    ),
+    (
+        ("w", "u0", 2), ("s", "u0", 2, "c", 2), ("s", "u0", 0, "x", 1), ("w", "q0", "c", 3), ("w", "q1", "c", 3),
         ("w", "q2", "c", 3),
     ),
     (
-        ("w", "g1", 2), ("s", "g1", 2, "c", 2), ("s", "g0", 0, "y", 0), ("w", "o", "c", 0), ("w", "o", "c", 1),
-        ("w", "o", "c", 2), ("w", "o", "c", 3), ("w", "o", "c", 4), ("w", "o", "c", 5), ("w", "o", "c", 6),
-        ("w", "o", "c", 7),
-    ),
-    (
-        ("w", "d", 2), ("s", "d", 2, "c", 2), ("w", "u0", 1), ("s", "u0", 1, "c", 1), ("s", "g1", 0, "x", 1),
-        ("w", "d", 4), ("s", "d", 4, "c", 4), ("s", "u0", 1, "y", 1), ("w", "d", 6), ("s", "d", 6, "c", 6),
-        ("w", "g0", 1), ("s", "g0", 1, "c", 1), ("s", "g1", 2, "x", 3), ("s", "g1", 0, "y", 0), ("w", "u1", 3),
-        ("s", "u1", 3, "c", 3), ("w", "g1", 1), ("s", "g1", 1, "c", 1), ("s", "d", 0, "x", 1), ("s", "g1", 1, "y", 1),
-        ("w", "g1", 3), ("s", "g1", 3, "c", 3), ("s", "d", 4, "x", 5), ("w", "g0", 3), ("s", "g0", 3, "c", 3),
-    ),
-    (
-        ("s", "d", 0, "y", 2),
-    ),
-    (
-        ("w", "d", 1), ("s", "d", 1, "c", 1), ("w", "g0", "c", 0), ("w", "g1", "c", 0), ("w", "u0", "c", 0),
+        ("w", "u1", "t"), ("s", "u1", "t", "z", 2), ("s", "u1", 0, "y", 0), ("w", "g0", 1), ("s", "g0", 1, "c", 1),
+        ("s", "u1", 0, "x", 1), ("w", "o", 7), ("s", "o", 7, "c", 7), ("w", "u1", 2), ("s", "u1", 2, "c", 2),
+        ("w", "g1", "t"), ("s", "g1", "t", "z", 2), ("s", "g1", 0, "y", 0), ("w", "o", 3), ("s", "o", 3, "c", 3),
+        ("s", "g1", 0, "x", 1), ("w", "u0", 1), ("s", "u0", 1, "c", 1), ("w", "g1", 2), ("s", "g1", 2, "c", 2),
+        ("w", "o", "c", 0), ("w", "o", "c", 1), ("w", "o", "c", 2), ("w", "o", "c", 3), ("w", "o", "c", 4),
+        ("w", "o", "c", 5), ("w", "o", "c", 6), ("w", "o", "c", 7),
+    ),
+    (
+        ("s", "d", 0, "y", 2), ("w", "d", 2), ("s", "d", 2, "c", 2), ("s", "d", 0, "x", 1), ("w", "u1", 1),
+        ("s", "u1", 1, "c", 1), ("s", "d", 4, "y", 6), ("w", "d", 6), ("s", "d", 6, "c", 6), ("s", "d", 4, "x", 5),
+        ("w", "g1", 1), ("s", "g1", 1, "c", 1), ("s", "u0", 1, "y", 1), ("w", "g0", 3), ("s", "g0", 3, "c", 3),
+        ("s", "g1", 2, "x", 3), ("w", "d", 1), ("s", "d", 1, "c", 1),
+    ),
+    (
+        ("s", "d", 1, "y", 3),
+    ),
+    (
+        ("w", "u0", 3), ("s", "u0", 3, "c", 3), ("w", "g0", "c", 0), ("w", "g1", "c", 0), ("w", "u0", "c", 0),
         ("w", "u1", "c", 0),
     ),
     (
-        ("s", "d", 2, "x", 3),
-    ),
-    (
-        ("w", "u0", 3), ("s", "u0", 3, "c", 3), ("w", "g0", "c", 1), ("w", "g1", "c", 1), ("w", "u0", "c", 1),
-        ("w", "u1", "c", 1),
-    ),
-    (),
-    (
-        ("s", "d", 4, "y", 6), ("w", "g0", "c", 2), ("w", "g1", "c", 2), ("w", "u0", "c", 2), ("w", "u1", "c", 2),
-    ),
-    (),
-    (
-        ("w", "d", 5), ("s", "d", 5, "c", 5), ("w", "g0", "c", 3), ("w", "g1", "c", 3), ("w", "u0", "c", 3),
-        ("w", "u1", "c", 3),
+        ("w", "d", 5), ("s", "d", 5, "c", 5), ("s", "d", 6, "x", 7),
+    ),
+    (
+        ("w", "g0", "c", 1), ("w", "g1", "c", 1), ("w", "u0", "c", 1), ("w", "u1", "c", 1),
+    ),
+    (),
+    (
+        ("w", "g0", "c", 2), ("w", "g1", "c", 2), ("w", "u0", "c", 2), ("w", "u1", "c", 2),
+    ),
+    (
+        ("w", "u1", 3), ("s", "u1", 3, "c", 3), ("w", "g1", 3), ("s", "g1", 3, "c", 3),
+    ),
+    (
+        ("w", "g0", "c", 3), ("w", "g1", "c", 3), ("w", "u0", "c", 3), ("w", "u1", "c", 3),
     ),
     (),
     (
         ("w", "d", "c", 0), ("w", "d", "c", 4),
     ),
-    (),
-    (
-        ("s", "d", 5, "y", 7), ("w", "d", "c", 1), ("w", "d", "c", 5),
+    (
+        ("w", "d", 3), ("s", "d", 3, "c", 3),
+    ),
+    (
+        ("w", "d", 7), ("s", "d", 7, "c", 7), ("w", "d", "c", 1), ("w", "d", "c", 5),
     ),
     (),
     (
         ("w", "d", "c", 2), ("w", "d", "c", 6),
     ),
-    (
-        ("w", "d", 3), ("s", "d", 3, "c", 3), ("w", "d", 7), ("s", "d", 7, "c", 7),
-    ),
+    (),
     (
         ("w", "d", "c", 3), ("w", "d", "c", 7),
     ),
-    (),
-    (),
-    (),
-    (),
-    (),
-    (),
-    (),
-    (),
     (),
 )
 HOME_BLOCKS = {
-    "attend": ((0, 0), (0, 1), (1, 0), (1, 1), (2, 0), (2, 1), (3, 0), (3, 1)),
+    "attend": ((0, 0), (0, 1), (2, 0), (1, 0), (1, 1), (2, 1), (3, 0), (3, 1)),
     "gated": ((0, 0), (0, 1), (1, 0), (1, 1), (2, 0), (2, 1), (3, 0), (3, 1)),
     "down": ((0, 0), (0, 1), (1, 0), (1, 1), (2, 0), (2, 1), (3, 0), (3, 1)),
 }
 AWAY_STEPS = (
     (
-        ("s", "o", 0, "c", 0), ("s", "d", 0, "c", 0), ("s", "q0", "own", "z", 2), ("s", "q0", "own", "y", "t"),
-        ("s", "o", 0, "x", 1), ("s", "d", 0, "x", 1),
-    ),
-    (
-        ("s", "q2", "own", "z", 2), ("s", "o", 0, "y", 2), ("s", "q1", "own", "y", "t"), ("w", "o", 1),
-        ("s", "o", 1, "c", 1), ("w", "o", 4), ("s", "o", 4, "c", 4), ("s", "o", 4, "x", 5), ("s", "o", "z", "z", 4),
-        ("w", "q0", 0), ("s", "q0", 0, "c", 0), ("s", "q0", 0, "x", 1), ("s", "q1", "own", "z", 2),
-        ("s", "o", 4, "y", 6), ("s", "u1", "own", "y", "t"), ("w", "d", 1), ("s", "d", 1, "c", 1), ("w", "d", 4),
-        ("s", "d", 4, "c", 4), ("w", "q2", 0), ("s", "q2", 0, "c", 0), ("s", "q2", 0, "x", 1),
-        ("s", "u1", "own", "z", 2), ("w", "o", 5), ("s", "o", 5, "c", 5), ("w", "o", 2), ("s", "o", 2, "c", 2),
-        ("s", "g0", "own", "y", "t"), ("s", "o", 2, "x", 3), ("w", "q0", 2), ("s", "q0", 2, "c", 2), ("w", "q0", 1),
-        ("s", "q0", 1, "c", 1), ("w", "q1", 0), ("s", "q1", 0, "c", 0),
-    ),
-    (
-        ("s", "u0", "own", "z", 2), ("s", "q0", 2, "x", 3), ("w", "q0", "c", 0), ("w", "q1", "c", 0),
+        ("s", "o", 0, "c", 0), ("s", "d", 0, "c", 0), ("s", "o", "z", "z", 4), ("s", "q1", "own", "z", 2),
+        ("s", "q1", "own", "y", "t"), ("s", "o", 0, "x", 1), ("s", "d", 0, "x", 1),
+    ),
+    (
+        ("s", "q2", "own", "z", 2), ("s", "q2", "own", "y", "t"), ("w", "o", 1), ("s", "o", 1, "c", 1), ("w", "o", 4),
+        ("s", "o", 4, "c", 4), ("s", "o", 4, "x", 5), ("s", "q0", "own", "y", "t"), ("w", "q1", 0),
+        ("s", "q1", 0, "c", 0), ("s", "q1", 0, "x", 1), ("s", "q0", "own", "z", 2), ("w", "o", 2),
+        ("s", "o", 2, "c", 2), ("s", "o", 0, "y", 2), ("w", "d", 1), ("s", "d", 1, "c", 1), ("w", "d", 4),
+        ("s", "d", 4, "c", 4), ("s", "d", 4, "x", 5), ("s", "g0", "own", "z", 2), ("s", "o", 4, "y", 6), ("w", "o", 5),
+        ("s", "o", 5, "c", 5), ("w", "q2", 0), ("s", "q2", 0, "c", 0), ("s", "g0", "own", "y", "t"), ("w", "o", 6),
+        ("s", "o", 6, "c", 6), ("w", "q1", 2), ("s", "q1", 2, "c", 2), ("s", "q2", 0, "x", 1), ("w", "q1", 1),
+        ("s", "q1", 1, "c", 1), ("s", "d", "z", "z", 4), ("s", "u0", "own", "y", "t"), ("w", "q0", 0),
+        ("s", "q0", 0, "c", 0),
+    ),
+    (
+        ("w", "q2", 2), ("s", "q2", 2, "c", 2), ("s", "q2", 2, "x", 3), ("w", "q0", "c", 0), ("w", "q1", "c", 0),
         ("w", "q2", "c", 0),
     ),
     (
-        ("w", "q1", 2), ("s", "q1", 2, "c", 2), ("w", "q2", 1), ("s", "q2", 1, "c", 1), ("w", "q2", 2),
-        ("s", "q2", 2, "c", 2), ("s", "g1", "own", "y", "t"), ("s", "q2", 2, "x", 3),
-    ),
-    (
-        ("w", "o", 3), ("s", "o", 3, "c", 3), ("w", "o", 6), ("s", "o", 6, "c", 6), ("s", "g0", "own", "z", 2),
-        ("s", "q1", 2, "x", 3), ("w", "q0", "c", 2), ("w", "q1", "c", 2), ("w", "q2", "c", 2),
-    ),
-    (
-        ("w", "q0", 3), ("s", "q0", 3, "c", 3), ("w", "q1", 1), ("s", "q1", 1, "c", 1), ("s", "q0", 3, "y", 3),
-    ),
-    (
-        ("w", "q2", 3), ("s", "q2", 3, "c", 3), ("w", "u1", 2), ("s", "u1", 2, "c", 2), ("s", "g1", "own", "z", 2),
-        ("s", "d", 0, "y", 2), ("s", "u1", 2, "x", 3), ("w", "q0", "c", 1), ("w", "q1", "c", 1), ("w", "q2", "c", 1),
-    ),
-    (
-        ("w", "u1", 0), ("s", "u1", 0, "c", 0), ("s", "d", "z", "z", 4), ("w", "o", 7), ("s", "o", 7, "c", 7),
-        ("w", "q1", 3), ("s", "q1", 3, "c", 3),
-    ),
-    (
-        ("w", "g0", 2), ("s", "g0", 2, "c", 2), ("s", "d", 4, "y", 6), ("s", "u1", 0, "x", 1), ("w", "q0", "c", 3),
-        ("w", "q1", "c", 3), ("w", "q2", "c", 3),
-    ),
-    (
-        ("w", "u0", 0), ("s", "u0", 0, "c", 0), ("w", "o", "c", 0), ("w", "o", "c", 1), ("w", "o", "c", 2),
-        ("w", "o", "c", 3), ("w", "o", "c", 4), ("w", "o", "c", 5), ("w", "o", "c", 6), ("w", "o", "c", 7),
-    ),
-    (
-        ("w", "u1", 3), ("s", "u1", 3, "c", 3), ("s", "u1", 3, "y", 3), ("s", "g0", 2, "x", 3), ("w", "g1", 2),
-        ("s", "g1", 2, "c", 2), ("w", "u0", 2), ("s", "u0", 2, "c", 2), ("w", "u1", 1), ("s", "u1", 1, "c", 1),
-        ("s", "u0", 2, "x", 3), ("w", "g0", 0), ("s", "g0", 0, "c", 0), ("w", "g0", 3), ("s", "g0", 3, "c", 3),
-        ("s", "g0", 3, "y", 3), ("s", "g0", 0, "x", 1), ("w", "u0", 1), ("s", "u0", 1, "c", 1), ("w", "u0", 3),
-        ("s", "u0", 3, "c", 3), ("s", "u0", 3, "y", 3), ("s", "g1", 2, "x", 3),
-    ),
-    (
-        ("w", "g1", 0), ("s", "g1", 0, "c", 0), ("w", "g0", 1), ("s", "g0", 1, "c", 1), ("s", "d", 4, "x", 5),
-    ),
-    (),
+        ("w", "d", 5), ("s", "d", 5, "c", 5), ("w", "q0", 2), ("s", "q0", 2, "c", 2), ("s", "u0", "own", "z", 2),
+        ("s", "u1", "own", "y", "t"), ("s", "q0", 2, "x", 3),
+    ),
+    (
+        ("w", "g0", 0), ("s", "g0", 0, "c", 0), ("w", "q2", 1), ("s", "q2", 1, "c", 1), ("w", "q0", "c", 2),
+        ("w", "q1", "c", 2), ("w", "q2", "c", 2),
+    ),
+    (
+        ("w", "q0", 1), ("s", "q0", 1, "c", 1), ("s", "u1", "own", "z", 2), ("s", "g1", "own", "y", "t"),
+        ("s", "g0", 0, "x", 1),
+    ),
+    (
+        ("w", "q2", 3), ("s", "q2", 3, "c", 3), ("w", "q1", 3), ("s", "q1", 3, "c", 3), ("w", "q0", "c", 1),
+        ("w", "q1", "c", 1), ("w", "q2", "c", 1),
+    ),
+    (
+        ("w", "g0", 2), ("s", "g0", 2, "c", 2), ("w", "q0", 3), ("s", "q0", 3, "c", 3), ("w", "o", 3),
+        ("s", "o", 3, "c", 3), ("s", "g1", "own", "z", 2), ("s", "o", 1, "y", 3), ("s", "g0", 2, "x", 3),
+    ),
+    (
+        ("w", "o", 7), ("s", "o", 7, "c", 7), ("s", "d", 0, "y", 2), ("w", "q0", "c", 3), ("w", "q1", "c", 3),
+        ("w", "q2", "c", 3),
+    ),
+    (
+        ("w", "u0", 2), ("s", "u0", 2, "c", 2), ("w", "g0", 1), ("s", "g0", 1, "c", 1), ("s", "u0", 2, "x", 3),
+        ("w", "o", "c", 0), ("w", "o", "c", 1), ("w", "o", "c", 2), ("w", "o", "c", 3), ("w", "o", "c", 4),
+        ("w", "o", "c", 5), ("w", "o", "c", 6), ("w", "o", "c", 7),
+    ),
+    (
+        ("w", "u0", 0), ("s", "u0", 0, "c", 0), ("s", "d", 4, "y", 6), ("w", "u1", 2), ("s", "u1", 2, "c", 2),
+        ("s", "u1", 2, "x", 3), ("w", "g0", 3), ("s", "g0", 3, "c", 3), ("w", "u1", 0), ("s", "u1", 0, "c", 0),
+        ("s", "g0", 3, "y", 3), ("s", "u1", 0, "x", 1), ("w", "g1", 2), ("s", "g1", 2, "c", 2), ("w", "u0", 3),
+        ("s", "u0", 3, "c", 3), ("w", "g1", 0), ("s", "g1", 0, "c", 0), ("s", "u0", 3, "y", 3), ("s", "g1", 0, "x", 1),
+        ("w", "u1", 3), ("s", "u1", 3, "c", 3), ("w", "d", 2), ("s", "d", 2, "c", 2), ("s", "u1", 3, "y", 3),
+        ("s", "g1", 2, "x", 3), ("w", "u1", 1), ("s", "u1", 1, "c", 1), ("w", "d", 6), ("s", "d", 6, "c", 6),
+        ("s", "d", 1, "y", 3),
+    ),
+    (
+        ("w", "g1", 1), ("s", "g1", 1, "c", 1), ("s", "d", 6, "x", 7),
+    ),
+    (
+        ("w", "u0", 1), ("s", "u0", 1, "c", 1), ("w", "g0", "c", 0), ("w", "g1", "c", 0), ("w", "u0", "c", 0),
+        ("w", "u1", "c", 0),
+    ),
+    (),
+    (),
+    (
+        ("w", "g1", 3), ("s", "g1", 3, "c", 3), ("w", "g0", "c", 1), ("w", "g1", "c", 1), ("w", "u0", "c", 1),
+        ("w", "u1", "c", 1),
+    ),
     (
         ("w", "g0", "c", 2), ("w", "g1", "c", 2), ("w", "u0", "c", 2), ("w", "u1", "c", 2),
     ),
-    (
-        ("w", "g0", "c", 0), ("w", "g1", "c", 0), ("w", "u0", "c", 0), ("w", "u1", "c", 0),
-    ),
-    (
-        ("w", "g1", 1), ("s", "g1", 1, "c", 1),
-    ),
-    (
-        ("w", "g1", 3), ("s", "g1", 3, "c", 3),
-    ),
-    (
-        ("w", "g0", "c", 1), ("w", "g1", "c", 1), ("w", "u0", "c", 1), ("w", "u1", "c", 1),
-    ),
-    (
-        ("w", "g0", "c", 3), ("w", "g1", "c", 3), ("w", "u0", "c", 3), ("w", "u1", "c", 3),
-    ),
-    (),
-    (
-        ("w", "d", 2), ("s", "d", 2, "c", 2), ("s", "d", 2, "x", 3), ("w", "d", "c", 0), ("w", "d", "c", 4),
-    ),
-    (
-        ("w", "d", 5), ("s", "d", 5, "c", 5), ("s", "d", 5, "y", 7),
+    (),
+    (
+        ("w", "d", 3), ("s", "d", 3, "c", 3), ("w", "g0", "c", 3), ("w", "g1", "c", 3), ("w", "u0", "c", 3),
+        ("w", "u1", "c", 3),
+    ),
+    (),
+    (
+        ("w", "d", "c", 0), ("w", "d", "c", 4),
+    ),
+    (
+        ("w", "d", 7), ("s", "d", 7, "c", 7),
     ),
     (
         ("w", "d", "c", 1), ("w", "d", "c", 5),
     ),
-    (
-        ("w", "d", 6), ("s", "d", 6, "c", 6),
-    ),
+    (),
     (
         ("w", "d", "c", 2), ("w", "d", "c", 6),
     ),
-    (
-        ("w", "d", 3), ("s", "d", 3, "c", 3), ("w", "d", 7), ("s", "d", 7, "c", 7),
-    ),
+    (),
     (
         ("w", "d", "c", 3), ("w", "d", "c", 7),
     ),
-    (),
-    (),
-    (),
-    (),
-    (),
-    (),
-    (),
-    (),
     (),
 )
 AWAY_BLOCKS = {
     "attend": ((0, 0), (0, 1), (2, 0), (2, 1), (1, 0), (1, 1), (3, 0), (3, 1)),
-    "gated": ((0, 0), (2, 0), (2, 1), (0, 1), (1, 0), (3, 0), (1, 1), (3, 1)),
+    "gated": ((0, 0), (0, 1), (1, 0), (2, 0), (1, 1), (2, 1), (3, 0), (3, 1)),
     "down": ((0, 0), (0, 1), (1, 0), (1, 1), (2, 0), (2, 1), (3, 0), (3, 1)),
 }
 
@@ -347,9 +331,9 @@
 
 
 def layer_kernel(wq, wk, wv, wo, wg, wu, wd, small, x_ref, cos_ref, sin_ref, len_ref, k_hbm, v_hbm,
-                 wqkv, wgu, wout, wdn, k_lo, k_hi, v_lo, v_hi, smalls, hid,
-                 h_ref, sc_ref, o_ref, part, part_in, x1_ref, h2_ref, a_ref, down, down_in, t_q, t_gu,
-                 k_sem, v_sem, s_send, s_recv, p_send, p_recv, d_send, d_recv, row_s, row_r, row_c, col_s, col_r, col_c):
+                 wqkv, wgu, wout, wdn, k_lo, k_hi, v_lo, v_hi, smalls, x1_ref, down,
+                 h_ref, sc_ref, o_ref, a_ref, t_q, t_gu,
+                 k_sem, v_sem, s_send, s_recv, p_send, p_recv, row_s, row_r, row_c, col_s, col_r, col_c):
     place = Place()
     me = place.dp * 2 + place.z
     row_sem, col_sem = (row_s, row_r, row_c), (col_s, col_r, col_c)
@@ -488,11 +472,13 @@
         go()
 
     o = o_ref[...].T
+    part, part_in, h2_ref = down, x1_ref, h_ref
     part[...] = dot(o, wout[...].reshape(1024, 512), ROW_BYTES).astype(BF16)
     swap = remote(part, part_in, p_send, p_recv, place.device["z"])
     swap.start()
     go()
     swap.wait_recv()
+    swap.wait_send()
     total = (part[...].astype(F32) + part_in[...].astype(F32)).astype(BF16)
     x1 = (x_ref[...].astype(F32) + total.astype(F32)).astype(BF16)
     x1_ref[...] = x1
@@ -506,25 +492,11 @@
         a_ref[block] = (g / (1.0 + jnp.exp(-g)) * u).astype(BF16)
         go()
 
-    def pair_of(k, core):
-        return place.col_block(k, core) // 2
-
-    def down_copy(i, swap=False):
-        pair = by_role("down", i, pair_of, swap)
-        rows = pl.ds(pl.multiple_of(pair * 128, 128), 128)
-        return rows, pair, remote(down.at[rows], down_in.at[rows], d_send.at[pair], d_recv.at[pair], place.device["z"])
-
     for i in range(8):
-        rows, pair, copy = down_copy(i)
+        pair = by_role("down", i, lambda k, core: place.col_block(k, core) // 2)
         w = wdn[pl.ds(pair * 2, 2)].reshape(128, 1408)
-        down[rows] = dot(w, a_ref[...].reshape(1408, 256), NAT).astype(BF16)
-        copy.start()
-        go()
-    for i in range(8):
-        rows, _, copy = down_copy(i, True)
-        copy.wait_recv()
-        both = (down[rows].astype(F32) + down_in[rows].astype(F32)).T.astype(BF16).astype(F32)
-        hid[:, rows] = (x1_ref[:, rows].astype(F32) + both).astype(BF16)
+        cols = pl.ds(pl.multiple_of(pair * 128, 128), 128)
+        down[:, cols] = dot(w, a_ref[...].reshape(1408, 256), NAT).T.astype(BF16)
         go()
 
     for far, steps, _ in roles:
@@ -536,18 +508,15 @@
 
     for i in range(1, 16):
         small_copy(i).wait_send()
-    swap.wait_send()
-    for i in range(8):
-        down_copy(i)[2].wait_send()
-
-
-def store_kernel(wqkv, wgu, wout, wdn, k_lo, k_hi, v_lo, v_hi, smalls, hid,
-                 wq, wk, wv, wo, wg, wu, wd, k_out, v_out, hid_out, bq, bk, bv, ga, gm, sem):
+
+
+def store_kernel(wqkv, wgu, wout, wdn, k_lo, k_hi, v_lo, v_hi, smalls,
+                 wq, wk, wv, wo, wg, wu, wd, k_out, v_out, bq, bk, bv, ga, gm, sem):
     lo, hi = pl.ds(0, 32), pl.ds(32, 32)
     pairs = [(k_lo, k_out.at[lo]), (k_hi, k_out.at[hi]), (v_lo, v_out.at[lo]), (v_hi, v_out.at[hi]),
              (wdn, wd), (wgu.at[:, pl.ds(0, 176)], wg), (wgu.at[:, pl.ds(176, 176)], wu),
              (wqkv.at[:, pl.ds(0, 64)], wq), (wqkv.at[:, pl.ds(64, 64)], wk), (wqkv.at[:, pl.ds(128, 64)], wv),
-             (wout, wo), (hid, hid_out)]
+             (wout, wo)]
     copies = [pltpu.make_async_copy(src, dst, sem.at[i]) for i, (src, dst) in enumerate(pairs)]
     for copy in copies:
         copy.start()
@@ -560,6 +529,11 @@
         ref[...] = (whole[:, 0, 3 + i] + whole[:, 1, 3 + i]).astype(BF16)
     for copy in copies:
         copy.wait()
+
+
+def finish_kernel(x1, mine, peer, hid):
+    total = (mine[...].astype(F32) + peer[...].astype(F32)).astype(BF16)
+    hid[...] = (x1[...].astype(F32) + total.astype(F32)).astype(BF16)
 
 
 def local_step(w_query, b_query, w_key, b_key, w_value, b_value, w_out, w_gate, w_up, w_down, gain_attn, gain_mlp,
@@ -581,47 +555,51 @@
     anywhere = pl.BlockSpec(memory_space=pl.ANY)
     dma = pltpu.SemaphoreType.DMA
     shapes = [(8, 192, 1024), (8, 352, 1024), (16, 64, 512), (16, 64, 1408), *[(32, 8, 64, 256)] * 4,
-              (16, 8, 128), (256, 1024)]
+              (16, 8, 128), (256, 1024), (256, 1024)]
     held = pl.pallas_call(
         layer_kernel,
         out_shape=[pltpu.VMEM(s, BF16) for s in shapes],
         in_specs=[vmem] * 12 + [hbm] * 2,
-        out_specs=[vmem] * 10,
+        out_specs=[vmem] * 11,
         scratch_shapes=[
             pltpu.VMEM((256, 1024), BF16),
             pltpu.VMEM((64, 256), F32),
             pltpu.VMEM((512, 256), BF16),
-            pltpu.VMEM((256, 1024), BF16),
-            pltpu.VMEM((256, 1024), BF16),
-            pltpu.VMEM((256, 1024), BF16),
-            pltpu.VMEM((256, 1024), BF16),
             pltpu.VMEM((8, 176, 256), BF16),
-            pltpu.VMEM((1024, 256), BF16),
-            pltpu.VMEM((1024, 256), BF16),
             pltpu.VMEM((3, 64, 1024), BF16),
             pltpu.VMEM((4, 88, 1024), BF16),
-            dma((16,)), dma((16,)), dma((16,)), dma((16,)), dma, dma, dma((8,)), dma((8,)),
+            dma((16,)), dma((16,)), dma((16,)), dma((16,)), dma, dma,
             dma((7, 4, 5)), dma((7, 5)), dma((7, 4)), dma((2, 4, 8)), dma((2, 8)), dma((2, 8)),
         ],
-        compiler_params=pltpu.CompilerParams(collective_id=0, has_side_effects=True, vmem_limit_bytes=10 * 2**20),
+        compiler_params=pltpu.CompilerParams(collective_id=0, has_side_effects=True, vmem_limit_bytes=5 * 2**20),
         name="layer",
     )(w_query, w_key, w_value, w_out, w_gate, w_up, w_down, small, hidden, cos, sin, lens, k_view, v_view)
 
     def shape(*dims):
         return jax.ShapeDtypeStruct(dims, BF16)
 
+    peer = lax.ppermute(held[10], "tp", [(0, 1), (1, 0)])
     outs = pl.pallas_call(
         store_kernel,
         out_shape=[shape(8, 64, 1024)] * 3 + [shape(16, 64, 512), shape(8, 176, 1024), shape(8, 176, 1024),
-                   shape(16, 64, 1408), shape(*k_view.shape), shape(*v_view.shape), shape(256, 1024),
+                   shape(16, 64, 1408), shape(*k_view.shape), shape(*v_view.shape),
                    shape(4, 128), shape(4, 128), shape(4, 128), shape(8, 128), shape(8, 128)],
-        in_specs=[anywhere] * 8 + [vmem, anywhere],
-        out_specs=[hbm] * 10 + [vmem] * 5,
-        scratch_shapes=[dma((12,))],
-        compiler_params=pltpu.CompilerParams(vmem_limit_bytes=2 * 2**20),
+        in_specs=[anywhere] * 8 + [vmem],
+        out_specs=[hbm] * 9 + [vmem] * 5,
+        scratch_shapes=[dma((11,))],
+        compiler_params=pltpu.CompilerParams(vmem_limit_bytes=2**20),
+        cost_estimate=pl.CostEstimate(flops=2 * 10**10, bytes_accessed=5 * 10**7, transcendentals=0),
         name="store",
-    )(*held)
-    wq, wk, wv, wo, wg, wu, wd, k_out, v_out, hid, bq, bk, bv, ga, gm = outs
+    )(*held[:9])
+    hid = pl.pallas_call(
+        finish_kernel,
+        out_shape=shape(256, 1024),
+        in_specs=[vmem] * 3,
+        out_specs=vmem,
+        compiler_params=pltpu.CompilerParams(vmem_limit_bytes=4 * 2**20),
+        name="finish",
+    )(held[9], held[10], peer)
+    wq, wk, wv, wo, wg, wu, wd, k_out, v_out, bq, bk, bv, ga, gm = outs
     flat = lambda a, n: a.reshape(-1, n)
     return (flat(wq, 1024), bq.reshape(512), flat(wk, 1024), bk.reshape(512), flat(wv, 1024), bv.reshape(512),
             flat(wo, 512), flat(wg, 1024), flat(wu, 1024), flat(wd, 1408), ga.reshape(1024), gm.reshape(1024),

time: 95.7 us -> 95.3 us (level)
  Pallas kernels: 91.8 us -> 82.3 us
  local copies, waits for them, and re-layouts: 0.75 us -> 8.35 us
  starting transfers between devices: 0 us -> 2.57 us
  other arithmetic: 2.18 us -> 0.98 us
    pallas_call x1, Pallas kernels: 76.1 us -> 65.7 us  [local_step(): pl.pallas_call(layer_kernel, out_shape=[pltpu.VMEM(s, BF16) for s in shap...]
    unnamed x2 -> x16, local copies, waits for them, and re-layouts: 0.01 us -> 7.6 us
    ppermute x0 -> x1, starting transfers between devices: none -> 2.57 us  [local_step(): peer = lax.ppermute(held[10], 'tp', [(0, 1), (1, 0)])]
    pallas_call x0 -> x1, Pallas kernels: none -> 1.04 us  [local_step(): pl.pallas_call(finish_kernel, out_shape=shape(256, 1024), in_specs=[vmem]...]
  transfers between devices with their start and end apart: 0 -> 1, of which waited for: 0 -> 0; matrix products, arithmetic and copies ran while one was open for 0% -> 0% of each run, Pallas kernels for 0% -> 16%
where the time goes in v3:
time: 95.3 us; the launch traced here: 94.9 us
  Pallas kernels  82.3 us (86%)
  local copies, waits for them, and re-layouts  8.35 us (9%)
  starting transfers between devices  2.57 us (3%)
  other arithmetic  0.98 us (1%)
    pallas_call x1, Pallas kernels, local_step(): pl.pallas_call(layer_kernel, out_shape=[pltpu.VMEM(s, BF16) for s in shap...  65.7 us
    pallas_call x1, Pallas kernels, local_step(): pl.pallas_call(store_kernel, out_shape=[shape(8, 64, 1024)] * 3 + [shape(...  15.5 us
    unnamed x16, local copies, waits for them, and re-layouts  7.6 us
    ppermute x1, starting transfers between devices, local_step(): peer = lax.ppermute(held[10], 'tp', [(0, 1), (1, 0)])  2.57 us
  transfers between devices with their start and end apart: 1, of which 0 were waited for; matrix products, arithmetic and copies ran while one was open for 0% of the time, Pallas kernels for 16%

profile of v3, /device:TPU:0, one launch (start us, length us, event | category | flops | bytes accessed | tf_op | source)
XLA Modules:
  0.0 94.9 jit_solution(18302759588361535206)
XLA Ops:
  0.7 0.7 convert_element_type.6
  1.4 0.7 stack.23
  2.1 0.1 fusion.2.small
  2.2 0.2 multiply_sine_fusion
  2.4 0.0 copy-start
  2.4 1.0 %copy-done = bf16[256,1024]{1,0:T(8,128)(2,1)S(1)} copy-done((bf16[256,1024]{1,0:T(8,128)(2,1)S(1)}, bf16[256,1024]{1,0:T(8,128)(2,1)}, u32[]{:S(2)}) %copy-start) | copy-done | bytes 524312
  3.4 0.0 copy-start.1
  3.4 1.0 %copy-done.1 = bf16[176,1024]{1,0:T(8,128)(2,1)S(1)} copy-done((bf16[176,1024]{1,0:T(8,128)(2,1)S(1)}, bf16[176,1024]{1,0:T(8,128)(2,1)}, u32[]{:S(2)}) %copy-start.1) | copy-done | bytes 360472
  4.4 0.0 copy-start.2
  4.4 1.0 %copy-done.2 = bf16[176,1024]{1,0:T(8,128)(2,1)S(1)} copy-done((bf16[176,1024]{1,0:T(8,128)(2,1)S(1)}, bf16[176,1024]{1,0:T(8,128)(2,1)}, u32[]{:S(2)}) %copy-start.2) | copy-done | bytes 360472
  5.4 0.0 copy-start.3
  5.4 1.0 %copy-done.3 = bf16[64,2816]{1,0:T(8,128)(2,1)S(1)} copy-done((bf16[64,2816]{1,0:T(8,128)(2,1)S(1)}, bf16[64,2816]{1,0:T(8,128)(2,1)}, u32[]{:S(2)}) %copy-start.3) | copy-done | bytes 360472
  6.4 0.0 copy-start.4
  6.4 0.9 copy-done.4
  7.3 0.0 copy-start.5
  7.3 0.9 copy-done.5
  8.2 0.0 copy-start.6
  8.2 0.9 copy-done.6
  9.1 0.0 copy-start.7
  9.1 0.9 copy-done.7
  10.0 65.7 %layer.1 = (bf16[8,192,1024]{2,1,0:T(8,128)(2,1)S(1)}, bf16[8,352,1024]{2,1,0:T(8,128)(2,1)S(1)}, bf16[16,64,512]{2,1,0:T(8,128)(2,1)S(1)}, bf16[16,64,1408]{2,1...) custom-call(bf16[64,1024]{1,0:T(8,128)(2,1)S(1)} %copy-done.4, ...), custom_call_target="tpu_custom_call" | custom-call | tf_op jit(solution)/shard_map/layer/pallas_call | solution.py:559
  75.7 2.6 %collective-permute-start = (bf16[256,1024]{1,0:T(8,128)(2,1)S(1)}, bf16[256,1024]{1,0:T(8,128)(2,1)S(1)}, u32[]{:S(2)}, u32[]{:S(2)}) collective-permute-start(bf16[256,1024]{1,0:T(8,128)(2,1)S(1)} %get-tuple-element.62.mine), channel_id=1, source_target_pairs={{0,8},{8,0},{1,9},{9,1},{2,10},{10,2},{3,11},{11,3},{4,12},{12,4},... | collective-permute-start | bytes 1572872 | tf_op jit(solution)/shard_map/ppermute | solution.py:581
  78.3 15.5 %store.1 = (bf16[8,64,1024]{2,1,0:T(8,128)(2,1)}, bf16[8,64,1024]{2,1,0:T(8,128)(2,1)}, bf16[8,64,1024]{2,1,0:T(8,128)(2,1)}, bf16[16,64,512]{2,1,0:T(8,128)(2,1...) custom-call(bf16[8,192,1024]{2,1,0:T(8,128)(2,1)S(1)} %get-tuple-ele, ...), custom_call_target="tpu_custom_call" | custom-call | flops 20000000000 | bytes 50000000 | tf_op jit(solution)/shard_map/store/pallas_call | solution.py:582
  93.8 0.0 collective-permute-done.peer
  93.8 1.0 %finish.1 = bf16[256,1024]{1,0:T(8,128)(2,1)} custom-call(bf16[256,1024]{1,0:T(8,128)(2,1)S(1)} %get-tuple-element.61.x1, bf16[256,1024]{1,0:T(8,128)(2,1)S(1)} %get-tuple-element.62.mine, bf16[256,1024]{1,0:T(8,128)(2,1)S(1)} %collective-permute-done.peer), custom_call_target="tpu_custom_call" | custom-call | tf_op jit(solution)/shard_map/finish/pallas_call | solution.py:594
  (2 shorter events, 0.0 us)
Async XLA Ops:
  2.4 1.0 %copy-start = (bf16[256,1024]{1,0:T(8,128)(2,1)S(1)}, bf16[256,1024]{1,0:T(8,128)(2,1)}, u32[]{:S(2)}) copy-start(bf16[256,1024]{1,0:T(8,128)(2,1)} %x_ref.1) | copy-start | bytes 1572868
  3.4 1.0 %copy-start.1 = (bf16[176,1024]{1,0:T(8,128)(2,1)S(1)}, bf16[176,1024]{1,0:T(8,128)(2,1)}, u32[]{:S(2)}) copy-start(bf16[176,1024]{1,0:T(8,128)(2,1)} %wg.1) | copy-start | bytes 1081348
  4.4 1.0 %copy-start.2 = (bf16[176,1024]{1,0:T(8,128)(2,1)S(1)}, bf16[176,1024]{1,0:T(8,128)(2,1)}, u32[]{:S(2)}) copy-start(bf16[176,1024]{1,0:T(8,128)(2,1)} %wu.1) | copy-start | bytes 1081348
  5.4 1.0 %copy-start.3 = (bf16[64,2816]{1,0:T(8,128)(2,1)S(1)}, bf16[64,2816]{1,0:T(8,128)(2,1)}, u32[]{:S(2)}) copy-start(bf16[64,2816]{1,0:T(8,128)(2,1)} %wd.1) | copy-start | bytes 1081348
  6.4 0.9 copy-start.4
  7.3 0.9 copy-start.5
  8.2 0.9 copy-start.6
  9.1 0.9 copy-start.7
  75.7 18.1 %collective-permute-start = (bf16[256,1024]{1,0:T(8,128)(2,1)S(1)}, bf16[256,1024]{1,0:T(8,128)(2,1)S(1)}, u32[]{:S(2)}, u32[]{:S(2)}) collective-permute-start(bf16[256,1024]{1,0:T(8,128)(2,1)S(1)} %get-tuple-element.62.mine), channel_id=1, source_target_pairs={{0,8},{8,0},{1,9},{9,1},{2,10},{10,2},{3,11},{11,3},{4,12},{12,4},... | collective-permute-start | bytes 1572872 | tf_op jit(solution)/shard_map/ppermute | solution.py:581

commit v4 on v3

--- a/solution.py
+++ b/solution.py
@@ -330,19 +330,24 @@
         self.buf[self.p.col_block(0)] = self.own[:, pl.ds(pl.multiple_of(self.p.z * self.n, 128), self.n)]
 
 
-def layer_kernel(wq, wk, wv, wo, wg, wu, wd, small, x_ref, cos_ref, sin_ref, len_ref, k_hbm, v_hbm,
+def layer_kernel(wq_hbm, wk_hbm, wv_hbm, wo_hbm, wg_hbm, wu_hbm, wd_hbm, x_hbm, k_hbm, v_hbm,
+                 bq, bk, bv, ga, gm, cos_ref, sin_ref, len_ref,
                  wqkv, wgu, wout, wdn, k_lo, k_hi, v_lo, v_hi, smalls, x1_ref, down,
-                 h_ref, sc_ref, o_ref, a_ref, t_q, t_gu,
+                 h_ref, sc_ref, o_ref, a_ref, t_q, t_gu, w_q, w_gu, wo, wd, x_ref, small, l_sem,
                  k_sem, v_sem, s_send, s_recv, p_send, p_recv, row_s, row_r, row_c, col_s, col_r, col_c):
     place = Place()
     me = place.dp * 2 + place.z
     row_sem, col_sem = (row_s, row_r, row_c), (col_s, col_r, col_c)
-    half = pl.ds(0, 88), pl.ds(88, 88)
+    loads = [(wq_hbm, w_q.at[0]), (wk_hbm, w_q.at[1]), (wv_hbm, w_q.at[2]), (wo_hbm, wo), (wg_hbm, w_gu.at[0]),
+             (wu_hbm, w_gu.at[1]), (wd_hbm, wd), (x_hbm, x_ref)]
+    loads = [pltpu.make_async_copy(src, dst, l_sem.at[i]) for i, (src, dst) in enumerate(loads)]
+    for load in loads:
+        load.start()
     chunks = {}
-    for i, ref in enumerate((wq, wk, wv)):
-        chunks[f"q{i}"] = Rows(place, wqkv, 64 * i, ref, t_q.at[i], i, row_sem)
+    for i in range(3):
+        chunks[f"q{i}"] = Rows(place, wqkv, 64 * i, w_q.at[i], t_q.at[i], i, row_sem)
     for i in range(4):
-        ref = (wg, wu)[i // 2].at[half[i % 2]]
+        ref = w_gu.at[i // 2, pl.ds(88 * (i % 2), 88)]
         chunks["gu"[i // 2] + str(i % 2)] = Rows(place, wgu, 88 * i, ref, t_gu.at[i], 3 + i, row_sem)
     chunks["o"] = Cols(place, wout, wo, 0, col_sem)
     chunks["d"] = Cols(place, wdn, wd, 1, col_sem)
@@ -385,6 +390,14 @@
     for i in range(8):
         for copy in cache_copy(i):
             copy.start()
+    vectors = jnp.concatenate([v[...].astype(F32) for v in (bq, bk, bv, ga, gm)] + [jnp.zeros((3, 64), F32)], axis=0)
+    vectors = jnp.concatenate([vectors, vectors], axis=1)
+    mine = lax.broadcasted_iota(jnp.int32, (8, 128), 1) // 64 == place.z
+    vectors = jnp.where(mine, vectors, 0.0).astype(BF16)
+    small[...] = vectors
+    smalls[me] = vectors
+    for load in loads:
+        load.wait()
     pl.semaphore_wait(barrier, 15)
 
     def small_copy(i):
@@ -397,7 +410,6 @@
 
     for chunk in chunks.values():
         chunk.local()
-    smalls[me] = small[...]
     for i in range(1, 16):
         small_copy(i).wait_recv()
 
@@ -431,7 +443,7 @@
         q = rotated(0, 0).astype(F32)
         k_new = rotated(64, 1)
         v_new = (res[128:192] + bias_column(head, 2)).astype(BF16)
-        lens = len_ref[...]
+        lens = len_ref[...].astype(F32)
         for copy in cache_copy(i):
             copy.wait()
 
@@ -538,15 +550,11 @@
 
 def local_step(w_query, b_query, w_key, b_key, w_value, b_value, w_out, w_gate, w_up, w_down, gain_attn, gain_mlp,
                hidden, k_cache, v_cache, lengths):
-    z = lax.axis_index("tp")
-    vectors = jnp.stack([b_query, b_key, b_value, gain_attn, gain_mlp])
-    zeros = jnp.zeros_like(vectors)
-    small = jnp.concatenate([jnp.where(z == 0, vectors, zeros), jnp.where(z == 0, zeros, vectors)], axis=1)
-    small = jnp.pad(small, ((0, 3), (0, 0)))
     inv_freq = 1.0 / (THETA ** (jnp.arange(0, 64, 2, dtype=F32) / 64))
     angles = inv_freq[:, None] * lengths.astype(F32)[None, :]
     cos, sin = jnp.cos(angles), jnp.sin(angles)
-    lens = lengths.astype(F32)[None, :]
+    lens = lengths[None, :]
+    rows = [v[None, :] for v in (b_query, b_key, b_value, gain_attn, gain_mlp)]
     k_view = jnp.transpose(k_cache, (1, 2, 3, 0))
     v_view = jnp.transpose(v_cache, (1, 2, 3, 0))
 
@@ -559,7 +567,7 @@
     held = pl.pallas_call(
         layer_kernel,
         out_shape=[pltpu.VMEM(s, BF16) for s in shapes],
-        in_specs=[vmem] * 12 + [hbm] * 2,
+        in_specs=[hbm] * 10 + [vmem] * 8,
         out_specs=[vmem] * 11,
         scratch_shapes=[
             pltpu.VMEM((256, 1024), BF16),
@@ -568,12 +576,19 @@
             pltpu.VMEM((8, 176, 256), BF16),
             pltpu.VMEM((3, 64, 1024), BF16),
             pltpu.VMEM((4, 88, 1024), BF16),
+            pltpu.VMEM((3, 64, 1024), BF16),
+            pltpu.VMEM((2, 176, 1024), BF16),
+            pltpu.VMEM((64, 1024), BF16),
+            pltpu.VMEM((64, 2816), BF16),
+            pltpu.VMEM((256, 1024), BF16),
+            pltpu.VMEM((8, 128), BF16),
+            dma((8,)),
             dma((16,)), dma((16,)), dma((16,)), dma((16,)), dma, dma,
             dma((7, 4, 5)), dma((7, 5)), dma((7, 4)), dma((2, 4, 8)), dma((2, 8)), dma((2, 8)),
         ],
-        compiler_params=pltpu.CompilerParams(collective_id=0, has_side_effects=True, vmem_limit_bytes=5 * 2**20),
+        compiler_params=pltpu.CompilerParams(collective_id=0, has_side_effects=True, vmem_limit_bytes=9437184),
         name="layer",
-    )(w_query, w_key, w_value, w_out, w_gate, w_up, w_down, small, hidden, cos, sin, lens, k_view, v_view)
+    )(w_query, w_key, w_value, w_out, w_gate, w_up, w_down, hidden, k_view, v_view, *rows, cos, sin, lens)
 
     def shape(*dims):
         return jax.ShapeDtypeStruct(dims, BF16)
@@ -587,7 +602,7 @@
         in_specs=[anywhere] * 8 + [vmem],
         out_specs=[hbm] * 9 + [vmem] * 5,
         scratch_shapes=[dma((11,))],
-        compiler_params=pltpu.CompilerParams(vmem_limit_bytes=2**20),
+        compiler_params=pltpu.CompilerParams(vmem_limit_bytes=9437184),
         cost_estimate=pl.CostEstimate(flops=2 * 10**10, bytes_accessed=5 * 10**7, transcendentals=0),
         name="store",
     )(*held[:9])
@@ -596,7 +611,7 @@
         out_shape=shape(256, 1024),
         in_specs=[vmem] * 3,
         out_specs=vmem,
-        compiler_params=pltpu.CompilerParams(vmem_limit_bytes=4 * 2**20),
+        compiler_params=pltpu.CompilerParams(vmem_limit_bytes=9437184),
         name="finish",
     )(held[9], held[10], peer)
     wq, wk, wv, wo, wg, wu, wd, k_out, v_out, bq, bk, bv, ga, gm = outs

time: 95.3 us -> 88.1 us (0.924)
  local copies, waits for them, and re-layouts: 8.35 us -> 0 us
    unnamed x16 -> x0, local copies, waits for them, and re-layouts: 7.6 us -> none
  transfers between devices with their start and end apart: 1 -> 1, of which waited for: 0 -> 0; matrix products, arithmetic and copies ran while one was open for 0% -> 0% of each run, Pallas kernels for 16% -> 18%
where the time goes in v4:
time: 88.1 us; the launch traced here: 87.9 us
  Pallas kernels  83.2 us (94%)
  starting transfers between devices  2.57 us (3%)
  other arithmetic  1.52 us (2%)
    pallas_call x1, Pallas kernels, local_step(): pl.pallas_call(layer_kernel, out_shape=[pltpu.VMEM(s, BF16) for s in shap...  66.6 us
    pallas_call x1, Pallas kernels, local_step(): pl.pallas_call(store_kernel, out_shape=[shape(8, 64, 1024)] * 3 + [shape(...  15.5 us
    ppermute x1, starting transfers between devices, local_step(): peer = lax.ppermute(held[10], 'tp', [(0, 1), (1, 0)])  2.57 us
  transfers between devices with their start and end apart: 1, of which 0 were waited for; matrix products, arithmetic and copies ran while one was open for 0% of the time, Pallas kernels for 18%

profile of v4, /device:TPU:0, one launch (start us, length us, event | category | flops | bytes accessed | tf_op | source)
XLA Modules:
  0.0 87.9 jit_solution(8625556101402556727)
XLA Ops:
  0.7 0.7 convert_element_type.3
  1.3 0.8 multiply_sine_fusion
  2.2 66.6 %layer.1 = (bf16[8,192,1024]{2,1,0:T(8,128)(2,1)S(1)}, bf16[8,352,1024]{2,1,0:T(8,128)(2,1)S(1)}, bf16[16,64,512]{2,1,0:T(8,128)(2,1)S(1)}, bf16[16,64,1408]{2,1...) custom-call(bf16[64,1024]{1,0:T(8,128)(2,1)} %wq_hbm.1, ...), custom_call_target="tpu_custom_call" | custom-call | tf_op jit(solution)/shard_map/layer/pallas_call | solution.py:567
  68.8 2.6 %collective-permute-start = (bf16[256,1024]{1,0:T(8,128)(2,1)S(1)}, bf16[256,1024]{1,0:T(8,128)(2,1)S(1)}, u32[]{:S(2)}, u32[]{:S(2)}) collective-permute-start(bf16[256,1024]{1,0:T(8,128)(2,1)S(1)} %get-tuple-element.62.mine), channel_id=1, source_target_pairs={{0,8},{8,0},{1,9},{9,1},{2,10},{10,2},{3,11},{11,3},{4,12},{12,4},... | collective-permute-start | bytes 1572872 | tf_op jit(solution)/shard_map/ppermute | solution.py:596
  71.4 15.5 %store.1 = (bf16[8,64,1024]{2,1,0:T(8,128)(2,1)}, bf16[8,64,1024]{2,1,0:T(8,128)(2,1)}, bf16[8,64,1024]{2,1,0:T(8,128)(2,1)}, bf16[16,64,512]{2,1,0:T(8,128)(2,1...) custom-call(bf16[8,192,1024]{2,1,0:T(8,128)(2,1)S(1)} %get-tuple-ele, ...), custom_call_target="tpu_custom_call" | custom-call | flops 20000000000 | bytes 50000000 | tf_op jit(solution)/shard_map/store/pallas_call | solution.py:597
  86.9 0.0 collective-permute-done.peer
  86.9 1.0 %finish.1 = bf16[256,1024]{1,0:T(8,128)(2,1)} custom-call(bf16[256,1024]{1,0:T(8,128)(2,1)S(1)} %get-tuple-element.61.x1, bf16[256,1024]{1,0:T(8,128)(2,1)S(1)} %get-tuple-element.62.mine, bf16[256,1024]{1,0:T(8,128)(2,1)S(1)} %collective-permute-done.peer), custom_call_target="tpu_custom_call" | custom-call | tf_op jit(solution)/shard_map/finish/pallas_call | solution.py:609
  (1 shorter events, 0.0 us)
Async XLA Ops:
  68.8 18.1 %collective-permute-start = (bf16[256,1024]{1,0:T(8,128)(2,1)S(1)}, bf16[256,1024]{1,0:T(8,128)(2,1)S(1)}, u32[]{:S(2)}, u32[]{:S(2)}) collective-permute-start(bf16[256,1024]{1,0:T(8,128)(2,1)S(1)} %get-tuple-element.62.mine), channel_id=1, source_target_pairs={{0,8},{8,0},{1,9},{9,1},{2,10},{10,2},{3,11},{11,3},{4,12},{12,4},... | collective-permute-start | bytes 1572872 | tf_op jit(solution)/shard_map/ppermute | solution.py:596

commit v5 on v4

--- a/solution.py
+++ b/solution.py
@@ -331,9 +331,9 @@
 
 
 def layer_kernel(wq_hbm, wk_hbm, wv_hbm, wo_hbm, wg_hbm, wu_hbm, wd_hbm, x_hbm, k_hbm, v_hbm,
-                 bq, bk, bv, ga, gm, cos_ref, sin_ref, len_ref,
+                 bq, bk, bv, ga, gm, freq_ref, len_ref,
                  wqkv, wgu, wout, wdn, k_lo, k_hi, v_lo, v_hi, smalls, x1_ref, down,
-                 h_ref, sc_ref, o_ref, a_ref, t_q, t_gu, w_q, w_gu, wo, wd, x_ref, small, l_sem,
+                 h_ref, sc_ref, o_ref, a_ref, cos_ref, sin_ref, t_q, t_gu, w_q, w_gu, wo, wd, x_ref, small, l_sem,
                  k_sem, v_sem, s_send, s_recv, p_send, p_recv, row_s, row_r, row_c, col_s, col_r, col_c):
     place = Place()
     me = place.dp * 2 + place.z
@@ -387,15 +387,15 @@
     for i in range(1, 16):
         other = lax.rem(me + i, 16)
         pl.semaphore_signal(barrier, inc=1, device_id=(other % 2, other // 2), device_id_type=MESH)
-    for i in range(8):
-        for copy in cache_copy(i):
-            copy.start()
     vectors = jnp.concatenate([v[...].astype(F32) for v in (bq, bk, bv, ga, gm)] + [jnp.zeros((3, 64), F32)], axis=0)
     vectors = jnp.concatenate([vectors, vectors], axis=1)
     mine = lax.broadcasted_iota(jnp.int32, (8, 128), 1) // 64 == place.z
     vectors = jnp.where(mine, vectors, 0.0).astype(BF16)
     small[...] = vectors
     smalls[me] = vectors
+    angles = freq_ref[...] * len_ref[...].astype(F32)
+    cos_ref[...] = jnp.cos(angles)
+    sin_ref[...] = jnp.sin(angles)
     for load in loads:
         load.wait()
     pl.semaphore_wait(barrier, 15)
@@ -404,9 +404,12 @@
         other = lax.rem(me + i, 16)
         return remote(small, smalls.at[me], s_send.at[i], s_recv.at[i], (other % 2, other // 2))
 
+    go()
     for i in range(1, 16):
         small_copy(i).start()
-    go()
+    for i in range(8):
+        for copy in cache_copy(i):
+            copy.start()
 
     for chunk in chunks.values():
         chunk.local()
@@ -524,9 +527,9 @@
 
 def store_kernel(wqkv, wgu, wout, wdn, k_lo, k_hi, v_lo, v_hi, smalls,
                  wq, wk, wv, wo, wg, wu, wd, k_out, v_out, bq, bk, bv, ga, gm, sem):
-    lo, hi = pl.ds(0, 32), pl.ds(32, 32)
-    pairs = [(k_lo, k_out.at[lo]), (k_hi, k_out.at[hi]), (v_lo, v_out.at[lo]), (v_hi, v_out.at[hi]),
-             (wdn, wd), (wgu.at[:, pl.ds(0, 176)], wg), (wgu.at[:, pl.ds(176, 176)], wu),
+    pairs = [(src.at[pl.ds(16 * i, 16)], dst.at[pl.ds(base + 16 * i, 16)]) for src, dst, base in (
+        (k_lo, k_out, 0), (k_hi, k_out, 32), (v_lo, v_out, 0), (v_hi, v_out, 32)) for i in range(2)]
+    pairs += [(wdn, wd), (wgu.at[:, pl.ds(0, 176)], wg), (wgu.at[:, pl.ds(176, 176)], wu),
              (wqkv.at[:, pl.ds(0, 64)], wq), (wqkv.at[:, pl.ds(64, 64)], wk), (wqkv.at[:, pl.ds(128, 64)], wv),
              (wout, wo)]
     copies = [pltpu.make_async_copy(src, dst, sem.at[i]) for i, (src, dst) in enumerate(pairs)]
@@ -551,8 +554,7 @@
 def local_step(w_query, b_query, w_key, b_key, w_value, b_value, w_out, w_gate, w_up, w_down, gain_attn, gain_mlp,
                hidden, k_cache, v_cache, lengths):
     inv_freq = 1.0 / (THETA ** (jnp.arange(0, 64, 2, dtype=F32) / 64))
-    angles = inv_freq[:, None] * lengths.astype(F32)[None, :]
-    cos, sin = jnp.cos(angles), jnp.sin(angles)
+    freq = jnp.broadcast_to(inv_freq[:, None], (32, 256))
     lens = lengths[None, :]
     rows = [v[None, :] for v in (b_query, b_key, b_value, gain_attn, gain_mlp)]
     k_view = jnp.transpose(k_cache, (1, 2, 3, 0))
@@ -567,13 +569,15 @@
     held = pl.pallas_call(
         layer_kernel,
         out_shape=[pltpu.VMEM(s, BF16) for s in shapes],
-        in_specs=[hbm] * 10 + [vmem] * 8,
+        in_specs=[hbm] * 10 + [vmem] * 7,
         out_specs=[vmem] * 11,
         scratch_shapes=[
             pltpu.VMEM((256, 1024), BF16),
             pltpu.VMEM((64, 256), F32),
             pltpu.VMEM((512, 256), BF16),
             pltpu.VMEM((8, 176, 256), BF16),
+            pltpu.VMEM((32, 256), F32),
+            pltpu.VMEM((32, 256), F32),
             pltpu.VMEM((3, 64, 1024), BF16),
             pltpu.VMEM((4, 88, 1024), BF16),
             pltpu.VMEM((3, 64, 1024), BF16),
@@ -588,7 +592,7 @@
         ],
         compiler_params=pltpu.CompilerParams(collective_id=0, has_side_effects=True, vmem_limit_bytes=9437184),
         name="layer",
-    )(w_query, w_key, w_value, w_out, w_gate, w_up, w_down, hidden, k_view, v_view, *rows, cos, sin, lens)
+    )(w_query, w_key, w_value, w_out, w_gate, w_up, w_down, hidden, k_view, v_view, *rows, freq, lens)
 
     def shape(*dims):
         return jax.ShapeDtypeStruct(dims, BF16)
@@ -601,7 +605,7 @@
                    shape(4, 128), shape(4, 128), shape(4, 128), shape(8, 128), shape(8, 128)],
         in_specs=[anywhere] * 8 + [vmem],
         out_specs=[hbm] * 9 + [vmem] * 5,
-        scratch_shapes=[dma((11,))],
+        scratch_shapes=[dma((15,))],
         compiler_params=pltpu.CompilerParams(vmem_limit_bytes=9437184),
         cost_estimate=pl.CostEstimate(flops=2 * 10**10, bytes_accessed=5 * 10**7, transcendentals=0),
         name="store",

time: 88.1 us -> 91.1 us (1.034)
  Pallas kernels: 83.2 us -> 87.8 us
  other arithmetic: 1.52 us -> 0.01 us
    pallas_call x1, Pallas kernels: 66.6 us -> 71.3 us  [local_step(): pl.pallas_call(layer_kernel, out_shape=[pltpu.VMEM(s, BF16) for s in shap...]
  transfers between devices with their start and end apart: 1 -> 1, of which waited for: 0 -> 0; matrix products, arithmetic and copies ran while one was open for 0% -> 0% of each run, Pallas kernels for 18% -> 17%
where the time goes in v5:
time: 91.1 us; the launch traced here: 90.9 us
  Pallas kernels  87.8 us (96%)
  starting transfers between devices  1.69 us (2%)
    pallas_call x1, Pallas kernels, local_step(): pl.pallas_call(layer_kernel, out_shape=[pltpu.VMEM(s, BF16) for s in shap...  71.3 us
    pallas_call x1, Pallas kernels, local_step(): pl.pallas_call(store_kernel, out_shape=[shape(8, 64, 1024)] * 3 + [shape(...  15.5 us
  transfers between devices with their start and end apart: 1, of which 0 were waited for; matrix products, arithmetic and copies ran while one was open for 0% of the time, Pallas kernels for 17%

profile of v5, /device:TPU:0, one launch (start us, length us, event | category | flops | bytes accessed | tf_op | source)
XLA Modules:
  0.0 90.9 jit_solution(773347139021345685)
XLA Ops:
  0.7 0.7 broadcast_in_dim.29.freq_ref
  1.3 71.3 %layer.1 = (bf16[8,192,1024]{2,1,0:T(8,128)(2,1)S(1)}, bf16[8,352,1024]{2,1,0:T(8,128)(2,1)S(1)}, bf16[16,64,512]{2,1,0:T(8,128)(2,1)S(1)}, bf16[16,64,1408]{2,1...) custom-call(bf16[64,1024]{1,0:T(8,128)(2,1)} %wq_hbm.1, ...), custom_call_target="tpu_custom_call" | custom-call | tf_op jit(solution)/shard_map/layer/pallas_call | solution.py:569
  72.7 1.7 %collective-permute-start = (bf16[256,1024]{1,0:T(8,128)(2,1)S(1)}, bf16[256,1024]{1,0:T(8,128)(2,1)S(1)}, u32[]{:S(2)}, u32[]{:S(2)}) collective-permute-start(bf16[256,1024]{1,0:T(8,128)(2,1)S(1)} %get-tuple-element.62.mine), channel_id=1, source_target_pairs={{0,8},{8,0},{1,9},{9,1},{2,10},{10,2},{3,11},{11,3},{4,12},{12,4},... | collective-permute-start | bytes 1572872 | tf_op jit(solution)/shard_map/ppermute | solution.py:600
  74.4 15.5 %store.1 = (bf16[8,64,1024]{2,1,0:T(8,128)(2,1)}, bf16[8,64,1024]{2,1,0:T(8,128)(2,1)}, bf16[8,64,1024]{2,1,0:T(8,128)(2,1)}, bf16[16,64,512]{2,1,0:T(8,128)(2,1...) custom-call(bf16[8,192,1024]{2,1,0:T(8,128)(2,1)S(1)} %get-tuple-ele, ...), custom_call_target="tpu_custom_call" | custom-call | flops 20000000000 | bytes 50000000 | tf_op jit(solution)/shard_map/store/pallas_call | solution.py:601
  89.8 0.0 collective-permute-done.peer
  89.8 1.0 %finish.1 = bf16[256,1024]{1,0:T(8,128)(2,1)} custom-call(bf16[256,1024]{1,0:T(8,128)(2,1)S(1)} %get-tuple-element.61.x1, bf16[256,1024]{1,0:T(8,128)(2,1)S(1)} %get-tuple-element.62.mine, bf16[256,1024]{1,0:T(8,128)(2,1)S(1)} %collective-permute-done.peer), custom_call_target="tpu_custom_call" | custom-call | tf_op jit(solution)/shard_map/finish/pallas_call | solution.py:613
  (1 shorter events, 0.0 us)
Async XLA Ops:
  72.7 17.1 %collective-permute-start = (bf16[256,1024]{1,0:T(8,128)(2,1)S(1)}, bf16[256,1024]{1,0:T(8,128)(2,1)S(1)}, u32[]{:S(2)}, u32[]{:S(2)}) collective-permute-start(bf16[256,1024]{1,0:T(8,128)(2,1)S(1)} %get-tuple-element.62.mine), channel_id=1, source_target_pairs={{0,8},{8,0},{1,9},{9,1},{2,10},{10,2},{3,11},{11,3},{4,12},{12,4},... | collective-permute-start | bytes 1572872 | tf_op jit(solution)/shard_map/ppermute | solution.py:600

commit v6 on v5

--- a/solution.py
+++ b/solution.py
@@ -1,5 +1,6 @@
 import jax
 import jax.numpy as jnp
+import numpy as np
 from jax import lax
 from jax.experimental import pallas as pl
 from jax.experimental.pallas import tpu as pltpu
@@ -10,9 +11,10 @@
 MESH = pl.DeviceIdType.MESH
 F32 = jnp.float32
 BF16 = jnp.bfloat16
-ROW_BYTES = (((1,), (1,)), ((), ()))
+BY_ROWS = (((1,), (1,)), ((), ()))
 NAT = (((1,), (0,)), ((), ()))
 GROUP = 8
+AHEAD = 3
 
 
 def dot(lhs, rhs, dims):
@@ -387,32 +389,32 @@
     for i in range(1, 16):
         other = lax.rem(me + i, 16)
         pl.semaphore_signal(barrier, inc=1, device_id=(other % 2, other // 2), device_id_type=MESH)
+    for i in range(AHEAD):
+        for copy in cache_copy(i):
+            copy.start()
     vectors = jnp.concatenate([v[...].astype(F32) for v in (bq, bk, bv, ga, gm)] + [jnp.zeros((3, 64), F32)], axis=0)
     vectors = jnp.concatenate([vectors, vectors], axis=1)
     mine = lax.broadcasted_iota(jnp.int32, (8, 128), 1) // 64 == place.z
     vectors = jnp.where(mine, vectors, 0.0).astype(BF16)
     small[...] = vectors
     smalls[me] = vectors
+    for load in loads:
+        load.wait()
+    pl.semaphore_wait(barrier, 15)
+
+    def small_copy(i):
+        other = lax.rem(me + i, 16)
+        return remote(small, smalls.at[me], s_send.at[i], s_recv.at[i], (other % 2, other // 2))
+
+    go()
+    for i in range(1, 16):
+        small_copy(i).start()
+
+    for chunk in chunks.values():
+        chunk.local()
     angles = freq_ref[...] * len_ref[...].astype(F32)
     cos_ref[...] = jnp.cos(angles)
     sin_ref[...] = jnp.sin(angles)
-    for load in loads:
-        load.wait()
-    pl.semaphore_wait(barrier, 15)
-
-    def small_copy(i):
-        other = lax.rem(me + i, 16)
-        return remote(small, smalls.at[me], s_send.at[i], s_recv.at[i], (other % 2, other // 2))
-
-    go()
-    for i in range(1, 16):
-        small_copy(i).start()
-    for i in range(8):
-        for copy in cache_copy(i):
-            copy.start()
-
-    for chunk in chunks.values():
-        chunk.local()
     for i in range(1, 16):
         small_copy(i).wait_recv()
 
@@ -435,7 +437,7 @@
 
     def attend(i):
         head = by_role("attend", i, place.row_block)
-        res = dot(wqkv[head], h_ref[...], ROW_BYTES)
+        res = dot(wqkv[head], h_ref[...], BY_ROWS)
         cos, sin = cos_ref[...], sin_ref[...]
 
         def rotated(start, b):
@@ -483,12 +485,15 @@
 
     go()
     for i in range(8):
+        if i + AHEAD < 8:
+            for copy in cache_copy(i + AHEAD):
+                copy.start()
         attend(i)
         go()
 
     o = o_ref[...].T
     part, part_in, h2_ref = down, x1_ref, h_ref
-    part[...] = dot(o, wout[...].reshape(1024, 512), ROW_BYTES).astype(BF16)
+    part[...] = dot(o, wout[...].reshape(1024, 512), BY_ROWS).astype(BF16)
     swap = remote(part, part_in, p_send, p_recv, place.device["z"])
     swap.start()
     go()
@@ -502,7 +507,7 @@
 
     for i in range(8):
         block = by_role("gated", i, place.row_block)
-        res = dot(wgu[block], h2_ref[...], ROW_BYTES).astype(BF16).astype(F32)
+        res = dot(wgu[block], h2_ref[...], BY_ROWS).astype(BF16).astype(F32)
         g, u = res[:176], res[176:]
         a_ref[block] = (g / (1.0 + jnp.exp(-g)) * u).astype(BF16)
         go()
@@ -553,8 +558,7 @@
 
 def local_step(w_query, b_query, w_key, b_key, w_value, b_value, w_out, w_gate, w_up, w_down, gain_attn, gain_mlp,
                hidden, k_cache, v_cache, lengths):
-    inv_freq = 1.0 / (THETA ** (jnp.arange(0, 64, 2, dtype=F32) / 64))
-    freq = jnp.broadcast_to(inv_freq[:, None], (32, 256))
+    freq = np.tile((1.0 / THETA ** (np.arange(0, 64, 2) / 64)).astype(np.float32)[:, None], (1, 256))
     lens = lengths[None, :]
     rows = [v[None, :] for v in (b_query, b_key, b_value, gain_attn, gain_mlp)]
     k_view = jnp.transpose(k_cache, (1, 2, 3, 0))

time: 91.1 us -> 90.4 us (level)
  no operation moved by 1% of the time
where the time goes in v6:
time: 90.4 us; the launch traced here: 90.2 us
  Pallas kernels  87.8 us (97%)
  starting transfers between devices  1.68 us (2%)
    pallas_call x1, Pallas kernels, local_step(): pl.pallas_call(layer_kernel, out_shape=[pltpu.VMEM(s, BF16) for s in shap...  71.3 us
    pallas_call x1, Pallas kernels, local_step(): pl.pallas_call(store_kernel, out_shape=[shape(8, 64, 1024)] * 3 + [shape(...  15.5 us
  transfers between devices with their start and end apart: 1, of which 0 were waited for; matrix products, arithmetic and copies ran while one was open for 0% of the time, Pallas kernels for 17%

profile of v6, /device:TPU:0, one launch (start us, length us, event | category | flops | bytes accessed | tf_op | source)
XLA Modules:
  0.0 90.2 jit_solution(36272438171019286)
XLA Ops:
  0.7 71.3 %layer.1 = (bf16[8,192,1024]{2,1,0:T(8,128)(2,1)S(1)}, bf16[8,352,1024]{2,1,0:T(8,128)(2,1)S(1)}, bf16[16,64,512]{2,1,0:T(8,128)(2,1)S(1)}, bf16[16,64,1408]{2,1...) custom-call(bf16[64,1024]{1,0:T(8,128)(2,1)} %wq_hbm.1, ...), custom_call_target="tpu_custom_call" | custom-call | tf_op jit(solution)/shard_map/layer/pallas_call | solution.py:573
  72.0 1.7 %collective-permute-start = (bf16[256,1024]{1,0:T(8,128)(2,1)S(1)}, bf16[256,1024]{1,0:T(8,128)(2,1)S(1)}, u32[]{:S(2)}, u32[]{:S(2)}) collective-permute-start(bf16[256,1024]{1,0:T(8,128)(2,1)S(1)} %get-tuple-element.62.mine), channel_id=1, source_target_pairs={{0,8},{8,0},{1,9},{9,1},{2,10},{10,2},{3,11},{11,3},{4,12},{12,4},... | collective-permute-start | bytes 1572872 | tf_op jit(solution)/shard_map/ppermute | solution.py:604
  73.7 15.5 %store.1 = (bf16[8,64,1024]{2,1,0:T(8,128)(2,1)}, bf16[8,64,1024]{2,1,0:T(8,128)(2,1)}, bf16[8,64,1024]{2,1,0:T(8,128)(2,1)}, bf16[16,64,512]{2,1,0:T(8,128)(2,1...) custom-call(bf16[8,192,1024]{2,1,0:T(8,128)(2,1)S(1)} %get-tuple-ele, ...), custom_call_target="tpu_custom_call" | custom-call | flops 20000000000 | bytes 50000000 | tf_op jit(solution)/shard_map/store/pallas_call | solution.py:605
  89.1 0.0 collective-permute-done.peer
  89.2 1.0 %finish.1 = bf16[256,1024]{1,0:T(8,128)(2,1)} custom-call(bf16[256,1024]{1,0:T(8,128)(2,1)S(1)} %get-tuple-element.61.x1, bf16[256,1024]{1,0:T(8,128)(2,1)S(1)} %get-tuple-element.62.mine, bf16[256,1024]{1,0:T(8,128)(2,1)S(1)} %collective-permute-done.peer), custom_call_target="tpu_custom_call" | custom-call | tf_op jit(solution)/shard_map/finish/pallas_call | solution.py:617
Async XLA Ops:
  72.0 17.1 %collective-permute-start = (bf16[256,1024]{1,0:T(8,128)(2,1)S(1)}, bf16[256,1024]{1,0:T(8,128)(2,1)S(1)}, u32[]{:S(2)}, u32[]{:S(2)}) collective-permute-start(bf16[256,1024]{1,0:T(8,128)(2,1)S(1)} %get-tuple-element.62.mine), channel_id=1, source_target_pairs={{0,8},{8,0},{1,9},{9,1},{2,10},{10,2},{3,11},{11,3},{4,12},{12,4},... | collective-permute-start | bytes 1572872 | tf_op jit(solution)/shard_map/ppermute | solution.py:604

commit v7 on v6

--- a/solution.py
+++ b/solution.py
@@ -23,13 +23,14 @@
 
 HOME_STEPS = (
     (
-        ("s", "q0", 0, "c", 0), ("s", "q1", 0, "c", 0), ("s", "q2", 0, "c", 0), ("s", "g0", 0, "c", 0),
-        ("s", "g1", 0, "c", 0), ("s", "u0", 0, "c", 0), ("s", "u1", 0, "c", 0), ("s", "o", 0, "c", 0),
-        ("s", "d", 0, "c", 0), ("s", "o", "z", "z", 4), ("s", "d", "z", "z", 4), ("s", "q1", 0, "y", 0),
-        ("s", "q1", 0, "x", 1),
-    ),
-    (
-        ("s", "o", 0, "y", 2), ("s", "q2", 0, "y", 0), ("s", "o", 0, "x", 1), ("s", "q2", 0, "x", 1),
+        ("s", "q1", 0, "y", 0), ("s", "q1", 0, "x", 1), ("s", "q2", 0, "y", 0), ("s", "q2", 0, "x", 1),
+        ("s", "q0", 0, "y", 0), ("s", "q0", 0, "x", 1), ("s", "q0", 0, "c", 0), ("s", "q1", 0, "c", 0),
+        ("s", "q2", 0, "c", 0), ("s", "g0", 0, "c", 0), ("s", "g1", 0, "c", 0), ("s", "u0", 0, "c", 0),
+        ("s", "u1", 0, "c", 0), ("s", "o", 0, "c", 0), ("s", "d", 0, "c", 0), ("s", "o", "z", "z", 4),
+        ("s", "d", "z", "z", 4),
+    ),
+    (
+        ("s", "o", 0, "y", 2), ("s", "o", 0, "x", 1),
     ),
     (
         ("w", "o", 4), ("s", "o", 4, "c", 4), ("w", "q0", "c", 0), ("w", "q1", "c", 0), ("w", "q2", "c", 0),
@@ -37,10 +38,10 @@
     (
         ("w", "q1", "t"), ("w", "q1", 1), ("s", "q1", 1, "c", 1), ("s", "q1", "t", "z", 2), ("s", "o", 4, "y", 6),
         ("s", "o", 4, "x", 5), ("w", "q1", 2), ("s", "q1", 2, "c", 2), ("w", "o", 1), ("s", "o", 1, "c", 1),
-        ("s", "q0", 0, "y", 0), ("s", "q0", 0, "x", 1), ("w", "q2", "t"), ("s", "q2", "t", "z", 2), ("w", "q2", 1),
-        ("s", "q2", 1, "c", 1), ("w", "q2", 2), ("s", "q2", 2, "c", 2), ("s", "g0", 0, "y", 0), ("s", "q1", 2, "x", 3),
-        ("w", "o", 5), ("s", "o", 5, "c", 5), ("w", "q0", "t"), ("s", "q0", "t", "z", 2), ("w", "o", 2),
-        ("s", "o", 2, "c", 2), ("w", "q0", 2), ("s", "q0", 2, "c", 2),
+        ("w", "q2", "t"), ("s", "q2", "t", "z", 2), ("w", "q2", 1), ("s", "q2", 1, "c", 1), ("w", "q2", 2),
+        ("s", "q2", 2, "c", 2), ("s", "g0", 0, "y", 0), ("s", "q1", 2, "x", 3), ("w", "o", 5), ("s", "o", 5, "c", 5),
+        ("w", "q0", "t"), ("s", "q0", "t", "z", 2), ("w", "o", 2), ("s", "o", 2, "c", 2), ("w", "q0", 2),
+        ("s", "q0", 2, "c", 2),
     ),
     (
         ("w", "o", 6), ("s", "o", 6, "c", 6), ("w", "q0", 1), ("s", "q0", 1, "c", 1), ("s", "q0", 1, "y", 1),
@@ -126,19 +127,18 @@
 }
 AWAY_STEPS = (
     (
-        ("s", "o", 0, "c", 0), ("s", "d", 0, "c", 0), ("s", "o", "z", "z", 4), ("s", "q1", "own", "z", 2),
-        ("s", "q1", "own", "y", "t"), ("s", "o", 0, "x", 1), ("s", "d", 0, "x", 1),
-    ),
-    (
-        ("s", "q2", "own", "z", 2), ("s", "q2", "own", "y", "t"), ("w", "o", 1), ("s", "o", 1, "c", 1), ("w", "o", 4),
-        ("s", "o", 4, "c", 4), ("s", "o", 4, "x", 5), ("s", "q0", "own", "y", "t"), ("w", "q1", 0),
-        ("s", "q1", 0, "c", 0), ("s", "q1", 0, "x", 1), ("s", "q0", "own", "z", 2), ("w", "o", 2),
-        ("s", "o", 2, "c", 2), ("s", "o", 0, "y", 2), ("w", "d", 1), ("s", "d", 1, "c", 1), ("w", "d", 4),
-        ("s", "d", 4, "c", 4), ("s", "d", 4, "x", 5), ("s", "g0", "own", "z", 2), ("s", "o", 4, "y", 6), ("w", "o", 5),
-        ("s", "o", 5, "c", 5), ("w", "q2", 0), ("s", "q2", 0, "c", 0), ("s", "g0", "own", "y", "t"), ("w", "o", 6),
-        ("s", "o", 6, "c", 6), ("w", "q1", 2), ("s", "q1", 2, "c", 2), ("s", "q2", 0, "x", 1), ("w", "q1", 1),
-        ("s", "q1", 1, "c", 1), ("s", "d", "z", "z", 4), ("s", "u0", "own", "y", "t"), ("w", "q0", 0),
-        ("s", "q0", 0, "c", 0),
+        ("s", "q1", "own", "z", 2), ("s", "q1", "own", "y", "t"), ("s", "q2", "own", "z", 2),
+        ("s", "q2", "own", "y", "t"), ("s", "q0", "own", "y", "t"), ("s", "q0", "own", "z", 2), ("s", "o", 0, "c", 0),
+        ("s", "d", 0, "c", 0), ("s", "o", "z", "z", 4), ("s", "o", 0, "x", 1), ("s", "d", 0, "x", 1),
+    ),
+    (
+        ("w", "o", 1), ("s", "o", 1, "c", 1), ("w", "o", 4), ("s", "o", 4, "c", 4), ("s", "o", 4, "x", 5),
+        ("w", "q1", 0), ("s", "q1", 0, "c", 0), ("s", "q1", 0, "x", 1), ("w", "o", 2), ("s", "o", 2, "c", 2),
+        ("s", "o", 0, "y", 2), ("w", "d", 1), ("s", "d", 1, "c", 1), ("w", "d", 4), ("s", "d", 4, "c", 4),
+        ("s", "d", 4, "x", 5), ("s", "g0", "own", "z", 2), ("s", "o", 4, "y", 6), ("w", "o", 5), ("s", "o", 5, "c", 5),
+        ("w", "q2", 0), ("s", "q2", 0, "c", 0), ("s", "g0", "own", "y", "t"), ("w", "o", 6), ("s", "o", 6, "c", 6),
+        ("w", "q1", 2), ("s", "q1", 2, "c", 2), ("s", "q2", 0, "x", 1), ("w", "q1", 1), ("s", "q1", 1, "c", 1),
+        ("s", "d", "z", "z", 4), ("s", "u0", "own", "y", "t"), ("w", "q0", 0), ("s", "q0", 0, "c", 0),
     ),
     (
         ("w", "q2", 2), ("s", "q2", 2, "c", 2), ("s", "q2", 2, "x", 3), ("w", "q0", "c", 0), ("w", "q1", "c", 0),
@@ -406,9 +406,9 @@
         other = lax.rem(me + i, 16)
         return remote(small, smalls.at[me], s_send.at[i], s_recv.at[i], (other % 2, other // 2))
 
-    go()
     for i in range(1, 16):
         small_copy(i).start()
+    go()
 
     for chunk in chunks.values():
         chunk.local()

time: 90.4 us -> 91.1 us (level)
  no operation moved by 1% of the time
where the time goes in v7:
time: 91.1 us; the launch traced here: 90.9 us
  Pallas kernels  87.8 us (96%)
  starting transfers between devices  2.44 us (3%)
    pallas_call x1, Pallas kernels, local_step(): pl.pallas_call(layer_kernel, out_shape=[pltpu.VMEM(s, BF16) for s in shap...  71.3 us
    pallas_call x1, Pallas kernels, local_step(): pl.pallas_call(store_kernel, out_shape=[shape(8, 64, 1024)] * 3 + [shape(...  15.5 us
    ppermute x1, starting transfers between devices, local_step(): peer = lax.ppermute(held[10], 'tp', [(0, 1), (1, 0)])  2.44 us
  transfers between devices with their start and end apart: 1, of which 0 were waited for; matrix products, arithmetic and copies ran while one was open for 0% of the time, Pallas kernels for 17%

profile of v7, /device:TPU:0, one launch (start us, length us, event | category | flops | bytes accessed | tf_op | source)
XLA Modules:
  0.0 90.9 jit_solution(10737513019448997805)
XLA Ops:
  0.7 71.3 %layer.1 = (bf16[8,192,1024]{2,1,0:T(8,128)(2,1)S(1)}, bf16[8,352,1024]{2,1,0:T(8,128)(2,1)S(1)}, bf16[16,64,512]{2,1,0:T(8,128)(2,1)S(1)}, bf16[16,64,1408]{2,1...) custom-call(bf16[64,1024]{1,0:T(8,128)(2,1)} %wq_hbm.1, ...), custom_call_target="tpu_custom_call" | custom-call | tf_op jit(solution)/shard_map/layer/pallas_call | solution.py:573
  72.0 2.4 %collective-permute-start = (bf16[256,1024]{1,0:T(8,128)(2,1)S(1)}, bf16[256,1024]{1,0:T(8,128)(2,1)S(1)}, u32[]{:S(2)}, u32[]{:S(2)}) collective-permute-start(bf16[256,1024]{1,0:T(8,128)(2,1)S(1)} %get-tuple-element.62.mine), channel_id=1, source_target_pairs={{0,8},{8,0},{1,9},{9,1},{2,10},{10,2},{3,11},{11,3},{4,12},{12,4},... | collective-permute-start | bytes 1572872 | tf_op jit(solution)/shard_map/ppermute | solution.py:604
  74.4 15.5 %store.1 = (bf16[8,64,1024]{2,1,0:T(8,128)(2,1)}, bf16[8,64,1024]{2,1,0:T(8,128)(2,1)}, bf16[8,64,1024]{2,1,0:T(8,128)(2,1)}, bf16[16,64,512]{2,1,0:T(8,128)(2,1...) custom-call(bf16[8,192,1024]{2,1,0:T(8,128)(2,1)S(1)} %get-tuple-ele, ...), custom_call_target="tpu_custom_call" | custom-call | flops 20000000000 | bytes 50000000 | tf_op jit(solution)/shard_map/store/pallas_call | solution.py:605
  89.9 0.0 collective-permute-done.peer
  89.9 1.0 %finish.1 = bf16[256,1024]{1,0:T(8,128)(2,1)} custom-call(bf16[256,1024]{1,0:T(8,128)(2,1)S(1)} %get-tuple-element.61.x1, bf16[256,1024]{1,0:T(8,128)(2,1)S(1)} %get-tuple-element.62.mine, bf16[256,1024]{1,0:T(8,128)(2,1)S(1)} %collective-permute-done.peer), custom_call_target="tpu_custom_call" | custom-call | tf_op jit(solution)/shard_map/finish/pallas_call | solution.py:617
Async XLA Ops:
  72.0 17.9 %collective-permute-start = (bf16[256,1024]{1,0:T(8,128)(2,1)S(1)}, bf16[256,1024]{1,0:T(8,128)(2,1)S(1)}, u32[]{:S(2)}, u32[]{:S(2)}) collective-permute-start(bf16[256,1024]{1,0:T(8,128)(2,1)S(1)} %get-tuple-element.62.mine), channel_id=1, source_target_pairs={{0,8},{8,0},{1,9},{9,1},{2,10},{10,2},{3,11},{11,3},{4,12},{12,4},... | collective-permute-start | bytes 1572872 | tf_op jit(solution)/shard_map/ppermute | solution.py:604

commit v8 on v7

--- a/solution.py
+++ b/solution.py
@@ -14,7 +14,6 @@
 BY_ROWS = (((1,), (1,)), ((), ()))
 NAT = (((1,), (0,)), ((), ()))
 GROUP = 8
-AHEAD = 3
 
 
 def dot(lhs, rhs, dims):
@@ -333,9 +332,9 @@
 
 
 def layer_kernel(wq_hbm, wk_hbm, wv_hbm, wo_hbm, wg_hbm, wu_hbm, wd_hbm, x_hbm, k_hbm, v_hbm,
-                 bq, bk, bv, ga, gm, freq_ref, len_ref,
+                 bq, bk, bv, ga, gm, cos_ref, sin_ref, len_ref,
                  wqkv, wgu, wout, wdn, k_lo, k_hi, v_lo, v_hi, smalls, x1_ref, down,
-                 h_ref, sc_ref, o_ref, a_ref, cos_ref, sin_ref, t_q, t_gu, w_q, w_gu, wo, wd, x_ref, small, l_sem,
+                 h_ref, sc_ref, o_ref, a_ref, t_q, t_gu, w_q, w_gu, wo, wd, x_ref, small, l_sem,
                  k_sem, v_sem, s_send, s_recv, p_send, p_recv, row_s, row_r, row_c, col_s, col_r, col_c):
     place = Place()
     me = place.dp * 2 + place.z
@@ -389,7 +388,7 @@
     for i in range(1, 16):
         other = lax.rem(me + i, 16)
         pl.semaphore_signal(barrier, inc=1, device_id=(other % 2, other // 2), device_id_type=MESH)
-    for i in range(AHEAD):
+    for i in range(8):
         for copy in cache_copy(i):
             copy.start()
     vectors = jnp.concatenate([v[...].astype(F32) for v in (bq, bk, bv, ga, gm)] + [jnp.zeros((3, 64), F32)], axis=0)
@@ -412,9 +411,6 @@
 
     for chunk in chunks.values():
         chunk.local()
-    angles = freq_ref[...] * len_ref[...].astype(F32)
-    cos_ref[...] = jnp.cos(angles)
-    sin_ref[...] = jnp.sin(angles)
     for i in range(1, 16):
         small_copy(i).wait_recv()
 
@@ -485,9 +481,6 @@
 
     go()
     for i in range(8):
-        if i + AHEAD < 8:
-            for copy in cache_copy(i + AHEAD):
-                copy.start()
         attend(i)
         go()
 
@@ -532,9 +525,9 @@
 
 def store_kernel(wqkv, wgu, wout, wdn, k_lo, k_hi, v_lo, v_hi, smalls,
                  wq, wk, wv, wo, wg, wu, wd, k_out, v_out, bq, bk, bv, ga, gm, sem):
-    pairs = [(src.at[pl.ds(16 * i, 16)], dst.at[pl.ds(base + 16 * i, 16)]) for src, dst, base in (
-        (k_lo, k_out, 0), (k_hi, k_out, 32), (v_lo, v_out, 0), (v_hi, v_out, 32)) for i in range(2)]
-    pairs += [(wdn, wd), (wgu.at[:, pl.ds(0, 176)], wg), (wgu.at[:, pl.ds(176, 176)], wu),
+    lo, hi = pl.ds(0, 32), pl.ds(32, 32)
+    pairs = [(k_lo, k_out.at[lo]), (k_hi, k_out.at[hi]), (v_lo, v_out.at[lo]), (v_hi, v_out.at[hi]),
+             (wdn, wd), (wgu.at[:, pl.ds(0, 176)], wg), (wgu.at[:, pl.ds(176, 176)], wu),
              (wqkv.at[:, pl.ds(0, 64)], wq), (wqkv.at[:, pl.ds(64, 64)], wk), (wqkv.at[:, pl.ds(128, 64)], wv),
              (wout, wo)]
     copies = [pltpu.make_async_copy(src, dst, sem.at[i]) for i, (src, dst) in enumerate(pairs)]
@@ -558,7 +551,9 @@
 
 def local_step(w_query, b_query, w_key, b_key, w_value, b_value, w_out, w_gate, w_up, w_down, gain_attn, gain_mlp,
                hidden, k_cache, v_cache, lengths):
-    freq = np.tile((1.0 / THETA ** (np.arange(0, 64, 2) / 64)).astype(np.float32)[:, None], (1, 256))
+    inv_freq = (1.0 / THETA ** (np.arange(0, 64, 2) / 64)).astype(np.float32)
+    angles = inv_freq[:, None] * jnp.broadcast_to(lengths[None, :], (32, 256)).astype(F32)
+    cos, sin = jnp.cos(angles), jnp.sin(angles)
     lens = lengths[None, :]
     rows = [v[None, :] for v in (b_query, b_key, b_value, gain_attn, gain_mlp)]
     k_view = jnp.transpose(k_cache, (1, 2, 3, 0))
@@ -573,15 +568,13 @@
     held = pl.pallas_call(
         layer_kernel,
         out_shape=[pltpu.VMEM(s, BF16) for s in shapes],
-        in_specs=[hbm] * 10 + [vmem] * 7,
+        in_specs=[hbm] * 10 + [vmem] * 8,
         out_specs=[vmem] * 11,
         scratch_shapes=[
             pltpu.VMEM((256, 1024), BF16),
             pltpu.VMEM((64, 256), F32),
             pltpu.VMEM((512, 256), BF16),
             pltpu.VMEM((8, 176, 256), BF16),
-            pltpu.VMEM((32, 256), F32),
-            pltpu.VMEM((32, 256), F32),
             pltpu.VMEM((3, 64, 1024), BF16),
             pltpu.VMEM((4, 88, 1024), BF16),
             pltpu.VMEM((3, 64, 1024), BF16),
@@ -596,7 +589,7 @@
         ],
         compiler_params=pltpu.CompilerParams(collective_id=0, has_side_effects=True, vmem_limit_bytes=9437184),
         name="layer",
-    )(w_query, w_key, w_value, w_out, w_gate, w_up, w_down, hidden, k_view, v_view, *rows, freq, lens)
+    )(w_query, w_key, w_value, w_out, w_gate, w_up, w_down, hidden, k_view, v_view, *rows, cos, sin, lens)
 
     def shape(*dims):
         return jax.ShapeDtypeStruct(dims, BF16)
@@ -609,7 +602,7 @@
                    shape(4, 128), shape(4, 128), shape(4, 128), shape(8, 128), shape(8, 128)],
         in_specs=[anywhere] * 8 + [vmem],
         out_specs=[hbm] * 9 + [vmem] * 5,
-        scratch_shapes=[dma((15,))],
+        scratch_shapes=[dma((11,))],
         compiler_params=pltpu.CompilerParams(vmem_limit_bytes=9437184),
         cost_estimate=pl.CostEstimate(flops=2 * 10**10, bytes_accessed=5 * 10**7, transcendentals=0),
         name="store",

time: 91.1 us -> 93.4 us (1.025)
  other arithmetic: 0 us -> 2.16 us
    sin x0 -> x1, other arithmetic: none -> 1.48 us  [local_step(): cos, sin = (jnp.cos(angles), jnp.sin(angles))]
where the time goes in v8:
time: 93.4 us; the launch traced here: 93.2 us
  Pallas kernels  87.9 us (94%)
  starting transfers between devices  2.44 us (3%)
  other arithmetic  2.16 us (2%)
    pallas_call x1, Pallas kernels, local_step(): pl.pallas_call(layer_kernel, out_shape=[pltpu.VMEM(s, BF16) for s in shap...  71.4 us
    pallas_call x1, Pallas kernels, local_step(): pl.pallas_call(store_kernel, out_shape=[shape(8, 64, 1024)] * 3 + [shape(...  15.5 us
    ppermute x1, starting transfers between devices, local_step(): peer = lax.ppermute(held[10], 'tp', [(0, 1), (1, 0)])  2.44 us
  transfers between devices with their start and end apart: 1, of which 0 were waited for; matrix products, arithmetic and copies ran while one was open for 0% of the time, Pallas kernels for 17%

profile of v8, /device:TPU:0, one launch (start us, length us, event | category | flops | bytes accessed | tf_op | source)
XLA Modules:
  0.0 93.2 jit_solution(11494793040311609988)
XLA Ops:
  0.6 0.7 convert_element_type.4
  1.3 1.5 %multiply_sine_fusion = (f32[32,256]{1,0:T(8,128)}, f32[32,256]{1,0:T(8,128)}) fusion(f32[256]{0:T(256)S(1)} %convert_element_type.4, f32[32]{0:T(128)} %constant.3), kind=kLoop, calls=%fused_computation | loop fusion | flops 8192 | bytes 66688 | tf_op jit(solution)/shard_map/sin | solution.py:556
  2.8 71.4 %layer.1 = (bf16[8,192,1024]{2,1,0:T(8,128)(2,1)S(1)}, bf16[8,352,1024]{2,1,0:T(8,128)(2,1)S(1)}, bf16[16,64,512]{2,1,0:T(8,128)(2,1)S(1)}, bf16[16,64,1408]{2,1...) custom-call(bf16[64,1024]{1,0:T(8,128)(2,1)} %wq_hbm.1, ...), custom_call_target="tpu_custom_call" | custom-call | tf_op jit(solution)/shard_map/layer/pallas_call | solution.py:568
  74.2 2.4 %collective-permute-start = (bf16[256,1024]{1,0:T(8,128)(2,1)S(1)}, bf16[256,1024]{1,0:T(8,128)(2,1)S(1)}, u32[]{:S(2)}, u32[]{:S(2)}) collective-permute-start(bf16[256,1024]{1,0:T(8,128)(2,1)S(1)} %get-tuple-element.62.mine), channel_id=1, source_target_pairs={{0,8},{8,0},{1,9},{9,1},{2,10},{10,2},{3,11},{11,3},{4,12},{12,4},... | collective-permute-start | bytes 1572872 | tf_op jit(solution)/shard_map/ppermute | solution.py:597
  76.6 15.5 %store.1 = (bf16[8,64,1024]{2,1,0:T(8,128)(2,1)}, bf16[8,64,1024]{2,1,0:T(8,128)(2,1)}, bf16[8,64,1024]{2,1,0:T(8,128)(2,1)}, bf16[16,64,512]{2,1,0:T(8,128)(2,1...) custom-call(bf16[8,192,1024]{2,1,0:T(8,128)(2,1)S(1)} %get-tuple-ele, ...), custom_call_target="tpu_custom_call" | custom-call | flops 20000000000 | bytes 50000000 | tf_op jit(solution)/shard_map/store/pallas_call | solution.py:598
  92.2 0.0 collective-permute-done.peer
  92.2 1.0 %finish.1 = bf16[256,1024]{1,0:T(8,128)(2,1)} custom-call(bf16[256,1024]{1,0:T(8,128)(2,1)S(1)} %get-tuple-element.61.x1, bf16[256,1024]{1,0:T(8,128)(2,1)S(1)} %get-tuple-element.62.mine, bf16[256,1024]{1,0:T(8,128)(2,1)S(1)} %collective-permute-done.peer), custom_call_target="tpu_custom_call" | custom-call | tf_op jit(solution)/shard_map/finish/pallas_call | solution.py:610
Async XLA Ops:
  74.2 18.0 %collective-permute-start = (bf16[256,1024]{1,0:T(8,128)(2,1)S(1)}, bf16[256,1024]{1,0:T(8,128)(2,1)S(1)}, u32[]{:S(2)}, u32[]{:S(2)}) collective-permute-start(bf16[256,1024]{1,0:T(8,128)(2,1)S(1)} %get-tuple-element.62.mine), channel_id=1, source_target_pairs={{0,8},{8,0},{1,9},{9,1},{2,10},{10,2},{3,11},{11,3},{4,12},{12,4},... | collective-permute-start | bytes 1572872 | tf_op jit(solution)/shard_map/ppermute | solution.py:597

commit v9 on v6

--- a/solution.py
+++ b/solution.py
@@ -14,7 +14,6 @@
 BY_ROWS = (((1,), (1,)), ((), ()))
 NAT = (((1,), (0,)), ((), ()))
 GROUP = 8
-AHEAD = 3
 
 
 def dot(lhs, rhs, dims):
@@ -389,7 +388,7 @@
     for i in range(1, 16):
         other = lax.rem(me + i, 16)
         pl.semaphore_signal(barrier, inc=1, device_id=(other % 2, other // 2), device_id_type=MESH)
-    for i in range(AHEAD):
+    for i in range(8):
         for copy in cache_copy(i):
             copy.start()
     vectors = jnp.concatenate([v[...].astype(F32) for v in (bq, bk, bv, ga, gm)] + [jnp.zeros((3, 64), F32)], axis=0)
@@ -406,15 +405,12 @@
         other = lax.rem(me + i, 16)
         return remote(small, smalls.at[me], s_send.at[i], s_recv.at[i], (other % 2, other // 2))
 
-    go()
     for i in range(1, 16):
         small_copy(i).start()
+    go()
 
     for chunk in chunks.values():
         chunk.local()
-    angles = freq_ref[...] * len_ref[...].astype(F32)
-    cos_ref[...] = jnp.cos(angles)
-    sin_ref[...] = jnp.sin(angles)
     for i in range(1, 16):
         small_copy(i).wait_recv()
 
@@ -484,10 +480,10 @@
         o_ref[pl.ds(pl.multiple_of(head * 64, 64), 64)] = acc.astype(BF16)
 
     go()
+    angles = freq_ref[...] * len_ref[...].astype(F32)
+    cos_ref[...] = jnp.cos(angles)
+    sin_ref[...] = jnp.sin(angles)
     for i in range(8):
-        if i + AHEAD < 8:
-            for copy in cache_copy(i + AHEAD):
-                copy.start()
         attend(i)
         go()
 
@@ -532,9 +528,9 @@
 
 def store_kernel(wqkv, wgu, wout, wdn, k_lo, k_hi, v_lo, v_hi, smalls,
                  wq, wk, wv, wo, wg, wu, wd, k_out, v_out, bq, bk, bv, ga, gm, sem):
-    pairs = [(src.at[pl.ds(16 * i, 16)], dst.at[pl.ds(base + 16 * i, 16)]) for src, dst, base in (
-        (k_lo, k_out, 0), (k_hi, k_out, 32), (v_lo, v_out, 0), (v_hi, v_out, 32)) for i in range(2)]
-    pairs += [(wdn, wd), (wgu.at[:, pl.ds(0, 176)], wg), (wgu.at[:, pl.ds(176, 176)], wu),
+    lo, hi = pl.ds(0, 32), pl.ds(32, 32)
+    pairs = [(k_lo, k_out.at[lo]), (k_hi, k_out.at[hi]), (v_lo, v_out.at[lo]), (v_hi, v_out.at[hi]),
+             (wdn, wd), (wgu.at[:, pl.ds(0, 176)], wg), (wgu.at[:, pl.ds(176, 176)], wu),
              (wqkv.at[:, pl.ds(0, 64)], wq), (wqkv.at[:, pl.ds(64, 64)], wk), (wqkv.at[:, pl.ds(128, 64)], wv),
              (wout, wo)]
     copies = [pltpu.make_async_copy(src, dst, sem.at[i]) for i, (src, dst) in enumerate(pairs)]
@@ -609,7 +605,7 @@
                    shape(4, 128), shape(4, 128), shape(4, 128), shape(8, 128), shape(8, 128)],
         in_specs=[anywhere] * 8 + [vmem],
         out_specs=[hbm] * 9 + [vmem] * 5,
-        scratch_shapes=[dma((15,))],
+        scratch_shapes=[dma((11,))],
         compiler_params=pltpu.CompilerParams(vmem_limit_bytes=9437184),
         cost_estimate=pl.CostEstimate(flops=2 * 10**10, bytes_accessed=5 * 10**7, transcendentals=0),
         name="store",

time: 90.4 us -> 86.6 us (0.958)
  Pallas kernels: 87.8 us -> 83.1 us
  starting transfers between devices: 1.68 us -> 2.59 us
    pallas_call x1, Pallas kernels: 71.3 us -> 66.6 us  [local_step(): pl.pallas_call(layer_kernel, out_shape=[pltpu.VMEM(s, BF16) for s in shap...]
    ppermute x1, starting transfers between devices: 1.68 us -> 2.59 us  [local_step(): peer = lax.ppermute(held[10], 'tp', [(0, 1), (1, 0)])]
  transfers between devices with their start and end apart: 1 -> 1, of which waited for: 0 -> 0; matrix products, arithmetic and copies ran while one was open for 0% -> 0% of each run, Pallas kernels for 17% -> 18%
where the time goes in v9:
time: 86.6 us; the launch traced here: 86.4 us
  Pallas kernels  83.1 us (96%)
  starting transfers between devices  2.59 us (3%)
    pallas_call x1, Pallas kernels, local_step(): pl.pallas_call(layer_kernel, out_shape=[pltpu.VMEM(s, BF16) for s in shap...  66.6 us
    pallas_call x1, Pallas kernels, local_step(): pl.pallas_call(store_kernel, out_shape=[shape(8, 64, 1024)] * 3 + [shape(...  15.5 us
    ppermute x1, starting transfers between devices, local_step(): peer = lax.ppermute(held[10], 'tp', [(0, 1), (1, 0)])  2.59 us
  transfers between devices with their start and end apart: 1, of which 0 were waited for; matrix products, arithmetic and copies ran while one was open for 0% of the time, Pallas kernels for 18%

profile of v9, /device:TPU:0, one launch (start us, length us, event | category | flops | bytes accessed | tf_op | source)
XLA Modules:
  0.0 86.4 jit_solution(13674084343756253821)
XLA Ops:
  0.7 66.6 %layer.1 = (bf16[8,192,1024]{2,1,0:T(8,128)(2,1)S(1)}, bf16[8,352,1024]{2,1,0:T(8,128)(2,1)S(1)}, bf16[16,64,512]{2,1,0:T(8,128)(2,1)S(1)}, bf16[16,64,1408]{2,1...) custom-call(bf16[64,1024]{1,0:T(8,128)(2,1)} %wq_hbm.1, ...), custom_call_target="tpu_custom_call" | custom-call | tf_op jit(solution)/shard_map/layer/pallas_call | solution.py:569
  67.2 2.6 %collective-permute-start = (bf16[256,1024]{1,0:T(8,128)(2,1)S(1)}, bf16[256,1024]{1,0:T(8,128)(2,1)S(1)}, u32[]{:S(2)}, u32[]{:S(2)}) collective-permute-start(bf16[256,1024]{1,0:T(8,128)(2,1)S(1)} %get-tuple-element.62.mine), channel_id=1, source_target_pairs={{0,8},{8,0},{1,9},{9,1},{2,10},{10,2},{3,11},{11,3},{4,12},{12,4},... | collective-permute-start | bytes 1572872 | tf_op jit(solution)/shard_map/ppermute | solution.py:600
  69.8 15.5 %store.1 = (bf16[8,64,1024]{2,1,0:T(8,128)(2,1)}, bf16[8,64,1024]{2,1,0:T(8,128)(2,1)}, bf16[8,64,1024]{2,1,0:T(8,128)(2,1)}, bf16[16,64,512]{2,1,0:T(8,128)(2,1...) custom-call(bf16[8,192,1024]{2,1,0:T(8,128)(2,1)S(1)} %get-tuple-ele, ...), custom_call_target="tpu_custom_call" | custom-call | flops 20000000000 | bytes 50000000 | tf_op jit(solution)/shard_map/store/pallas_call | solution.py:601
  85.4 0.0 collective-permute-done.peer
  85.4 1.0 %finish.1 = bf16[256,1024]{1,0:T(8,128)(2,1)} custom-call(bf16[256,1024]{1,0:T(8,128)(2,1)S(1)} %get-tuple-element.61.x1, bf16[256,1024]{1,0:T(8,128)(2,1)S(1)} %get-tuple-element.62.mine, bf16[256,1024]{1,0:T(8,128)(2,1)S(1)} %collective-permute-done.peer), custom_call_target="tpu_custom_call" | custom-call | tf_op jit(solution)/shard_map/finish/pallas_call | solution.py:613
Async XLA Ops:
  67.2 18.1 %collective-permute-start = (bf16[256,1024]{1,0:T(8,128)(2,1)S(1)}, bf16[256,1024]{1,0:T(8,128)(2,1)S(1)}, u32[]{:S(2)}, u32[]{:S(2)}) collective-permute-start(bf16[256,1024]{1,0:T(8,128)(2,1)S(1)} %get-tuple-element.62.mine), channel_id=1, source_target_pairs={{0,8},{8,0},{1,9},{9,1},{2,10},{10,2},{3,11},{11,3},{4,12},{12,4},... | collective-permute-start | bytes 1572872 | tf_op jit(solution)/shard_map/ppermute | solution.py:600
